TPU v7x, 32 devices: a whole 2x2x4 slice. The times are simulated.
32 devices in a mesh: section: 4 (over y, x), dev: 8 (over z, core).
Axes of the slice: x: 2, y: 2, z: 4, core: 2. Of those that a mesh axis runs over, the one named last changes fastest.
Arguments:
- late_sent: bfloat16 [4, 784, 1024], P('section', 'dev'), may hold values from -5 to 5
- entry_rows: bfloat16 [784, 1024], P('dev'), may hold values from -5 to 5
- gain_first: float32 [4, 1024], P('section'), may hold values from 0.1 to 1.9
- shift_first: float32 [4, 1024], P('section'), may hold values from -3 to 3
- expand_late: bfloat16 [4, 1024, 4096], P('section', None, 'dev'), may hold values from -0.1875 to 0.1875
- gain_inner: float32 [4, 4096], P('section', 'dev'), may hold values from 0.1 to 1.9
- shift_inner: float32 [4, 4096], P('section', 'dev'), may hold values from -3 to 3
- reduce_late: bfloat16 [4, 4096, 1024], P('section', 'dev'), may hold values from -0.09375 to 0.09375
- early_saved: bfloat16 [4, 12544, 256], P('section', 'dev'), may hold values from -6 to 6
- upstream_grad: bfloat16 [4, 12544, 256], P('section', 'dev'), may hold values from -6 to 6
- exit_grad: bfloat16 [12544, 256], P('dev'), may hold values from -6 to 6
- expand_early: bfloat16 [4, 256, 1024], P('section'), may hold values from -0.375 to 0.375
- reduce_early: bfloat16 [4, 1024, 256], P('section'), may hold values from -0.1875 to 0.1875
Outputs:
- late_out: bfloat16 [4, 784, 1024], P('section', 'dev')
- input_grad: bfloat16 [4, 12544, 256], P('section', 'dev')
- grad_expand: float32 [4, 256, 1024], P('section')
- grad_reduce: float32 [4, 1024, 256], P('section')
All inputs are finite; a program needn't handle non-finite values.
Results may differ from a plain program's by a relative error of at most 0.02.
Values may be sent and summed in bfloat16 or wider, within the bound.
No kernel may reach another device: no remote copies, remote signals or barrier semaphores. Data moves between devices by JAX's collectives and lax.ppermute only.
A program may use at most 128 MiB of HBM per device.

v0:
```python
import math

import jax
import jax.numpy as jnp
from jax import lax
from jax.sharding import PartitionSpec as P

epsilon = 1e-05


def from_behind(x, axis, by):
    peers = lax.axis_size(axis)
    pairs = [(i, i + by) for i in range(peers) if 0 <= i + by < peers]
    return lax.ppermute(x, axis, pairs)


def affine(sums, squares, count, gain, shift):
    average = sums / count
    second = squares / count
    spread = gain * lax.rsqrt(second - average * average + epsilon)
    return (spread, shift - average * spread)


def silu_slope(values):
    sigma = jax.nn.sigmoid(values)
    return sigma * (1.0 + values * (1.0 - sigma))


def late_part(
    late_sent,
    entry_rows,
    gain_first,
    shift_first,
    expand_late,
    gain_inner,
    shift_inner,
    reduce_late,
):
    section_index = lax.axis_index("section")
    rows_dev = entry_rows.shape[0]
    total_rows = rows_dev * lax.axis_size("dev")
    expand = expand_late[0]
    arrived = from_behind(late_sent[0], "section", 1)
    own_rows = jnp.where(section_index == 0, entry_rows, arrived)
    values = own_rows.astype(jnp.float32)
    sums, squares = lax.psum((jnp.sum(values, axis=0), jnp.sum(values * values, axis=0)), "dev")
    spread, offset = affine(sums, squares, total_rows, gain_first[0], shift_first[0])
    first = jax.nn.silu(
        lax.all_gather(own_rows, "dev", axis=0, tiled=True).astype(jnp.float32) * spread + offset
    ).astype(jnp.bfloat16)
    inner = jnp.dot(first, expand, preferred_element_type=jnp.float32)
    spread_two, offset_two = affine(
        jnp.sum(inner, axis=0),
        jnp.sum(inner * inner, axis=0),
        total_rows,
        gain_inner[0],
        shift_inner[0],
    )
    hidden = jax.nn.silu(inner * spread_two + offset_two).astype(jnp.bfloat16)
    reduce_weight = reduce_late[0]
    summed = lax.psum_scatter(
        jnp.dot(hidden, reduce_weight, preferred_element_type=jnp.float32).astype(jnp.bfloat16),
        "dev",
        scatter_dimension=0,
        tiled=True,
    ).astype(jnp.float32)
    return (own_rows.astype(jnp.float32) + summed).astype(jnp.bfloat16)[None]


def early_part(early_saved, upstream_grad, exit_grad, expand_early, reduce_early):
    section_index = lax.axis_index("section")
    arrived = from_behind(upstream_grad[0], "section", -1)
    grad = jnp.where(section_index == lax.axis_size("section") - 1, exit_grad, arrived)
    saved = early_saved[0]
    expand = expand_early[0]
    reduce_weight = reduce_early[0]
    pre = jnp.dot(saved, expand, preferred_element_type=jnp.float32)
    hidden = jax.nn.silu(pre).astype(jnp.bfloat16)
    back = lax.dot_general(
        grad, reduce_weight, (((1,), (1,)), ((), ())), preferred_element_type=jnp.float32
    )
    slope = (back * silu_slope(pre)).astype(jnp.bfloat16)
    local_expand = lax.dot_general(
        saved, slope, (((0,), (0,)), ((), ())), preferred_element_type=jnp.float32
    )
    local_reduce = lax.dot_general(
        hidden, grad, (((0,), (0,)), ((), ())), preferred_element_type=jnp.float32
    )
    summed_expand, summed_reduce = lax.psum((local_expand, local_reduce), "dev")
    result = grad.astype(jnp.float32) + lax.dot_general(
        slope, expand, (((1,), (1,)), ((), ())), preferred_element_type=jnp.float32
    )
    factor = 1.0 / math.sqrt(saved.shape[0] * lax.axis_size("dev"))
    return (
        result.astype(jnp.bfloat16)[None],
        (summed_expand * factor)[None],
        (summed_reduce * factor)[None],
    )


def shards(
    late_sent,
    entry_rows,
    gain_first,
    shift_first,
    expand_late,
    gain_inner,
    shift_inner,
    reduce_late,
    early_saved,
    upstream_grad,
    exit_grad,
    expand_early,
    reduce_early,
):
    late_out = late_part(
        late_sent,
        entry_rows,
        gain_first,
        shift_first,
        expand_late,
        gain_inner,
        shift_inner,
        reduce_late,
    )
    input_grad, grad_expand, grad_reduce = early_part(
        early_saved, upstream_grad, exit_grad, expand_early, reduce_early
    )
    return (late_out, input_grad, grad_expand, grad_reduce)


def solution(mesh):
    in_specs = (
        P("section", "dev", None),
        P("dev", None),
        P("section", None),
        P("section", None),
        P("section", None, "dev"),
        P("section", "dev"),
        P("section", "dev"),
        P("section", "dev", None),
        P("section", "dev", None),
        P("section", "dev", None),
        P("dev", None),
        P("section", None, None),
        P("section", None, None),
    )
    out_specs = (
        P("section", "dev", None),
        P("section", "dev", None),
        P("section", None, None),
        P("section", None, None),
    )
    return jax.shard_map(shards, mesh=mesh, in_specs=in_specs, out_specs=out_specs, check_vma=False)
```

profile of v0, /device:TPU:0, one launch (start us, length us, event | category | flops | bytes accessed | tf_op | source)
XLA Modules:
  0.0 182.2 jit_solution(4073630690061553025)
XLA Ops:
  7.2 0.0 copy-start
  7.2 0.0 all-reduce.6.cloned.1.call-start
  7.2 1.4 collective-permute-start.1
  8.7 0.0 copy-start.3
  8.7 2.4 %fusion.7 = f32[1568,1024]{1,0:T(8,128)S(1)} fusion(bf16[1,1568,256]{2,1,0:T(8,128)(2,1)} %param.21, bf16[1,256,1024]{2,1,0:T(8,128)(2,1)} %param.24), kind=kOutput, calls=%fused_computation.17 | convolution fusion | flops 822083584 | bytes 7749632 | tf_op jit(solution)/shard_map/dot_general | solution.py:77
  11.0 19.3 %collective-permute-done.1 = bf16[1568,256]{1,0:T(8,128)(2,1)S(1)} collective-permute-done((bf16[1568,256]{1,0:T(8,128)(2,1)}, bf16[1568,256]{1,0:T(8,128)(2,1)S(1)}, u32[]{:S(2)}, u32[]{:S(2)}) %collective-permute-start.1) | collective-permute-done | bytes 802848 | tf_op jit(solution)/shard_map/ppermute | solution.py:14
  30.3 0.0 copy-done.3
  30.3 0.1 broadcast_select_fusion
  30.4 0.0 copy-start.12
  30.5 2.8 %fusion.1 = f32[1024,256]{1,0:T(8,128)} fusion(bf16[1568,256]{1,0:T(8,128)(2,1)S(1)} %broadcast_select_fusion, f32[1568,1024]{1,0:T(8,128)S(1)} %fusion.7), kind=kOutput, calls=%fused_computation.4 | convolution fusion | flops 830111744 | bytes 8273920 | tf_op jit(solution)/shard_map/dot_general | solution.py:86
  33.3 0.0 copy-done.12
  33.3 0.0 copy-start.2
  33.3 2.7 %multiply_convert_fusion.1 = bf16[1568,1024]{1,0:T(8,128)(2,1)S(1)} fusion(f32[1568,1024]{1,0:T(8,128)S(1)} %fusion.7, bf16[1568,256]{1,0:T(8,128)(2,1)S(1)} %broadcast_select_fusion, bf16[1,1024,256]{2,1,0:T(8,128)(2,1)S(1)} %copy-done.12), kind=kOutput, calls=%fused_computation.1 | convolution fusion | flops 836534272 | bytes 10960896 | tf_op jit(solution)/shard_map/dot_general | solution.py:79
  36.0 0.0 copy-start.14
  36.0 1.7 copy-done.14
  37.7 0.0 copy-done.2
  37.7 0.0 copy-start.13
  37.7 0.0 copy-start.5
  37.7 0.0 copy-start.10
  37.7 0.0 copy-start.6
  37.7 0.0 copy-start.7
  37.7 0.0 copy-start.4
  37.7 2.1 %convolution_bitcast_fusion = f32[256,1024]{0,1:T(8,128)} fusion(bf16[1568,1024]{1,0:T(8,128)(2,1)S(1)} %multiply_convert_fusion.1, bf16[1,1568,256]{2,1,0:T(8,128)(2,1)S(1)} %copy-done.2), kind=kOutput, calls=%fused_computation.10 | convolution fusion | flops 822083584 | bytes 5062656 | tf_op jit(solution)/shard_map/dot_general | solution.py:83
  39.9 0.0 all-reduce.6.cloned.1.call-update
  39.9 0.0 all-gather.3.cloned.1.call-start
  39.9 0.0 copy-done.13
  40.0 4.6 %collective-permute-start = (bf16[98,1024]{1,0:T(8,128)(2,1)S(1)}, bf16[98,1024]{1,0:T(8,128)(2,1)S(1)}, u32[]{:S(2)}, u32[]{:S(2)}) collective-permute-start(bf16[98,1024]{1,0:T(8,128)(2,1)S(1)} %bitcast.57), channel_id=1, source_target_pairs={{0,8},{8,16},{16,24},{1,9},{9,17},{17,25},{2,10},{10,18},{18,26},{... | collective-permute-start | bytes 602120 | tf_op jit(solution)/shard_map/ppermute | solution.py:14
  44.5 3.6 %collective-permute-done = bf16[98,1024]{1,0:T(8,128)(2,1)S(1)} collective-permute-done((bf16[98,1024]{1,0:T(8,128)(2,1)S(1)}, bf16[98,1024]{1,0:T(8,128)(2,1)S(1)}, u32[]{:S(2)}, u32[]{:S(2)}) %collective-permute-start) | collective-permute-done | bytes 200736 | tf_op jit(solution)/shard_map/ppermute | solution.py:14
  48.2 0.0 copy-done.5
  48.2 0.8 convert_reduce_fusion
  48.9 0.0 all-gather.3.cloned.1.call-update
  49.0 0.0 copy-done.10
  49.0 0.6 dynamic-slice.4
  50.2 15.7 %all-reduce.2 = (f32[1024]{0:T(1024)S(1)}, f32[1024]{0:T(1024)S(1)}) all-reduce(f32[1024]{0:T(1024)S(1)} %get-tuple-element.19, f32[1024]{0:T(1024)S(1)} %get-tuple-element.18), channel_id=1, replica_groups=mesh['section'=4,'dev'=8] {'dev'}, use_global_device_ids=true, to_apply=%region_1.2 | all-reduce | flops 2048 | bytes 16384 | tf_op jit(solution)/shard_map/psum | solution.py:46
  65.9 0.0 copy-done.6
  65.9 0.0 copy-done.7
  65.9 0.0 copy-done.4
  65.9 3.9 %fusion.5 = bf16[1,1568,256]{2,1,0:T(8,128)(2,1)} fusion(bf16[1568,256]{1,0:T(8,128)(2,1)S(1)} %broadcast_select_fusion, bf16[1568,1024]{1,0:T(8,128)(2,1)} %copy-done.14, bf16[1,256,1024]{2,1,0:T(8,128)(2,1)S(1)} %copy-done.4), kind=kOutput, calls=%fused_computation.15 | convolution fusion | flops 823287808 | bytes 5341184 | tf_op jit(solution)/shard_map/dot_general | solution.py:90
  69.8 37.3 %all-reduce.6.cloned.1.call-done = (f32[256,1024]{0,1:T(8,128)}, f32[1024,256]{1,0:T(8,128)}) async-done(((f32[256,1024]{0,1:T(8,128)}, f32[1024,256]{1,0:T(8,128)}), (f32[256,1024]{0,1:T(8,128)}, f32[1024,256]{1,0:T(8,128)})) %all-reduce.6.cloned.1.call-update) | async-done | bytes 2097168 | tf_op jit(solution)/shard_map/psum | solution.py:89
  107.1 0.0 copy-start.11
  107.1 1.4 multiply_bitcast_fusion.1
  108.5 26.5 %all-gather.3.cloned.1.call-done = bf16[8,98,1024]{2,1,0:T(8,128)(2,1)} async-done(((bf16[1,98,1024]{2,1,0:T(8,128)(2,1)}), bf16[8,98,1024]{2,1,0:T(8,128)(2,1)}) %all-gather.3.cloned.1.call-update) | async-done | bytes 1605648 | tf_op jit(solution)/shard_map/all_gather | solution.py:49
  135.0 3.0 %reshape.47 = f32[784,1024]{1,0:T(8,128)} reshape(bf16[8,98,1024]{2,1,0:T(8,128)(2,1)} %all-gather.3.cloned.1.call-done) | data formatting | bytes 4816896 | tf_op jit(solution)/shard_map/convert_element_type | solution.py:49
  138.0 0.0 copy-done.11
  138.0 0.0 copy-start.8
  138.0 0.0 copy-start.9
  138.0 3.0 %multiply_reduce_fusion = (f32[512]{0:T(512)S(1)}, f32[512]{0:T(512)S(1)}, f32[784,512]{1,0:T(8,128)S(1)}) fusion(bf16[1,1024,512]{2,1,0:T(8,128)(2,1)S(1)} %copy-done.11, f32[784,1024]{1,0:T(8,128)} %reshape.47, f32[1024]{0:T(1024)S(1)} %get-tuple-element.26, f32[1024]{0:T(1024)S(1)} %get-tuple-element.27), kind=kOutput, calls=%fused_computation.8 | convolution fusion | flops 828906496 | bytes 5877760 | tf_op jit(solution)/shard_map/dot_general | solution.py:51
  141.1 0.0 copy-done.8
  141.1 0.0 copy-done.9
  141.1 0.0 copy-done
  141.2 2.2 %convolution_convert_fusion = bf16[784,1024]{1,0:T(8,128)(2,1)} fusion(bf16[1,512,1024]{2,1,0:T(8,128)(2,1)S(1)} %copy-done, f32[784,512]{1,0:T(8,128)S(1)} %get-tuple-element.29, f32[512]{0:T(512)S(1)} %bitcast.54, f32[512]{0:T(512)S(1)} %bitcast.55), kind=kOutput, calls=%fused_computation.5 | convolution fusion | flops 825696256 | bytes 4263936 | tf_op jit(solution)/shard_map/dot_general | solution.py:62
  143.4 0.0 copy-start.1
  143.4 26.0 %fusion = bf16[104,1024]{1,0:T(8,128)(2,1)S(1)} fusion(bf16[784,1024]{1,0:T(8,128)(2,1)} %convolution_convert_fusion), kind=kCustom, calls=%all-reduce-scatter | all-reduce-scatter fusion | flops 851969 | bytes 1819136
  169.4 1.3 collective-permute-start.2
  170.7 2.3 %multiply_bitcast_fusion = f32[1,1024,256]{2,1,0:T(8,128)} fusion(f32[1024,256]{1,0:T(8,128)} %get-tuple-element.23), kind=kLoop, calls=%fused_computation.13 | loop fusion | flops 262144 | bytes 2097152 | tf_op jit(solution)/shard_map/broadcast_in_dim | solution.py:97
  173.0 1.3 copy.19
  174.3 0.0 collective-permute-done.2
  174.3 0.3 concatenate
  174.6 0.0 copy-done.1
  174.6 0.8 fusion.20
  (4 shorter events, 0.1 us)
Async XLA Ops:
  7.2 134.0 %copy-start = (bf16[1,512,1024]{2,1,0:T(8,128)(2,1)S(1)}, bf16[1,512,1024]{2,1,0:T(8,128)(2,1)}, u32[]{:S(2)}) copy-start(bf16[1,512,1024]{2,1,0:T(8,128)(2,1)} %param.20) | copy-start | bytes 3145732
  7.2 99.9 %all-reduce.6.cloned.1.call-start = ((), (), s32[]{:S(2)}) async-start(), calls=%async_computation.1 | async-start | bytes 4194304 | tf_op jit(solution)/shard_map/psum | solution.py:89
  7.2 23.1 %collective-permute-start.1 = (bf16[1568,256]{1,0:T(8,128)(2,1)}, bf16[1568,256]{1,0:T(8,128)(2,1)S(1)}, u32[]{:S(2)}, u32[]{:S(2)}) collective-permute-start(bf16[1568,256]{1,0:T(8,128)(2,1)} %bitcast.56), channel_id=1, source_target_pairs={{8,0},{16,8},{24,16},{9,1},{17,9},{25,17},{10,2},{18,10},{26,18},{... | collective-permute-start | bytes 2408456 | tf_op jit(solution)/shard_map/ppermute | solution.py:14
  8.7 21.7 %copy-start.3 = (bf16[1568,256]{1,0:T(8,128)(2,1)S(1)}, bf16[1568,256]{1,0:T(8,128)(2,1)}, u32[]{:S(2)}) copy-start(bf16[1568,256]{1,0:T(8,128)(2,1)} %param.23) | copy-start | bytes 2408452
  30.4 2.9 %copy-start.12 = (bf16[1,1024,256]{2,1,0:T(8,128)(2,1)S(1)}, bf16[1,1024,256]{2,1,0:T(8,128)(2,1)}, u32[]{:S(2)}) copy-start(bf16[1,1024,256]{2,1,0:T(8,128)(2,1)} %param.25) | copy-start | bytes 1572868
  33.3 4.4 %copy-start.2 = (bf16[1,1568,256]{2,1,0:T(8,128)(2,1)S(1)}, bf16[1,1568,256]{2,1,0:T(8,128)(2,1)}, u32[]{:S(2)}) copy-start(bf16[1,1568,256]{2,1,0:T(8,128)(2,1)} %param.21) | copy-start | bytes 2408452
  36.0 1.7 copy-start.14
  37.7 2.3 %copy-start.13 = (bf16[1,98,1024]{2,1,0:T(8,128)(2,1)S(1)}, bf16[1,98,1024]{2,1,0:T(8,128)(2,1)}, u32[]{:S(2)}) copy-start(bf16[1,98,1024]{2,1,0:T(8,128)(2,1)} %param.13) | copy-start | bytes 602116
  37.7 10.5 %copy-start.5 = (bf16[98,1024]{1,0:T(8,128)(2,1)S(1)}, bf16[98,1024]{1,0:T(8,128)(2,1)}, u32[]{:S(2)}) copy-start(bf16[98,1024]{1,0:T(8,128)(2,1)} %param.14) | copy-start | bytes 602116
  37.7 11.3 %copy-start.10 = (u32[32]{0:T(128)S(1)}, u32[32]{0:T(128)}, u32[]{:S(2)}) copy-start(u32[32]{0:T(128)} %constant.46) | copy-start | bytes 388
  37.7 28.2 %copy-start.6 = (f32[1,1024]{1,0:T(1,128)S(1)}, f32[1,1024]{1,0:T(1,128)}, u32[]{:S(2)}) copy-start(f32[1,1024]{1,0:T(1,128)} %param.16) | copy-start | bytes 12292
  37.7 28.2 %copy-start.7 = (f32[1,1024]{1,0:T(1,128)S(1)}, f32[1,1024]{1,0:T(1,128)}, u32[]{:S(2)}) copy-start(f32[1,1024]{1,0:T(1,128)} %param.15) | copy-start | bytes 12292
  37.7 28.2 %copy-start.4 = (bf16[1,256,1024]{2,1,0:T(8,128)(2,1)S(1)}, bf16[1,256,1024]{2,1,0:T(8,128)(2,1)}, u32[]{:S(2)}) copy-start(bf16[1,256,1024]{2,1,0:T(8,128)(2,1)} %param.24) | copy-start | bytes 1572868
  39.9 95.1 %all-gather.3.cloned.1.call-start = ((), (), s32[]{:S(2)}) async-start(), calls=%async_computation | async-start | bytes 1916928 | tf_op jit(solution)/shard_map/all_gather | solution.py:49
  40.0 8.2 %collective-permute-start = (bf16[98,1024]{1,0:T(8,128)(2,1)S(1)}, bf16[98,1024]{1,0:T(8,128)(2,1)S(1)}, u32[]{:S(2)}, u32[]{:S(2)}) collective-permute-start(bf16[98,1024]{1,0:T(8,128)(2,1)S(1)} %bitcast.57), channel_id=1, source_target_pairs={{0,8},{8,16},{16,24},{1,9},{9,17},{17,25},{2,10},{10,18},{18,26},{... | collective-permute-start | bytes 602120 | tf_op jit(solution)/shard_map/ppermute | solution.py:14
  107.1 30.9 %copy-start.11 = (bf16[1,1024,512]{2,1,0:T(8,128)(2,1)S(1)}, bf16[1,1024,512]{2,1,0:T(8,128)(2,1)}, u32[]{:S(2)}) copy-start(bf16[1,1024,512]{2,1,0:T(8,128)(2,1)} %param.17) | copy-start | bytes 3145732
  138.0 3.1 %copy-start.8 = (f32[1,512]{1,0:T(1,128)S(1)}, f32[1,512]{1,0:T(1,128)}, u32[]{:S(2)}) copy-start(f32[1,512]{1,0:T(1,128)} %param.19) | copy-start | bytes 6148
  138.0 3.1 %copy-start.9 = (f32[1,512]{1,0:T(1,128)S(1)}, f32[1,512]{1,0:T(1,128)}, u32[]{:S(2)}) copy-start(f32[1,512]{1,0:T(1,128)} %param.18) | copy-start | bytes 6148
  143.4 31.2 %copy-start.1 = (bf16[98,1024]{1,0:T(8,128)(2,1)S(1)}, bf16[98,1024]{1,0:T(8,128)(2,1)}, u32[]{:S(2)}) copy-start(bf16[98,1024]{1,0:T(8,128)(2,1)} %get-tuple-element.28) | copy-start | bytes 602116
  169.4 4.9 %collective-permute-start.2 = (bf16[42,1024]{1,0:T(8,128)(2,1)S(1)}, bf16[42,1024]{1,0:T(8,128)(2,1)S(1)}, u32[]{:S(2)}, u32[]{:S(2)}) collective-permute-start(bf16[42,1024]{1,0:T(8,128)(2,1)S(1)} %slice), channel_id=1, source_target_pairs={{0,1},{1,2},{2,3},{3,4},{4,5},{5,6},{6,7},{8,9},{9,10},{10,11},{11... | collective-permute-start | bytes 258056
Sparse Core Ops, SparseCore 0:
  40.0 67.0 all-reduce.5
  109.3 25.6 all-gather.2
where the time goes:
time: 183 us; the launch traced here: 182 us
  waiting for transfers between devices  86.8 us (47%)
  blocking collectives  41.6 us (23%)
  matrix products  19.2 us (10%)
  between operations  14.9 us (8%)
  starting transfers between devices  7.37 us (4%)
  local copies, waits for them, and re-layouts  6.93 us (4%)
  other arithmetic  5.38 us (3%)
    psum x1, waiting for transfers between devices, early_part(): summed_expand, summed_reduce = lax.psum((local_expand, local_reduce), 'dev')  37.3 us
    all_gather x1, waiting for transfers between devices, late_part(): lax.all_gather(own_rows, 'dev', axis=0, tiled=True).astype(jnp.float32)  26.5 us
    unnamed x1, blocking collectives  26 us
    ppermute x2, waiting for transfers between devices, from_behind(): return lax.ppermute(x, axis, pairs)  22.9 us
    psum x1, blocking collectives, late_part(): lax.psum((jnp.sum(values, axis=0), jnp.sum(values * values, axis=0)), 'dev')  15.7 us
    ppermute x2, starting transfers between devices, from_behind(): return lax.ppermute(x, axis, pairs)  6 us
    unnamed x34, local copies, waits for them, and re-layouts  3.93 us
    dot_general x1, matrix products, early_part(): lax.dot_general(slope, expand, (((1,), (1,)), ((), ())), preferred_elemen...  3.86 us
  transfers between devices with their start and end apart: 5, of which 4 were waited for; matrix products, arithmetic and copies ran while one was open for 7% of the time, Pallas kernels for 0%

commit v1 on v0

v1 whole, which is shorter than its diff:
```python
import math

import jax
import jax.numpy as jnp
from jax import lax
from jax.sharding import PartitionSpec as P

epsilon = 1e-05
bf16 = jnp.bfloat16
f32 = jnp.float32


def from_behind(x, axis, by):
    peers = lax.axis_size(axis)
    pairs = [(i, i + by) for i in range(peers) if 0 <= i + by < peers]
    return lax.ppermute(x, axis, pairs)


def swap(x):
    return lax.ppermute(x, "dev", [(i, i ^ 1) for i in range(lax.axis_size("dev"))])


def chips():
    return lax.axis_size("dev") // 2


def partner(chip, step):
    count = chips()
    return chip ^ step if count & (count - 1) == 0 else (chip + step) % count


def across(x, step, back=False):
    pairs = []
    for chip in range(chips()):
        for core in range(2):
            here, there = 2 * chip + core, 2 * partner(chip, step) + core
            pairs.append((there, here) if back else (here, there))
    return lax.ppermute(x, "dev", pairs)


def steps_far_first():
    return list(range(chips() - 1, 0, -1))


def affine(sums, squares, count, gain, shift):
    average = sums / count
    second = squares / count
    spread = gain * lax.rsqrt(second - average * average + epsilon)
    return (spread, shift - average * spread)


def silu_slope(values):
    sigma = jax.nn.sigmoid(values)
    return sigma * (1.0 + values * (1.0 - sigma))


def late_part(
    late_sent,
    entry_rows,
    gain_first,
    shift_first,
    expand_late,
    gain_inner,
    shift_inner,
    reduce_late,
):
    section_index = lax.axis_index("section")
    total_rows = entry_rows.shape[0] * lax.axis_size("dev")
    arrived = from_behind(late_sent[0], "section", 1)
    expand, reduce_weight = expand_late[0], reduce_late[0]
    expand_two, reduce_two = swap(expand), swap(reduce_weight)
    inner_affine = jnp.concatenate([gain_inner, shift_inner], axis=0)
    affine_two = swap(inner_affine)
    own_rows = jnp.where(section_index == 0, entry_rows, arrived)
    blocks = {0: own_rows}
    for step in steps_far_first():
        blocks[step] = across(own_rows, step, back=True)
    rows = jnp.stack([blocks[step] for step in range(chips())])
    values = rows.astype(f32)
    mine = jnp.stack([jnp.sum(values, axis=(0, 1)), jnp.sum(values * values, axis=(0, 1))])
    total = mine + swap(mine)
    spread, offset = affine(total[0], total[1], total_rows, gain_first[0], shift_first[0])
    first = jax.nn.silu(values * spread + offset).astype(bf16)

    def expanded(weight):
        inner = lax.dot_general(first, weight, (((2,), (0,)), ((), ())), preferred_element_type=f32)
        return inner, jnp.stack([jnp.sum(inner, axis=(0, 1)), jnp.sum(inner * inner, axis=(0, 1))])

    inner_one, sums_one = expanded(expand)
    inner_two, sums_two = expanded(expand_two)
    got = swap(jnp.stack([sums_two, sums_one]))
    total_one, total_two = sums_one + got[0], sums_two + got[1]

    def hidden_of(inner, total, gain_shift):
        spread_two, offset_two = affine(total[0], total[1], total_rows, gain_shift[0], gain_shift[1])
        return jax.nn.silu(inner * spread_two + offset_two).astype(bf16)

    hidden_one = hidden_of(inner_one, total_one, inner_affine)
    hidden_two = hidden_of(inner_two, total_two, affine_two)

    def reduced(step):
        return jnp.dot(hidden_one[step], reduce_weight, preferred_element_type=f32) + jnp.dot(
            hidden_two[step], reduce_two, preferred_element_type=f32
        )

    result = own_rows.astype(f32) + reduced(0)
    for step in steps_far_first():
        result = result + across(reduced(step).astype(bf16), step).astype(f32)
    return result.astype(bf16)[None]


def summed_over_dev(terms, factor):
    count = chips()
    device = lax.axis_index("dev")
    chip, core = device // 2, device % 2
    halves = []
    for term in terms:
        part = term.reshape(2, term.shape[0] // 2, term.shape[1])
        keep = lax.dynamic_index_in_dim(part, core, 0, keepdims=False)
        send = lax.dynamic_index_in_dim(part, 1 - core, 0, keepdims=False).astype(bf16)
        halves.append(keep + swap(send).astype(f32))
    shares = []
    for half in halves:
        pieces = half.reshape(count, half.shape[0] // count, half.shape[1])
        shares.append(pieces)
    sums = [lax.dynamic_index_in_dim(pieces, chip, 0, keepdims=False) for pieces in shares]
    for step in steps_far_first():
        for index, pieces in enumerate(shares):
            piece = lax.dynamic_index_in_dim(pieces, partner(chip, step), 0, keepdims=False)
            sums[index] = sums[index] + across(piece.astype(bf16), step).astype(f32)
    results = []
    for term, total in zip(terms, sums):
        own = (total * factor).astype(bf16)
        gathered = jnp.zeros((count,) + own.shape, bf16)
        gathered = lax.dynamic_update_index_in_dim(gathered, own, chip, 0)
        for step in steps_far_first():
            gathered = lax.dynamic_update_index_in_dim(
                gathered, across(own, step, back=True), partner(chip, step), 0
            )
        half = gathered.reshape(term.shape[0] // 2, term.shape[1])
        other = swap(half)
        both = jnp.where(core == 0, jnp.stack([half, other]), jnp.stack([other, half]))
        results.append(both.reshape(term.shape).astype(f32))
    return results


def early_part(early_saved, upstream_grad, exit_grad, expand_early, reduce_early):
    section_index = lax.axis_index("section")
    arrived = from_behind(upstream_grad[0], "section", -1)
    grad = jnp.where(section_index == lax.axis_size("section") - 1, exit_grad, arrived)
    saved = early_saved[0]
    expand = expand_early[0]
    reduce_weight = reduce_early[0]
    pre = jnp.dot(saved, expand, preferred_element_type=f32)
    hidden = jax.nn.silu(pre).astype(bf16)
    back = lax.dot_general(grad, reduce_weight, (((1,), (1,)), ((), ())), preferred_element_type=f32)
    slope = (back * silu_slope(pre)).astype(bf16)
    local_expand = lax.dot_general(
        saved, slope, (((0,), (0,)), ((), ())), preferred_element_type=f32
    )
    local_reduce = lax.dot_general(
        hidden, grad, (((0,), (0,)), ((), ())), preferred_element_type=f32
    )
    factor = 1.0 / math.sqrt(saved.shape[0] * lax.axis_size("dev"))
    sum_expand, sum_reduce = summed_over_dev((local_expand, local_reduce), factor)
    result = grad.astype(f32) + lax.dot_general(
        slope, expand, (((1,), (1,)), ((), ())), preferred_element_type=f32
    )
    return (result.astype(bf16)[None], sum_expand[None], sum_reduce[None])


def shards(
    late_sent,
    entry_rows,
    gain_first,
    shift_first,
    expand_late,
    gain_inner,
    shift_inner,
    reduce_late,
    early_saved,
    upstream_grad,
    exit_grad,
    expand_early,
    reduce_early,
):
    late_out = late_part(
        late_sent,
        entry_rows,
        gain_first,
        shift_first,
        expand_late,
        gain_inner,
        shift_inner,
        reduce_late,
    )
    input_grad, grad_expand, grad_reduce = early_part(
        early_saved, upstream_grad, exit_grad, expand_early, reduce_early
    )
    return (late_out, input_grad, grad_expand, grad_reduce)


def solution(mesh):
    in_specs = (
        P("section", "dev", None),
        P("dev", None),
        P("section", None),
        P("section", None),
        P("section", None, "dev"),
        P("section", "dev"),
        P("section", "dev"),
        P("section", "dev", None),
        P("section", "dev", None),
        P("section", "dev", None),
        P("dev", None),
        P("section", None, None),
        P("section", None, None),
    )
    out_specs = (
        P("section", "dev", None),
        P("section", "dev", None),
        P("section", None, None),
        P("section", None, None),
    )
    return jax.shard_map(shards, mesh=mesh, in_specs=in_specs, out_specs=out_specs, check_vma=False)
```

time: 183 us -> 108 us (0.59)
  blocking collectives: 41.6 us -> 0 us
  waiting for transfers between devices: 86.8 us -> 47.9 us
  starting transfers between devices: 7.37 us -> 33.6 us
  between operations: 14.9 us -> 1.16 us
  local copies, waits for them, and re-layouts: 6.93 us -> 0.29 us
    ppermute x0 -> x27, waiting for transfers between devices: none -> 44.5 us  [the longest x18 42.1 us: across(): return lax.ppermute(x, 'dev', pairs)]
    psum x1 -> x0, waiting for transfers between devices: 37.3 us -> none  [early_part(): summed_expand, summed_reduce = lax.psum((local_expand, local_reduce), 'dev')]
    ppermute x0 -> x27, starting transfers between devices: none -> 27.3 us  [the longest x18 25.8 us: across(): return lax.ppermute(x, 'dev', pairs)]
    all_gather x1 -> x0, waiting for transfers between devices: 26.5 us -> none  [late_part(): lax.all_gather(own_rows, 'dev', axis=0, tiled=True).astype(jnp.float32)]
    unnamed x1 -> x0, blocking collectives: 26 us -> none
    ppermute x2, waiting for transfers between devices: 22.9 us -> 3.41 us  [from_behind(): return lax.ppermute(x, axis, pairs)]
    psum x1 -> x0, blocking collectives: 15.7 us -> none  [late_part(): lax.psum((jnp.sum(values, axis=0), jnp.sum(values * values, axis=0)), 'dev')]
    unnamed x34 -> x22, local copies, waits for them, and re-layouts: 3.93 us -> 0.07 us
  transfers between devices with their start and end apart: 5 -> 29, of which waited for: 4 -> 14; matrix products, arithmetic and copies ran while one was open for 7% -> 22% of each run, Pallas kernels for 0% -> 0%
where the time goes in v1:
time: 108 us; the launch traced here: 107 us
  waiting for transfers between devices  47.9 us (44%)
  starting transfers between devices  33.6 us (31%)
  matrix products  19.2 us (18%)
  other arithmetic  5.28 us (5%)
  between operations  1.16 us (1%)
    ppermute x18, waiting for transfers between devices, across(): return lax.ppermute(x, 'dev', pairs)  42.1 us
    ppermute x18, starting transfers between devices, across(): return lax.ppermute(x, 'dev', pairs)  25.8 us
    ppermute x2, starting transfers between devices, from_behind(): return lax.ppermute(x, axis, pairs)  6.31 us
    dot_general x1, matrix products, early_part(): pre = jnp.dot(saved, expand, preferred_element_type=f32)  4.76 us
    dot_general x2, matrix products, expanded(): lax.dot_general(first, weight, (((2,), (0,)), ((), ())), preferred_elemen...  4.04 us
    ppermute x2, waiting for transfers between devices, from_behind(): return lax.ppermute(x, axis, pairs)  3.41 us
    dot_general x1, matrix products, early_part(): lax.dot_general(grad, reduce_weight, (((1,), (1,)), ((), ())), preferred_...  2.91 us
    ppermute x9, waiting for transfers between devices, swap(): lax.ppermute(x, 'dev', [(i, i ^ 1) for i in range(lax.axis_size('dev'))])  2.38 us
  transfers between devices with their start and end apart: 29, of which 14 were waited for; matrix products, arithmetic and copies ran while one was open for 22% of the time, Pallas kernels for 0%

profile of v1, /device:TPU:0, one launch (start us, length us, event | category | flops | bytes accessed | tf_op | source)
XLA Modules:
  0.0 107.4 jit_solution(7807776441780113066)
XLA Ops:
  0.6 5.0 %collective-permute-start = (bf16[98,1024]{1,0:T(8,128)(2,1)}, bf16[98,1024]{1,0:T(8,128)(2,1)S(1)}, u32[]{:S(2)}, u32[]{:S(2)}) collective-permute-start(bf16[98,1024]{1,0:T(8,128)(2,1)} %bitcast.242), channel_id=1, source_target_pairs={{0,8},{8,16},{16,24},{1,9},{9,17},{17,25},{2,10},{10,18},{18,26},{... | collective-permute-start | bytes 602120 | tf_op jit(solution)/shard_map/ppermute | solution.py:16
  5.7 1.3 %collective-permute-start.12 = (bf16[1568,256]{1,0:T(8,128)(2,1)}, bf16[1568,256]{1,0:T(8,128)(2,1)S(1)}, u32[]{:S(2)}, u32[]{:S(2)}) collective-permute-start(bf16[1568,256]{1,0:T(8,128)(2,1)} %bitcast.241), channel_id=1, source_target_pairs={{8,0},{16,8},{24,16},{9,1},{17,9},{25,17},{10,2},{18,10},{26,18},{... | collective-permute-start | bytes 2408456 | tf_op jit(solution)/shard_map/ppermute | solution.py:16
  7.0 0.1 collective-permute-start.5
  7.1 3.4 %collective-permute-done = bf16[98,1024]{1,0:T(8,128)(2,1)S(1)} collective-permute-done((bf16[98,1024]{1,0:T(8,128)(2,1)}, bf16[98,1024]{1,0:T(8,128)(2,1)S(1)}, u32[]{:S(2)}, u32[]{:S(2)}) %collective-permute-start) | collective-permute-done | bytes 200736 | tf_op jit(solution)/shard_map/ppermute | solution.py:16
  10.5 1.0 broadcast_select_fusion.1
  11.5 1.6 %collective-permute-start.1 = (bf16[98,1024]{1,0:T(8,128)(2,1)S(1)}, bf16[98,1024]{1,0:T(8,128)(2,1)S(1)}, u32[]{:S(2)}, u32[]{:S(2)}) collective-permute-start(bf16[98,1024]{1,0:T(8,128)(2,1)S(1)} %broadcast_select_fusion.1), channel_id=1, source_target_pairs={{2,0},{3,1},{0,2},{1,3},{6,4},{7,5},{4,6},{5,7},{10,8},{11,9},{8,1... | collective-permute-start | bytes 602120 | tf_op jit(solution)/shard_map/ppermute | solution.py:38
  13.1 2.6 %collective-permute-start.2 = (bf16[98,1024]{1,0:T(8,128)(2,1)S(1)}, bf16[98,1024]{1,0:T(8,128)(2,1)S(1)}, u32[]{:S(2)}, u32[]{:S(2)}) collective-permute-start(bf16[98,1024]{1,0:T(8,128)(2,1)S(1)} %broadcast_select_fusion.1), channel_id=1, source_target_pairs={{4,0},{5,1},{6,2},{7,3},{0,4},{1,5},{2,6},{3,7},{12,8},{13,9},{14,... | collective-permute-start | bytes 602120 | tf_op jit(solution)/shard_map/ppermute | solution.py:38
  15.7 0.2 collective-permute-start.3
  15.9 4.8 %fusion.19 = f32[1568,1024]{1,0:T(8,128)} fusion(bf16[1,1568,256]{2,1,0:T(8,128)(2,1)S(1)} %copy-done, bf16[1,256,1024]{2,1,0:T(8,128)(2,1)} %param.24), kind=kOutput, calls=%fused_computation.35 | convolution fusion | flops 822083584 | bytes 7749632 | tf_op jit(solution)/shard_map/dot_general | solution.py:154
  20.7 0.1 collective-permute-done.1
  20.8 10.5 %collective-permute-done.2 = bf16[98,1024]{1,0:T(8,128)(2,1)S(1)} collective-permute-done((bf16[98,1024]{1,0:T(8,128)(2,1)S(1)}, bf16[98,1024]{1,0:T(8,128)(2,1)S(1)}, u32[]{:S(2)}, u32[]{:S(2)}) %collective-permute-start.2) | collective-permute-done | bytes 200736 | tf_op jit(solution)/shard_map/ppermute | solution.py:38
  31.3 0.3 convert_reduce_fusion
  31.6 0.6 collective-permute-start.4
  32.2 1.8 %collective-permute-done.4 = f32[2,1024]{1,0:T(2,128)S(1)} collective-permute-done((f32[2,1024]{1,0:T(2,128)S(1)}, f32[2,1024]{1,0:T(2,128)S(1)}, u32[]{:S(2)}, u32[]{:S(2)}) %collective-permute-start.4) | collective-permute-done | bytes 8224 | tf_op jit(solution)/shard_map/ppermute | solution.py:20
  34.1 2.1 %fusion.61 = (f32[512]{0:T(512)S(1)}, f32[512]{0:T(512)S(1)}, f32[4,98,512]{2,1,0:T(8,128)S(1)}) fusion(bf16[1,1024,512]{2,1,0:T(8,128)(2,1)} %param.17, f32[1024]{0:T(1024)S(1)} %get-tuple-element.18, f32[1024]{0:T(1024)S(1)} %get-tuple-element.19, bf16[1,98,1024]{2,1,0:T(8,128)(2,1)S(1)} %bitcast.214, bf16[1,98,1024]{2,1,0:T(8,128)(2,1)S(1)} %bitcast.211, ...), kind=kOutput, calls=%fused_computation.127 | convolution fusion | flops 416058368 | bytes 2666496 | tf_op jit(solution)/shard_map/dot_general | solution.py:86
  36.2 0.1 broadcast_select_fusion
  36.3 1.9 %fusion = f32[1024,256]{1,0:T(8,128)S(1)} fusion(bf16[1568,256]{1,0:T(8,128)(2,1)S(1)} %broadcast_select_fusion, f32[1568,1024]{1,0:T(8,128)S(1)} %bitcast.187), kind=kOutput, calls=%fused_computation.3 | convolution fusion | flops 830111744 | bytes 8273920 | tf_op jit(solution)/shard_map/dot_general | solution.py:161
  38.3 0.2 collective-permute-start.21
  38.5 2.9 %multiply_convert_fusion.1 = bf16[1568,1024]{1,0:T(8,128)(2,1)S(1)} fusion(f32[1568,1024]{1,0:T(8,128)S(1)} %bitcast.187, bf16[1568,256]{1,0:T(8,128)(2,1)S(1)} %broadcast_select_fusion, bf16[1,1024,256]{2,1,0:T(8,128)(2,1)S(1)} %copy-done.8), kind=kOutput, calls=%fused_computation.1 | convolution fusion | flops 836534272 | bytes 10960896 | tf_op jit(solution)/shard_map/dot_general | solution.py:156
  41.4 1.2 %fusion.17 = f32[1024,256]{0,1:T(8,128)S(1)} fusion(bf16[1568,1024]{1,0:T(8,128)(2,1)S(1)} %multiply_convert_fusion.1, bf16[1,1568,256]{2,1,0:T(8,128)(2,1)S(1)} %copy-done), kind=kOutput, calls=%fused_computation.33 | convolution fusion | flops 822083584 | bytes 5062656 | tf_op jit(solution)/shard_map/dot_general | solution.py:158
  42.6 2.0 %fusion.16 = bf16[1,1568,256]{2,1,0:T(8,128)(2,1)} fusion(bf16[1568,256]{1,0:T(8,128)(2,1)S(1)} %broadcast_select_fusion, bf16[1568,1024]{1,0:T(8,128)(2,1)S(1)} %multiply_convert_fusion.1, bf16[1,256,1024]{2,1,0:T(8,128)(2,1)S(1)} %copy-done.3), kind=kOutput, calls=%fused_computation.32 | convolution fusion | flops 823287808 | bytes 5341184 | tf_op jit(solution)/shard_map/dot_general | solution.py:166
  44.6 1.9 %fusion.60 = (f32[512]{0:T(512)S(1)}, f32[512]{0:T(512)S(1)}, f32[4,98,512]{2,1,0:T(8,128)S(1)}) fusion(bf16[1024,512]{1,0:T(8,128)(2,1)} %collective-permute-done.5, f32[1024]{0:T(1024)S(1)} %get-tuple-element.18, f32[1024]{0:T(1024)S(1)} %get-tuple-element.19, bf16[1,98,1024]{2,1,0:T(8,128)(2,1)S(1)} %bitcast.215, ...), kind=kOutput, calls=%fused_computation.126 | convolution fusion | flops 416058368 | bytes 2666496 | tf_op jit(solution)/shard_map/dot_general | solution.py:86
  46.5 0.3 collective-permute-start.6
  46.9 0.3 collective-permute-start.13
  47.2 0.6 collective-permute-done.6
  47.8 0.2 multiply_convert_fusion.4
  48.1 0.3 fusion.41
  48.4 0.2 multiply_convert_fusion.3
  48.7 0.3 fusion.40
  49.0 0.3 fusion.39
  49.3 0.3 fusion.38
  49.6 0.3 fusion.9
  49.9 2.0 %collective-permute-start.9 = (bf16[98,1024]{1,0:T(8,128)(2,1)S(1)}, bf16[98,1024]{1,0:T(8,128)(2,1)S(1)}, u32[]{:S(2)}, u32[]{:S(2)}) collective-permute-start(bf16[98,1024]{1,0:T(8,128)(2,1)S(1)} %fusion.9), channel_id=1, source_target_pairs={{0,6},{1,7},{2,4},{3,5},{4,2},{5,3},{6,0},{7,1},{8,14},{9,15},{10,... | collective-permute-start | bytes 602120 | tf_op jit(solution)/shard_map/ppermute | solution.py:38
  52.0 0.3 fusion.10
  52.3 1.3 %collective-permute-start.10 = (bf16[98,1024]{1,0:T(8,128)(2,1)S(1)}, bf16[98,1024]{1,0:T(8,128)(2,1)S(1)}, u32[]{:S(2)}, u32[]{:S(2)}) collective-permute-start(bf16[98,1024]{1,0:T(8,128)(2,1)S(1)} %fusion.10), channel_id=1, source_target_pairs={{0,4},{1,5},{2,6},{3,7},{4,0},{5,1},{6,2},{7,3},{8,12},{9,13},{10,... | collective-permute-start | bytes 602120 | tf_op jit(solution)/shard_map/ppermute | solution.py:38
  53.6 0.3 convolution_add_fusion.3
  53.9 0.3 fusion.11
  54.4 2.5 %collective-permute-start.22 = (bf16[128,256]{1,0:T(8,128)(2,1)S(1)}, bf16[128,256]{1,0:T(8,128)(2,1)S(1)}, u32[]{:S(2)}, u32[]{:S(2)}) collective-permute-start(bf16[128,256]{1,0:T(8,128)(2,1)S(1)} %get-tuple-element.20), channel_id=1, source_target_pairs={{0,6},{1,7},{2,4},{3,5},{4,2},{5,3},{6,0},{7,1},{8,14},{9,15},{10,... | collective-permute-start | bytes 196616 | tf_op jit(solution)/shard_map/ppermute | solution.py:38
  56.9 0.1 collective-permute-start.23
  57.0 1.8 %collective-permute-start.24 = (bf16[128,256]{1,0:T(8,128)(2,1)S(1)}, bf16[128,256]{1,0:T(8,128)(2,1)S(1)}, u32[]{:S(2)}, u32[]{:S(2)}) collective-permute-start(bf16[128,256]{1,0:T(8,128)(2,1)S(1)} %get-tuple-element.21), channel_id=1, source_target_pairs={{0,2},{1,3},{2,0},{3,1},{4,6},{5,7},{6,4},{7,5},{8,10},{9,11},{10,... | collective-permute-start | bytes 196616 | tf_op jit(solution)/shard_map/ppermute | solution.py:38
  58.8 0.1 bitcast_add_fusion.1
  58.9 7.1 %collective-permute-done.22 = bf16[128,256]{1,0:T(8,128)(2,1)S(1)} collective-permute-done((bf16[128,256]{1,0:T(8,128)(2,1)S(1)}, bf16[128,256]{1,0:T(8,128)(2,1)S(1)}, u32[]{:S(2)}, u32[]{:S(2)}) %collective-permute-start.22) | collective-permute-done | bytes 65568 | tf_op jit(solution)/shard_map/ppermute | solution.py:38
  66.0 2.0 %collective-permute-start.14 = (bf16[32,1024]{1,0:T(8,128)(2,1)S(1)}, bf16[32,1024]{1,0:T(8,128)(2,1)S(1)}, u32[]{:S(2)}, u32[]{:S(2)}) collective-permute-start(bf16[32,1024]{1,0:T(8,128)(2,1)S(1)} %get-tuple-element.23), channel_id=1, source_target_pairs={{0,6},{1,7},{2,4},{3,5},{4,2},{5,3},{6,0},{7,1},{8,14},{9,15},{10,... | collective-permute-start | bytes 196616 | tf_op jit(solution)/shard_map/ppermute | solution.py:38
  68.0 11.4 %collective-permute-done.23 = bf16[128,256]{1,0:T(8,128)(2,1)S(1)} collective-permute-done((bf16[128,256]{1,0:T(8,128)(2,1)S(1)}, bf16[128,256]{1,0:T(8,128)(2,1)S(1)}, u32[]{:S(2)}, u32[]{:S(2)}) %collective-permute-start.23) | collective-permute-done | bytes 65568 | tf_op jit(solution)/shard_map/ppermute | solution.py:38
  79.4 1.3 %collective-permute-start.15 = (bf16[32,1024]{1,0:T(8,128)(2,1)S(1)}, bf16[32,1024]{1,0:T(8,128)(2,1)S(1)}, u32[]{:S(2)}, u32[]{:S(2)}) collective-permute-start(bf16[32,1024]{1,0:T(8,128)(2,1)S(1)} %get-tuple-element.25), channel_id=1, source_target_pairs={{0,4},{1,5},{2,6},{3,7},{4,0},{5,1},{6,2},{7,3},{8,12},{9,13},{10,... | collective-permute-start | bytes 196616 | tf_op jit(solution)/shard_map/ppermute | solution.py:38
  80.7 1.7 %collective-permute-start.16 = (bf16[32,1024]{1,0:T(8,128)(2,1)S(1)}, bf16[32,1024]{1,0:T(8,128)(2,1)S(1)}, u32[]{:S(2)}, u32[]{:S(2)}) collective-permute-start(bf16[32,1024]{1,0:T(8,128)(2,1)S(1)} %get-tuple-element.24), channel_id=1, source_target_pairs={{0,2},{1,3},{2,0},{3,1},{4,6},{5,7},{6,4},{7,5},{8,10},{9,11},{10,... | collective-permute-start | bytes 196616 | tf_op jit(solution)/shard_map/ppermute | solution.py:38
  82.5 2.3 %collective-permute-start.11 = (bf16[98,1024]{1,0:T(8,128)(2,1)S(1)}, bf16[98,1024]{1,0:T(8,128)(2,1)S(1)}, u32[]{:S(2)}, u32[]{:S(2)}) collective-permute-start(bf16[98,1024]{1,0:T(8,128)(2,1)S(1)} %fusion.11), channel_id=1, source_target_pairs={{0,2},{1,3},{2,0},{3,1},{4,6},{5,7},{6,4},{7,5},{8,10},{9,11},{10,... | collective-permute-start | bytes 602120 | tf_op jit(solution)/shard_map/ppermute | solution.py:38
  84.8 1.0 collective-permute-done.15
  85.8 1.6 %collective-permute-start.25 = (bf16[128,256]{1,0:T(8,128)(2,1)S(1)}, bf16[128,256]{1,0:T(8,128)(2,1)S(1)}, u32[]{:S(2)}, u32[]{:S(2)}) collective-permute-start(bf16[128,256]{1,0:T(8,128)(2,1)S(1)} %get-tuple-element.11), channel_id=1, source_target_pairs={{6,0},{7,1},{4,2},{5,3},{2,4},{3,5},{0,6},{1,7},{14,8},{15,9},{12,... | collective-permute-start | bytes 196616 | tf_op jit(solution)/shard_map/ppermute | solution.py:38
  87.5 4.8 %collective-permute-done.25 = bf16[128,256]{1,0:T(8,128)(2,1)S(1)} collective-permute-done((bf16[128,256]{1,0:T(8,128)(2,1)S(1)}, bf16[128,256]{1,0:T(8,128)(2,1)S(1)}, u32[]{:S(2)}, u32[]{:S(2)}) %collective-permute-start.25) | collective-permute-done | bytes 65568 | tf_op jit(solution)/shard_map/ppermute | solution.py:38
  92.3 1.3 %collective-permute-done.26 = bf16[128,256]{1,0:T(8,128)(2,1)S(1)} collective-permute-done((bf16[128,256]{1,0:T(8,128)(2,1)S(1)}, bf16[128,256]{1,0:T(8,128)(2,1)S(1)}, u32[]{:S(2)}, u32[]{:S(2)}) %collective-permute-start.26) | collective-permute-done | bytes 65568 | tf_op jit(solution)/shard_map/ppermute | solution.py:38
  93.7 2.8 %collective-permute-start.17 = (bf16[32,1024]{1,0:T(8,128)(2,1)S(1)}, bf16[32,1024]{1,0:T(8,128)(2,1)S(1)}, u32[]{:S(2)}, u32[]{:S(2)}) collective-permute-start(bf16[32,1024]{1,0:T(8,128)(2,1)S(1)} %get-tuple-element.13), channel_id=1, source_target_pairs={{6,0},{7,1},{4,2},{5,3},{2,4},{3,5},{0,6},{1,7},{14,8},{15,9},{12,... | collective-permute-start | bytes 196616 | tf_op jit(solution)/shard_map/ppermute | solution.py:38
  96.5 0.2 collective-permute-done.27
  96.7 1.1 %collective-permute-start.18 = (bf16[32,1024]{1,0:T(8,128)(2,1)S(1)}, bf16[32,1024]{1,0:T(8,128)(2,1)S(1)}, u32[]{:S(2)}, u32[]{:S(2)}) collective-permute-start(bf16[32,1024]{1,0:T(8,128)(2,1)S(1)} %get-tuple-element.13), channel_id=1, source_target_pairs={{4,0},{5,1},{6,2},{7,3},{0,4},{1,5},{2,6},{3,7},{12,8},{13,9},{14,... | collective-permute-start | bytes 196616 | tf_op jit(solution)/shard_map/ppermute | solution.py:38
  97.8 2.1 %collective-permute-done.17 = bf16[32,1024]{1,0:T(8,128)(2,1)S(1)} collective-permute-done((bf16[32,1024]{1,0:T(8,128)(2,1)S(1)}, bf16[32,1024]{1,0:T(8,128)(2,1)S(1)}, u32[]{:S(2)}, u32[]{:S(2)}) %collective-permute-start.17) | collective-permute-done | bytes 65568 | tf_op jit(solution)/shard_map/ppermute | solution.py:38
  99.9 0.7 collective-permute-start.19
  100.6 1.9 %collective-permute-done.18 = bf16[32,1024]{1,0:T(8,128)(2,1)S(1)} collective-permute-done((bf16[32,1024]{1,0:T(8,128)(2,1)S(1)}, bf16[32,1024]{1,0:T(8,128)(2,1)S(1)}, u32[]{:S(2)}, u32[]{:S(2)}) %collective-permute-start.18) | collective-permute-done | bytes 65568 | tf_op jit(solution)/shard_map/ppermute | solution.py:38
  102.5 1.6 %collective-permute-done.19 = bf16[32,1024]{1,0:T(8,128)(2,1)S(1)} collective-permute-done((bf16[32,1024]{1,0:T(8,128)(2,1)S(1)}, bf16[32,1024]{1,0:T(8,128)(2,1)S(1)}, u32[]{:S(2)}, u32[]{:S(2)}) %collective-permute-start.19) | collective-permute-done | bytes 65568 | tf_op jit(solution)/shard_map/ppermute | solution.py:38
  104.2 0.1 collective-permute-start.20
  104.3 0.8 fusion.29
  105.1 0.1 maximum_select_fusion.1
  105.2 1.0 bitcast_convert_fusion
  106.2 0.1 maximum_select_fusion
  106.3 1.1 %bitcast_convert_fusion.1 = f32[1,256,1024]{2,1,0:T(8,128)} fusion(bf16[1,256,1024]{2,1,0:T(8,128)(2,1)S(1)} %bitcast.188), kind=kLoop, calls=%fused_computation.41 | loop fusion | flops 262144 | bytes 1572864 | tf_op jit(solution)/shard_map/convert_element_type | solution.py:143
  (71 shorter events, 0.6 us)
Async XLA Ops:
  0.6 15.3 %copy-start = (bf16[1,1568,256]{2,1,0:T(8,128)(2,1)S(1)}, bf16[1,1568,256]{2,1,0:T(8,128)(2,1)}, u32[]{:S(2)}) copy-start(bf16[1,1568,256]{2,1,0:T(8,128)(2,1)} %param.21) | copy-start | bytes 2408452
  0.6 9.8 %collective-permute-start = (bf16[98,1024]{1,0:T(8,128)(2,1)}, bf16[98,1024]{1,0:T(8,128)(2,1)S(1)}, u32[]{:S(2)}, u32[]{:S(2)}) collective-permute-start(bf16[98,1024]{1,0:T(8,128)(2,1)} %bitcast.242), channel_id=1, source_target_pairs={{0,8},{8,16},{16,24},{1,9},{9,17},{17,25},{2,10},{10,18},{18,26},{... | collective-permute-start | bytes 602120 | tf_op jit(solution)/shard_map/ppermute | solution.py:16
  5.7 30.5 %collective-permute-start.12 = (bf16[1568,256]{1,0:T(8,128)(2,1)}, bf16[1568,256]{1,0:T(8,128)(2,1)S(1)}, u32[]{:S(2)}, u32[]{:S(2)}) collective-permute-start(bf16[1568,256]{1,0:T(8,128)(2,1)} %bitcast.241), channel_id=1, source_target_pairs={{8,0},{16,8},{24,16},{9,1},{17,9},{25,17},{10,2},{18,10},{26,18},{... | collective-permute-start | bytes 2408456 | tf_op jit(solution)/shard_map/ppermute | solution.py:16
  7.0 37.6 %collective-permute-start.5 = (bf16[1024,512]{1,0:T(8,128)(2,1)}, bf16[1024,512]{1,0:T(8,128)(2,1)}, u32[]{:S(2)}, u32[]{:S(2)}) collective-permute-start(bf16[1024,512]{1,0:T(8,128)(2,1)} %bitcast.240), channel_id=1, source_target_pairs={{0,1},{1,0},{2,3},{3,2},{4,5},{5,4},{6,7},{7,6},{8,9},{9,8},{10,11... | collective-permute-start | bytes 3145736 | tf_op jit(solution)/shard_map/ppermute | solution.py:20
  11.4 9.3 %copy-start.4 = (f32[1,512]{1,0:T(1,128)S(1)}, f32[1,512]{1,0:T(1,128)}, u32[]{:S(2)}) copy-start(f32[1,512]{1,0:T(1,128)} %param.19) | copy-start | bytes 6148
  11.4 9.3 %copy-start.5 = (f32[1,512]{1,0:T(1,128)S(1)}, f32[1,512]{1,0:T(1,128)}, u32[]{:S(2)}) copy-start(f32[1,512]{1,0:T(1,128)} %param.18) | copy-start | bytes 6148
  11.4 19.8 %copy-start.1 = (bf16[1,512,1024]{2,1,0:T(8,128)(2,1)S(1)}, bf16[1,512,1024]{2,1,0:T(8,128)(2,1)}, u32[]{:S(2)}) copy-start(bf16[1,512,1024]{2,1,0:T(8,128)(2,1)} %param.20) | copy-start | bytes 3145732
  11.5 22.5 %copy-start.6 = (f32[1,1024]{1,0:T(1,128)S(1)}, f32[1,1024]{1,0:T(1,128)}, u32[]{:S(2)}) copy-start(f32[1,1024]{1,0:T(1,128)} %param.16) | copy-start | bytes 12292
  11.5 22.5 %copy-start.7 = (f32[1,1024]{1,0:T(1,128)S(1)}, f32[1,1024]{1,0:T(1,128)}, u32[]{:S(2)}) copy-start(f32[1,1024]{1,0:T(1,128)} %param.15) | copy-start | bytes 12292
  11.5 9.3 %collective-permute-start.1 = (bf16[98,1024]{1,0:T(8,128)(2,1)S(1)}, bf16[98,1024]{1,0:T(8,128)(2,1)S(1)}, u32[]{:S(2)}, u32[]{:S(2)}) collective-permute-start(bf16[98,1024]{1,0:T(8,128)(2,1)S(1)} %broadcast_select_fusion.1), channel_id=1, source_target_pairs={{2,0},{3,1},{0,2},{1,3},{6,4},{7,5},{4,6},{5,7},{10,8},{11,9},{8,1... | collective-permute-start | bytes 602120 | tf_op jit(solution)/shard_map/ppermute | solution.py:38
  13.1 18.2 %collective-permute-start.2 = (bf16[98,1024]{1,0:T(8,128)(2,1)S(1)}, bf16[98,1024]{1,0:T(8,128)(2,1)S(1)}, u32[]{:S(2)}, u32[]{:S(2)}) collective-permute-start(bf16[98,1024]{1,0:T(8,128)(2,1)S(1)} %broadcast_select_fusion.1), channel_id=1, source_target_pairs={{4,0},{5,1},{6,2},{7,3},{0,4},{1,5},{2,6},{3,7},{12,8},{13,9},{14,... | collective-permute-start | bytes 602120 | tf_op jit(solution)/shard_map/ppermute | solution.py:38
  15.7 15.6 %collective-permute-start.3 = (bf16[98,1024]{1,0:T(8,128)(2,1)S(1)}, bf16[98,1024]{1,0:T(8,128)(2,1)S(1)}, u32[]{:S(2)}, u32[]{:S(2)}) collective-permute-start(bf16[98,1024]{1,0:T(8,128)(2,1)S(1)} %broadcast_select_fusion.1), channel_id=1, source_target_pairs={{6,0},{7,1},{4,2},{5,3},{2,4},{3,5},{0,6},{1,7},{14,8},{15,9},{12,... | collective-permute-start | bytes 602120 | tf_op jit(solution)/shard_map/ppermute | solution.py:38
  20.8 11.3 %collective-permute-start.7 = (f32[2,512]{1,0:T(2,128)S(1)}, f32[2,512]{1,0:T(2,128)S(1)}, u32[]{:S(2)}, u32[]{:S(2)}) collective-permute-start(f32[2,512]{1,0:T(2,128)S(1)} %pad_maximum_fusion.5), channel_id=1, source_target_pairs={{0,1},{1,0},{2,3},{3,2},{4,5},{5,4},{6,7},{7,6},{8,9},{9,8},{10,11... | collective-permute-start | bytes 12296 | tf_op jit(solution)/shard_map/ppermute | solution.py:20
  31.3 18.3 %collective-permute-start.8 = (bf16[512,1024]{1,0:T(8,128)(2,1)S(1)}, bf16[512,1024]{1,0:T(8,128)(2,1)S(1)}, u32[]{:S(2)}, u32[]{:S(2)}) collective-permute-start(bf16[512,1024]{1,0:T(8,128)(2,1)S(1)} %bitcast.185), channel_id=1, source_target_pairs={{0,1},{1,0},{2,3},{3,2},{4,5},{5,4},{6,7},{7,6},{8,9},{9,8},{10,11... | collective-permute-start | bytes 3145736 | tf_op jit(solution)/shard_map/ppermute | solution.py:20
  31.3 5.0 %slice-start = ((s8[6422528]{0:T(1024)(128)(4,1)}), s8[4194304]{0:T(1024)(128)(4,1)S(1)}, s32[]{:S(2)}) async-start(s8[6422528]{0:T(1024)(128)(4,1)} %bitcast.186), calls=%async_computation | async-start | bytes 8388608
  31.6 2.4 %collective-permute-start.4 = (f32[2,1024]{1,0:T(2,128)S(1)}, f32[2,1024]{1,0:T(2,128)S(1)}, u32[]{:S(2)}, u32[]{:S(2)}) collective-permute-start(f32[2,1024]{1,0:T(2,128)S(1)} %pad_maximum_fusion.1), channel_id=1, source_target_pairs={{0,1},{1,0},{2,3},{3,2},{4,5},{5,4},{6,7},{7,6},{8,9},{9,8},{10,11... | collective-permute-start | bytes 24584 | tf_op jit(solution)/shard_map/ppermute | solution.py:20
  34.0 2.1 %copy-start.2 = (bf16[1568,256]{1,0:T(8,128)(2,1)S(1)}, bf16[1568,256]{1,0:T(8,128)(2,1)}, u32[]{:S(2)}) copy-start(bf16[1568,256]{1,0:T(8,128)(2,1)} %param.23) | copy-start | bytes 2408452
  34.0 2.3 %slice-start.1 = ((s8[6422528]{0:T(1024)(128)(4,1)}), s8[2228224]{0:T(1024)(128)(4,1)S(1)}, s32[]{:S(2)}) async-start(s8[6422528]{0:T(1024)(128)(4,1)} %bitcast.186), calls=%async_computation.1 | async-start | bytes 4456448
  36.3 2.2 %copy-start.8 = (bf16[1,1024,256]{2,1,0:T(8,128)(2,1)S(1)}, bf16[1,1024,256]{2,1,0:T(8,128)(2,1)}, u32[]{:S(2)}) copy-start(bf16[1,1024,256]{2,1,0:T(8,128)(2,1)} %param.25) | copy-start | bytes 1572868
  38.3 16.0 %collective-permute-start.21 = (bf16[512,256]{1,0:T(8,128)(2,1)S(1)}, bf16[512,256]{1,0:T(8,128)(2,1)S(1)}, u32[]{:S(2)}, u32[]{:S(2)}) collective-permute-start(bf16[512,256]{1,0:T(8,128)(2,1)S(1)} %fusion.28), channel_id=1, source_target_pairs={{0,1},{1,0},{2,3},{3,2},{4,5},{5,4},{6,7},{7,6},{8,9},{9,8},{10,11... | collective-permute-start | bytes 786440 | tf_op jit(solution)/shard_map/ppermute | solution.py:20
  41.4 1.2 %copy-start.3 = (bf16[1,256,1024]{2,1,0:T(8,128)(2,1)S(1)}, bf16[1,256,1024]{2,1,0:T(8,128)(2,1)}, u32[]{:S(2)}) copy-start(bf16[1,256,1024]{2,1,0:T(8,128)(2,1)} %param.24) | copy-start | bytes 1572868
  46.5 1.2 %collective-permute-start.6 = (f32[2,2,512]{2,1,0:T(2,128)S(1)}, f32[2,2,512]{2,1,0:T(2,128)S(1)}, u32[]{:S(2)}, u32[]{:S(2)}) collective-permute-start(f32[2,2,512]{2,1,0:T(2,128)S(1)} %pad_maximum_fusion.2), channel_id=1, source_target_pairs={{0,1},{1,0},{2,3},{3,2},{4,5},{5,4},{6,7},{7,6},{8,9},{9,8},{10,11... | collective-permute-start | bytes 24584 | tf_op jit(solution)/shard_map/ppermute | solution.py:20
  46.9 10.1 %collective-permute-start.13 = (bf16[128,1024]{1,0:T(8,128)(2,1)S(1)}, bf16[128,1024]{1,0:T(8,128)(2,1)S(1)}, u32[]{:S(2)}, u32[]{:S(2)}) collective-permute-start(bf16[128,1024]{1,0:T(8,128)(2,1)S(1)} %fusion.27), channel_id=1, source_target_pairs={{0,1},{1,0},{2,3},{3,2},{4,5},{5,4},{6,7},{7,6},{8,9},{9,8},{10,11... | collective-permute-start | bytes 786440 | tf_op jit(solution)/shard_map/ppermute | solution.py:20
  49.9 54.3 %collective-permute-start.9 = (bf16[98,1024]{1,0:T(8,128)(2,1)S(1)}, bf16[98,1024]{1,0:T(8,128)(2,1)S(1)}, u32[]{:S(2)}, u32[]{:S(2)}) collective-permute-start(bf16[98,1024]{1,0:T(8,128)(2,1)S(1)} %fusion.9), channel_id=1, source_target_pairs={{0,6},{1,7},{2,4},{3,5},{4,2},{5,3},{6,0},{7,1},{8,14},{9,15},{10,... | collective-permute-start | bytes 602120 | tf_op jit(solution)/shard_map/ppermute | solution.py:38
  52.3 52.0 %collective-permute-start.10 = (bf16[98,1024]{1,0:T(8,128)(2,1)S(1)}, bf16[98,1024]{1,0:T(8,128)(2,1)S(1)}, u32[]{:S(2)}, u32[]{:S(2)}) collective-permute-start(bf16[98,1024]{1,0:T(8,128)(2,1)S(1)} %fusion.10), channel_id=1, source_target_pairs={{0,4},{1,5},{2,6},{3,7},{4,0},{5,1},{6,2},{7,3},{8,12},{9,13},{10,... | collective-permute-start | bytes 602120 | tf_op jit(solution)/shard_map/ppermute | solution.py:38
  54.4 11.6 %collective-permute-start.22 = (bf16[128,256]{1,0:T(8,128)(2,1)S(1)}, bf16[128,256]{1,0:T(8,128)(2,1)S(1)}, u32[]{:S(2)}, u32[]{:S(2)}) collective-permute-start(bf16[128,256]{1,0:T(8,128)(2,1)S(1)} %get-tuple-element.20), channel_id=1, source_target_pairs={{0,6},{1,7},{2,4},{3,5},{4,2},{5,3},{6,0},{7,1},{8,14},{9,15},{10,... | collective-permute-start | bytes 196616 | tf_op jit(solution)/shard_map/ppermute | solution.py:38
  56.9 22.5 %collective-permute-start.23 = (bf16[128,256]{1,0:T(8,128)(2,1)S(1)}, bf16[128,256]{1,0:T(8,128)(2,1)S(1)}, u32[]{:S(2)}, u32[]{:S(2)}) collective-permute-start(bf16[128,256]{1,0:T(8,128)(2,1)S(1)} %get-tuple-element.22), channel_id=1, source_target_pairs={{0,4},{1,5},{2,6},{3,7},{4,0},{5,1},{6,2},{7,3},{8,12},{9,13},{10,... | collective-permute-start | bytes 196616 | tf_op jit(solution)/shard_map/ppermute | solution.py:38
  57.0 23.6 %collective-permute-start.24 = (bf16[128,256]{1,0:T(8,128)(2,1)S(1)}, bf16[128,256]{1,0:T(8,128)(2,1)S(1)}, u32[]{:S(2)}, u32[]{:S(2)}) collective-permute-start(bf16[128,256]{1,0:T(8,128)(2,1)S(1)} %get-tuple-element.21), channel_id=1, source_target_pairs={{0,2},{1,3},{2,0},{3,1},{4,6},{5,7},{6,4},{7,5},{8,10},{9,11},{10,... | collective-permute-start | bytes 196616 | tf_op jit(solution)/shard_map/ppermute | solution.py:38
  66.0 16.5 %collective-permute-start.14 = (bf16[32,1024]{1,0:T(8,128)(2,1)S(1)}, bf16[32,1024]{1,0:T(8,128)(2,1)S(1)}, u32[]{:S(2)}, u32[]{:S(2)}) collective-permute-start(bf16[32,1024]{1,0:T(8,128)(2,1)S(1)} %get-tuple-element.23), channel_id=1, source_target_pairs={{0,6},{1,7},{2,4},{3,5},{4,2},{5,3},{6,0},{7,1},{8,14},{9,15},{10,... | collective-permute-start | bytes 196616 | tf_op jit(solution)/shard_map/ppermute | solution.py:38
  79.4 6.4 %collective-permute-start.15 = (bf16[32,1024]{1,0:T(8,128)(2,1)S(1)}, bf16[32,1024]{1,0:T(8,128)(2,1)S(1)}, u32[]{:S(2)}, u32[]{:S(2)}) collective-permute-start(bf16[32,1024]{1,0:T(8,128)(2,1)S(1)} %get-tuple-element.25), channel_id=1, source_target_pairs={{0,4},{1,5},{2,6},{3,7},{4,0},{5,1},{6,2},{7,3},{8,12},{9,13},{10,... | collective-permute-start | bytes 196616 | tf_op jit(solution)/shard_map/ppermute | solution.py:38
  80.7 6.8 %collective-permute-start.16 = (bf16[32,1024]{1,0:T(8,128)(2,1)S(1)}, bf16[32,1024]{1,0:T(8,128)(2,1)S(1)}, u32[]{:S(2)}, u32[]{:S(2)}) collective-permute-start(bf16[32,1024]{1,0:T(8,128)(2,1)S(1)} %get-tuple-element.24), channel_id=1, source_target_pairs={{0,2},{1,3},{2,0},{3,1},{4,6},{5,7},{6,4},{7,5},{8,10},{9,11},{10,... | collective-permute-start | bytes 196616 | tf_op jit(solution)/shard_map/ppermute | solution.py:38
  82.5 21.8 %collective-permute-start.11 = (bf16[98,1024]{1,0:T(8,128)(2,1)S(1)}, bf16[98,1024]{1,0:T(8,128)(2,1)S(1)}, u32[]{:S(2)}, u32[]{:S(2)}) collective-permute-start(bf16[98,1024]{1,0:T(8,128)(2,1)S(1)} %fusion.11), channel_id=1, source_target_pairs={{0,2},{1,3},{2,0},{3,1},{4,6},{5,7},{6,4},{7,5},{8,10},{9,11},{10,... | collective-permute-start | bytes 602120 | tf_op jit(solution)/shard_map/ppermute | solution.py:38
  85.8 6.5 %collective-permute-start.25 = (bf16[128,256]{1,0:T(8,128)(2,1)S(1)}, bf16[128,256]{1,0:T(8,128)(2,1)S(1)}, u32[]{:S(2)}, u32[]{:S(2)}) collective-permute-start(bf16[128,256]{1,0:T(8,128)(2,1)S(1)} %get-tuple-element.11), channel_id=1, source_target_pairs={{6,0},{7,1},{4,2},{5,3},{2,4},{3,5},{0,6},{1,7},{14,8},{15,9},{12,... | collective-permute-start | bytes 196616 | tf_op jit(solution)/shard_map/ppermute | solution.py:38
  87.4 6.2 %collective-permute-start.26 = (bf16[128,256]{1,0:T(8,128)(2,1)S(1)}, bf16[128,256]{1,0:T(8,128)(2,1)S(1)}, u32[]{:S(2)}, u32[]{:S(2)}) collective-permute-start(bf16[128,256]{1,0:T(8,128)(2,1)S(1)} %get-tuple-element.11), channel_id=1, source_target_pairs={{4,0},{5,1},{6,2},{7,3},{0,4},{1,5},{2,6},{3,7},{12,8},{13,9},{14,... | collective-permute-start | bytes 196616 | tf_op jit(solution)/shard_map/ppermute | solution.py:38
  92.3 4.3 %collective-permute-start.27 = (bf16[128,256]{1,0:T(8,128)(2,1)S(1)}, bf16[128,256]{1,0:T(8,128)(2,1)S(1)}, u32[]{:S(2)}, u32[]{:S(2)}) collective-permute-start(bf16[128,256]{1,0:T(8,128)(2,1)S(1)} %get-tuple-element.11), channel_id=1, source_target_pairs={{2,0},{3,1},{0,2},{1,3},{6,4},{7,5},{4,6},{5,7},{10,8},{11,9},{8,1... | collective-permute-start | bytes 196616 | tf_op jit(solution)/shard_map/ppermute | solution.py:38
  93.7 6.2 %collective-permute-start.17 = (bf16[32,1024]{1,0:T(8,128)(2,1)S(1)}, bf16[32,1024]{1,0:T(8,128)(2,1)S(1)}, u32[]{:S(2)}, u32[]{:S(2)}) collective-permute-start(bf16[32,1024]{1,0:T(8,128)(2,1)S(1)} %get-tuple-element.13), channel_id=1, source_target_pairs={{6,0},{7,1},{4,2},{5,3},{2,4},{3,5},{0,6},{1,7},{14,8},{15,9},{12,... | collective-permute-start | bytes 196616 | tf_op jit(solution)/shard_map/ppermute | solution.py:38
  96.7 5.8 %collective-permute-start.18 = (bf16[32,1024]{1,0:T(8,128)(2,1)S(1)}, bf16[32,1024]{1,0:T(8,128)(2,1)S(1)}, u32[]{:S(2)}, u32[]{:S(2)}) collective-permute-start(bf16[32,1024]{1,0:T(8,128)(2,1)S(1)} %get-tuple-element.13), channel_id=1, source_target_pairs={{4,0},{5,1},{6,2},{7,3},{0,4},{1,5},{2,6},{3,7},{12,8},{13,9},{14,... | collective-permute-start | bytes 196616 | tf_op jit(solution)/shard_map/ppermute | solution.py:38
  99.9 4.3 %collective-permute-start.19 = (bf16[32,1024]{1,0:T(8,128)(2,1)S(1)}, bf16[32,1024]{1,0:T(8,128)(2,1)S(1)}, u32[]{:S(2)}, u32[]{:S(2)}) collective-permute-start(bf16[32,1024]{1,0:T(8,128)(2,1)S(1)} %get-tuple-element.13), channel_id=1, source_target_pairs={{2,0},{3,1},{0,2},{1,3},{6,4},{7,5},{4,6},{5,7},{10,8},{11,9},{8,1... | collective-permute-start | bytes 196616 | tf_op jit(solution)/shard_map/ppermute | solution.py:38
  102.5 2.6 %collective-permute-start.28 = (bf16[512,256]{1,0:T(8,128)(2,1)S(1)}, bf16[512,256]{1,0:T(8,128)(2,1)S(1)}, u32[]{:S(2)}, u32[]{:S(2)}) collective-permute-start(bf16[512,256]{1,0:T(8,128)(2,1)S(1)} %bitcast.199), channel_id=1, source_target_pairs={{0,1},{1,0},{2,3},{3,2},{4,5},{5,4},{6,7},{7,6},{8,9},{9,8},{10,11... | collective-permute-start | bytes 786440 | tf_op jit(solution)/shard_map/ppermute | solution.py:20
  104.2 2.1 %collective-permute-start.20 = (bf16[128,1024]{1,0:T(8,128)(2,1)S(1)}, bf16[128,1024]{1,0:T(8,128)(2,1)S(1)}, u32[]{:S(2)}, u32[]{:S(2)}) collective-permute-start(bf16[128,1024]{1,0:T(8,128)(2,1)S(1)} %bitcast.197), channel_id=1, source_target_pairs={{0,1},{1,0},{2,3},{3,2},{4,5},{5,4},{6,7},{7,6},{8,9},{9,8},{10,11... | collective-permute-start | bytes 786440 | tf_op jit(solution)/shard_map/ppermute | solution.py:20

commit v2 on v0

v2 whole, which is shorter than its diff:
```python
import functools
import math

import jax
import jax.numpy as jnp
from jax import lax
from jax.experimental import pallas as pl
from jax.experimental.pallas import tpu as pltpu
from jax.sharding import PartitionSpec as P

epsilon = 1e-05
bf16 = jnp.bfloat16
f32 = jnp.float32


def from_behind(x, axis, by):
    peers = lax.axis_size(axis)
    pairs = [(i, i + by) for i in range(peers) if 0 <= i + by < peers]
    return lax.ppermute(x, axis, pairs)


def swap(x):
    return lax.ppermute(x, "dev", [(i, i ^ 1) for i in range(lax.axis_size("dev"))])


def partner(chip, step, count):
    return chip ^ step if count & (count - 1) == 0 else lax.rem(chip + step, count)


def across(x, step, back=False):
    count = lax.axis_size("dev") // 2
    pairs = []
    for chip in range(count):
        other = chip ^ step if count & (count - 1) == 0 else (chip + step) % count
        for core in range(2):
            here, there = 2 * chip + core, 2 * other + core
            pairs.append((there, here) if back else (here, there))
    return lax.ppermute(x, "dev", pairs)


def in_pairs(count):
    return count >= 4 and count & (count - 1) == 0


def gather(x):
    count = lax.axis_size("dev") // 2
    got = {0: x}
    if not in_pairs(count):
        for step in range(count - 1, 0, -1):
            got[step] = across(x, step, back=True)
        return got
    far = range(count - 2, 0, -2)
    for step in far:
        got[step] = across(x, step)
    got[1] = across(x, 1)
    for step in far:
        got[step ^ 1] = across(got[step], 1)
    return got


def scatter(pieces):
    count = lax.axis_size("dev") // 2
    if not in_pairs(count):
        return [across(pieces[step].astype(bf16), step) for step in range(count - 1, 0, -1)]
    far = range(count - 2, 0, -2)
    inner = {}
    for step in far:
        inner[step] = across(pieces[step ^ 1], 1)
    terms = [across(pieces[1], 1)]
    for step in far:
        both = (pieces[step].astype(f32) + inner[step].astype(f32)).astype(bf16)
        terms.append(across(both, step))
    return terms


def piece_type(step, count):
    return f32 if in_pairs(count) and step % 2 == 0 else bf16


def whole_arrays(body, outs, args, flops=0, scratch=(), mib=24):
    moved = sum(math.prod(a.shape) * a.dtype.itemsize for a in (*args, *outs))
    return pl.pallas_call(
        body,
        out_shape=list(outs),
        in_specs=[pl.BlockSpec(memory_space=pltpu.VMEM)] * len(args),
        out_specs=[pl.BlockSpec(memory_space=pltpu.VMEM)] * len(outs),
        scratch_shapes=list(scratch),
        compiler_params=pltpu.CompilerParams(vmem_limit_bytes=mib * 2**20),
        cost_estimate=pl.CostEstimate(
            flops=max(flops, moved), bytes_accessed=moved, transcendentals=0
        ),
    )(*args)


def shape(dims, dtype):
    return jax.ShapeDtypeStruct(dims, dtype)


def tile_of(extent, limit, unit):
    fitting = [t for t in range(unit, limit + 1, unit) if extent % t == 0]
    return fitting[-1] if fitting else extent


def tiles(extent, tile):
    def each(body):
        @pl.loop(0, extent // tile)
        def _(index):
            body(pl.ds(pl.multiple_of(index * tile, tile), tile))

    return each


def affine(sums, squares, count, gain, shift):
    average = sums / count
    second = squares / count
    spread = gain * lax.rsqrt(second - average * average + epsilon)
    return (spread, shift - average * spread)


def silu(values):
    return values * jax.nn.sigmoid(values)


def early_pre_kernel(saved, weight, act, bend):
    @tiles(saved.shape[0], tile_of(saved.shape[0], 256, 16))
    def _(rows):
        pre = jnp.dot(saved[rows, :], weight[...], preferred_element_type=f32)
        sigma = jax.nn.sigmoid(pre)
        act[rows, :] = (pre * sigma).astype(bf16)
        bend[rows, :] = (sigma * (1.0 + pre * (1.0 - sigma))).astype(bf16)


def early_grads_kernel(sections, saved, leaving, arrived, act, bend, weight, grad, slope, keep, send):
    last = lax.axis_index("section") == sections - 1
    first_core = lax.rem(lax.axis_index("dev"), 2) == 0

    @tiles(saved.shape[0], tile_of(saved.shape[0], 256, 16))
    def _(rows):
        here = jnp.where(last, leaving[rows, :], arrived[rows, :])
        grad[rows, :] = here
        back = lax.dot_general(
            here, weight[...], (((1,), (1,)), ((), ())), preferred_element_type=f32
        )
        slope[rows, :] = (back * bend[rows, :].astype(f32)).astype(bf16)

    over_rows = (((0,), (0,)), ((), ()))
    one = lax.dot_general(saved[...], slope[...], over_rows, preferred_element_type=f32)
    two = lax.dot_general(grad[...], act[...], over_rows, preferred_element_type=f32)
    keep[...] = jnp.where(first_core, one, two)
    send[...] = jnp.where(first_core, two, one).astype(bf16)


def pieces_kernel(count, keep, got, own, *pieces):
    chip = lax.div(lax.axis_index("dev"), 2)
    extent = own.shape[0]

    def piece(index):
        rows = pl.ds(pl.multiple_of(index * extent, extent), extent)
        return keep[rows, :] + got[rows, :].astype(f32)

    own[...] = piece(chip)
    for step in range(1, count):
        out = pieces[step - 1]
        out[...] = piece(partner(chip, step, count)).astype(out.dtype)


def total_kernel(factor, own, *refs):
    total = own[...]
    for got in refs[:-1]:
        total = total + got[...].astype(f32)
    refs[-1][...] = (total * factor).astype(bf16)


def assemble_kernel(count, *refs):
    mine, theirs = refs[:count], refs[count : 2 * count]
    expand, reduce, held = refs[2 * count :]
    chip = lax.div(lax.axis_index("dev"), 2)
    first_core = lax.rem(lax.axis_index("dev"), 2) == 0
    extent = mine[0].shape[0]
    for step in range(count):
        index = partner(chip, step, count) if step else chip
        rows = pl.ds(pl.multiple_of(index * extent, extent), extent)
        one, two = mine[step][...].astype(f32), theirs[step][...].astype(f32)
        expand[rows, :] = jnp.where(first_core, one, two)
        held[rows, :] = jnp.where(first_core, two, one)

    @tiles(held.shape[1], tile_of(held.shape[1], 256, 128))
    def _(columns):
        reduce[columns, :] = held[:, columns].T


def late_sums_kernel(*refs):
    sums = 0.0
    squares = 0.0
    for block in refs[:-1]:
        values = block[...].astype(f32)
        sums = sums + jnp.sum(values, axis=0, keepdims=True)
        squares = squares + jnp.sum(values * values, axis=0, keepdims=True)
    refs[-1][...] = jnp.concatenate([sums, squares], axis=0)


def late_inner_kernel(count, total_rows, *refs):
    blocks = refs[:count]
    mine, got, gain, shift, weight, weight_two, inner, sums, swapped, first = refs[count:]
    spread, offset = affine(
        mine[0:1, :] + got[0:1, :], mine[1:2, :] + got[1:2, :], total_rows, gain[...], shift[...]
    )
    used, held = blocks[0].shape[0], first.shape[0] // count
    if used < held:
        first[...] = jnp.zeros_like(first)
    for index, block in enumerate(blocks):
        values = silu(block[...].astype(f32) * spread + offset).astype(bf16)
        first[index * held : index * held + used, :] = values
    hidden = weight.shape[1]
    tile = tile_of(hidden, 256, 128)
    for part, source in enumerate((weight, weight_two)):
        for start in range(0, hidden, tile):
            term = jnp.dot(first[...], source[:, start : start + tile], preferred_element_type=f32)
            here = slice(part * hidden + start, part * hidden + start + tile)
            there = slice((1 - part) * hidden + start, (1 - part) * hidden + start + tile)
            inner[:, here] = term
            both = jnp.concatenate(
                [
                    jnp.sum(term, axis=0, keepdims=True),
                    jnp.sum(term * term, axis=0, keepdims=True),
                ],
                axis=0,
            )
            sums[:, here] = both
            swapped[:, there] = both


def late_hidden_kernel(
    count, total_rows, inner, sums, got, one, two, weight, weight_two, rows, own, *refs
):
    partials, hidden = refs[:-1], refs[-1]
    extent = weight.shape[0]
    for part, gain_shift in enumerate((one, two)):
        here = slice(part * extent, (part + 1) * extent)
        spread, offset = affine(
            sums[0:1, here] + got[0:1, here],
            sums[1:2, here] + got[1:2, here],
            total_rows,
            gain_shift[0:1, :],
            gain_shift[1:2, :],
        )
        hidden[:, here] = silu(inner[:, here] * spread + offset).astype(bf16)
    used, held = rows.shape[0], inner.shape[0] // count
    tile = tile_of(weight.shape[1], 256, 128)
    for start in range(0, weight.shape[1], tile):
        columns = slice(start, start + tile)
        term = jnp.dot(hidden[:, :extent], weight[:, columns], preferred_element_type=f32)
        term = term + jnp.dot(
            hidden[:, extent:], weight_two[:, columns], preferred_element_type=f32
        )
        own[:, columns] = rows[:, columns].astype(f32) + term[:used]
        for step in range(1, count):
            out = partials[step - 1]
            out[:, columns] = term[step * held : step * held + used].astype(out.dtype)


def late_total_kernel(own, *refs):
    total = own[...]
    for got in refs[:-1]:
        total = total + got[...].astype(f32)
    refs[-1][...] = total.astype(bf16)


def shards(
    late_sent,
    entry_rows,
    gain_first,
    shift_first,
    expand_late,
    gain_inner,
    shift_inner,
    reduce_late,
    early_saved,
    upstream_grad,
    exit_grad,
    expand_early,
    reduce_early,
):
    sections, count = lax.axis_size("section"), lax.axis_size("dev") // 2
    section = lax.axis_index("section")
    steps = range(1, count)

    late_arrived = from_behind(late_sent[0], "section", 1)
    early_arrived = from_behind(upstream_grad[0], "section", -1)
    expand_two, reduce_two = swap(expand_late[0]), swap(reduce_late[0])
    one = jnp.concatenate([gain_inner, shift_inner], axis=0)
    two = swap(one)

    own_rows = jnp.where(section == 0, entry_rows, late_arrived)
    blocks = gather(own_rows)

    saved = early_saved[0]
    pixels, narrow = saved.shape
    wide = expand_early.shape[2]
    work = 2 * pixels * narrow * wide
    act, bend = whole_arrays(
        early_pre_kernel, [shape((pixels, wide), bf16)] * 2, [saved, expand_early[0]], work
    )
    grad, slope, keep, send = whole_arrays(
        functools.partial(early_grads_kernel, sections),
        [
            shape((pixels, narrow), bf16),
            shape((pixels, wide), bf16),
            shape((narrow, wide), f32),
            shape((narrow, wide), bf16),
        ],
        [saved, exit_grad, early_arrived, act, bend, reduce_early[0]],
        3 * work,
    )
    got = swap(send)
    share = narrow // count
    own_share, *shares = whole_arrays(
        functools.partial(pieces_kernel, count),
        [shape((share, wide), f32)]
        + [shape((share, wide), piece_type(step, count)) for step in steps],
        [keep, got],
    )
    terms = scatter(dict(zip(steps, shares)))

    rows, channels = own_rows.shape
    total_rows = rows * lax.axis_size("dev")
    held = -(-rows // 16) * 16
    hidden = expand_late.shape[2]
    late_work = 4 * count * held * channels * hidden
    listed = lax.optimization_barrier(tuple(blocks[step] for step in range(count)) + (own_share,))
    listed, own_share = list(listed[:-1]), listed[-1]
    (mine,) = whole_arrays(late_sums_kernel, [shape((2, channels), f32)], listed)
    others = swap(mine)
    inner, sums, swapped = whole_arrays(
        functools.partial(late_inner_kernel, count, total_rows),
        [shape((count * held, 2 * hidden), f32), shape((2, 2 * hidden), f32), shape((2, 2 * hidden), f32)],
        listed + [mine, others, gain_first, shift_first, expand_late[0], expand_two],
        late_work,
        [pltpu.VMEM((count * held, channels), bf16)],
    )
    got_sums = swap(swapped)
    own_late, *partials = whole_arrays(
        functools.partial(late_hidden_kernel, count, total_rows),
        [shape((rows, channels), f32)]
        + [shape((rows, channels), piece_type(step, count)) for step in steps],
        [inner, sums, got_sums, one, two, reduce_late[0], reduce_two, own_rows],
        late_work,
        [pltpu.VMEM((count * held, 2 * hidden), bf16)],
    )
    late_terms = scatter(dict(zip(steps, partials)))

    factor = 1.0 / math.sqrt(pixels * lax.axis_size("dev"))
    (summed,) = whole_arrays(
        functools.partial(total_kernel, factor), [shape((share, wide), bf16)], [own_share] + terms
    )
    gathered = gather(summed)
    theirs = {step: swap(gathered[step]) for step in gathered}
    input_grad = grad.astype(f32) + lax.dot_general(
        slope, expand_early[0], (((1,), (1,)), ((), ())), preferred_element_type=f32
    )
    input_grad = input_grad.astype(bf16)
    grad_expand, grad_reduce = whole_arrays(
        functools.partial(assemble_kernel, count),
        [shape((narrow, wide), f32), shape((wide, narrow), f32)],
        [gathered[step] for step in range(count)] + [theirs[step] for step in range(count)],
        scratch=[pltpu.VMEM((narrow, wide), f32)],
    )
    (late_out,) = whole_arrays(
        late_total_kernel, [shape((rows, channels), bf16)], [own_late] + late_terms
    )
    return (late_out[None], input_grad[None], grad_expand[None], grad_reduce[None])


def solution(mesh):
    in_specs = (
        P("section", "dev", None),
        P("dev", None),
        P("section", None),
        P("section", None),
        P("section", None, "dev"),
        P("section", "dev"),
        P("section", "dev"),
        P("section", "dev", None),
        P("section", "dev", None),
        P("section", "dev", None),
        P("dev", None),
        P("section", None, None),
        P("section", None, None),
    )
    out_specs = (
        P("section", "dev", None),
        P("section", "dev", None),
        P("section", None, None),
        P("section", None, None),
    )
    return jax.shard_map(shards, mesh=mesh, in_specs=in_specs, out_specs=out_specs, check_vma=False)
```

time: 183 us -> 89.9 us (0.49)
  blocking collectives: 41.6 us -> 0 us
  waiting for transfers between devices: 86.8 us -> 45.4 us
  starting transfers between devices: 7.37 us -> 26 us
  matrix products: 19.2 us -> 1.96 us
  between operations: 14.9 us -> 0.87 us
  Pallas kernels: 0 us -> 13 us
  other arithmetic: 5.38 us -> 0.12 us
  local copies, waits for them, and re-layouts: 6.93 us -> 2.23 us
    psum x1 -> x0, waiting for transfers between devices: 37.3 us -> none  [early_part(): summed_expand, summed_reduce = lax.psum((local_expand, local_reduce), 'dev')]
    ppermute x0 -> x22, waiting for transfers between devices: none -> 34.3 us  [the longest x12 34.3 us: across(): return lax.ppermute(x, 'dev', pairs)]
    all_gather x1 -> x0, waiting for transfers between devices: 26.5 us -> none  [late_part(): lax.all_gather(own_rows, 'dev', axis=0, tiled=True).astype(jnp.float32)]
    unnamed x1 -> x0, blocking collectives: 26 us -> none
    ppermute x0 -> x22, starting transfers between devices: none -> 19.2 us  [the longest x12 17.8 us: across(): return lax.ppermute(x, 'dev', pairs)]
    dot_general x7 -> x1, matrix products: 19.2 us -> 1.96 us  [shards(): lax.dot_general(slope, expand_early[0], (((1,), (1,)), ((), ())), preferr...]
    psum x1 -> x0, blocking collectives: 15.7 us -> none  [late_part(): lax.psum((jnp.sum(values, axis=0), jnp.sum(values * values, axis=0)), 'dev')]
    pallas_call x0 -> x9, Pallas kernels: none -> 13 us  [whole_arrays(): pl.pallas_call(body, out_shape=list(outs), in_specs=[pl.BlockSpec(memory_...]
  transfers between devices with their start and end apart: 5 -> 24, of which waited for: 4 -> 8; matrix products, arithmetic and copies ran while one was open for 7% -> 2% of each run, Pallas kernels for 0% -> 12%
where the time goes in v2:
time: 89.9 us; the launch traced here: 89.6 us
  waiting for transfers between devices  45.4 us (51%)
  starting transfers between devices  26 us (29%)
  Pallas kernels  13 us (14%)
  local copies, waits for them, and re-layouts  2.23 us (2%)
  matrix products  1.96 us (2%)
    ppermute x12, waiting for transfers between devices, across(): return lax.ppermute(x, 'dev', pairs)  34.3 us
    ppermute x12, starting transfers between devices, across(): return lax.ppermute(x, 'dev', pairs)  17.8 us
    pallas_call x9, Pallas kernels, whole_arrays(): pl.pallas_call(body, out_shape=list(outs), in_specs=[pl.BlockSpec(memory_...  13 us
    ppermute x2, waiting for transfers between devices, from_behind(): return lax.ppermute(x, axis, pairs)  11.1 us
    ppermute x2, starting transfers between devices, from_behind(): return lax.ppermute(x, axis, pairs)  6.8 us
    unnamed x24, local copies, waits for them, and re-layouts  2.23 us
    dot_general x1, matrix products, shards(): lax.dot_general(slope, expand_early[0], (((1,), (1,)), ((), ())), preferr...  1.96 us
  transfers between devices with their start and end apart: 24, of which 8 were waited for; matrix products, arithmetic and copies ran while one was open for 2% of the time, Pallas kernels for 12%

profile of v2, /device:TPU:0, one launch (start us, length us, event | category | flops | bytes accessed | tf_op | source)
XLA Modules:
  0.0 89.6 jit_solution(7580276096040664430)
XLA Ops:
  0.6 1.3 %collective-permute-start.4 = (bf16[1568,256]{1,0:T(8,128)(2,1)}, bf16[1568,256]{1,0:T(8,128)(2,1)S(1)}, u32[]{:S(2)}, u32[]{:S(2)}) collective-permute-start(bf16[1568,256]{1,0:T(8,128)(2,1)} %bitcast.28), channel_id=1, source_target_pairs={{8,0},{16,8},{24,16},{9,1},{17,9},{25,17},{10,2},{18,10},{26,18},{... | collective-permute-start | bytes 2408456 | tf_op jit(solution)/shard_map/ppermute | solution.py:19
  1.9 5.5 %collective-permute-start = (bf16[98,1024]{1,0:T(8,128)(2,1)}, bf16[98,1024]{1,0:T(8,128)(2,1)S(1)}, u32[]{:S(2)}, u32[]{:S(2)}) collective-permute-start(bf16[98,1024]{1,0:T(8,128)(2,1)} %bitcast.29), channel_id=1, source_target_pairs={{0,8},{8,16},{16,24},{1,9},{9,17},{17,25},{2,10},{10,18},{18,26},{... | collective-permute-start | bytes 602120 | tf_op jit(solution)/shard_map/ppermute | solution.py:19
  7.5 0.1 collective-permute-start.7
  7.5 0.5 collective-permute-start.10
  8.0 1.1 %copy-done.1 = bf16[1,1568,256]{2,1,0:T(8,128)(2,1)S(1)} copy-done((bf16[1,1568,256]{2,1,0:T(8,128)(2,1)S(1)}, bf16[1,1568,256]{2,1,0:T(8,128)(2,1)}, u32[]{:S(2)}) %copy-start.1) | copy-done | bytes 802840
  9.2 1.0 %copy-done.5 = bf16[1,256,1024]{2,1,0:T(8,128)(2,1)S(1)} copy-done((bf16[1,256,1024]{2,1,0:T(8,128)(2,1)S(1)}, bf16[1,256,1024]{2,1,0:T(8,128)(2,1)}, u32[]{:S(2)}) %copy-start.5) | copy-done | bytes 524312
  10.2 3.1 %shard_map.156 = (bf16[1568,1024]{1,0:T(8,128)(2,1)S(1)}, bf16[1568,1024]{1,0:T(8,128)(2,1)S(1)}) custom-call(bf16[1568,256]{1,0:T(8,128)(2,1)S(1)} %bitcast.19, bf16[256,1024]{1,0:T(8,128)(2,1)S(1)} %bitcast.24), custom_call_target="tpu_custom_call" | custom-call | flops 822083584 | bytes 7749632 | tf_op jit(solution)/shard_map/pallas_call | solution.py:82
  13.4 11.1 %collective-permute-done.4.arrived = bf16[1568,256]{1,0:T(8,128)(2,1)S(1)} collective-permute-done((bf16[1568,256]{1,0:T(8,128)(2,1)}, bf16[1568,256]{1,0:T(8,128)(2,1)S(1)}, u32[]{:S(2)}, u32[]{:S(2)}) %collective-permute-start.4) | collective-permute-done | bytes 802848 | tf_op jit(solution)/shard_map/ppermute | solution.py:19
  24.5 0.0 copy-start.11
  24.5 0.0 copy-start.4
  24.5 0.0 copy-start.7
  24.5 0.0 copy-start.8
  24.5 4.4 %shard_map.157 = (bf16[1568,256]{1,0:T(8,128)(2,1)S(1)}, bf16[1568,1024]{1,0:T(8,128)(2,1)S(1)}, f32[256,1024]{1,0:T(8,128)S(1)}, bf16[256,1024]{1,0:T(8,128)(2,1)S(1)}) custom-call(bf16[1568,256]{1,0:T(8,128)(2,1)S(1)} %bitcast.20, bf16[1568,256]{1,0:T(8,128)(2,1)S(1)} %copy-done.2, bf16[1568,256]{1,0:T(8,128)(2,1)S(1)} %collective-permute-done.4.arrived, ...), custom_call_target="tpu_custom_call" | custom-call | flops 2466250752 | bytes 14942208 | tf_op jit(solution)/shard_map/pallas_call | solution.py:82
  29.0 0.1 collective-permute-start.5
  29.0 0.0 collective-permute-done
  29.1 3.2 %collective-permute-start.2 = (bf16[98,1024]{1,0:T(8,128)(2,1)S(1)}, bf16[98,1024]{1,0:T(8,128)(2,1)S(1)}, u32[]{:S(2)}, u32[]{:S(2)}) collective-permute-start(bf16[98,1024]{1,0:T(8,128)(2,1)S(1)} %broadcast_select_fusion.refs_0_.rows), channel_id=1, source_target_pairs={{0,4},{1,5},{2,6},{3,7},{4,0},{5,1},{6,2},{7,3},{8,12},{9,13},{10,... | collective-permute-start | bytes 602120 | tf_op jit(solution)/shard_map/ppermute | solution.py:38
  32.3 1.6 %collective-permute-start.1 = (bf16[98,1024]{1,0:T(8,128)(2,1)S(1)}, bf16[98,1024]{1,0:T(8,128)(2,1)S(1)}, u32[]{:S(2)}, u32[]{:S(2)}) collective-permute-start(bf16[98,1024]{1,0:T(8,128)(2,1)S(1)} %broadcast_select_fusion.refs_0_.rows), channel_id=1, source_target_pairs={{0,2},{1,3},{2,0},{3,1},{4,6},{5,7},{6,4},{7,5},{8,10},{9,11},{10,... | collective-permute-start | bytes 602120 | tf_op jit(solution)/shard_map/ppermute | solution.py:38
  33.9 9.0 %collective-permute-done.2.refs_2_ = bf16[98,1024]{1,0:T(8,128)(2,1)S(1)} collective-permute-done((bf16[98,1024]{1,0:T(8,128)(2,1)S(1)}, bf16[98,1024]{1,0:T(8,128)(2,1)S(1)}, u32[]{:S(2)}, u32[]{:S(2)}) %collective-permute-start.2) | collective-permute-done | bytes 200736 | tf_op jit(solution)/shard_map/ppermute | solution.py:38
  42.8 0.6 collective-permute-start.3
  43.5 0.0 collective-permute-done.5.got
  43.5 0.1 shard_map.158
  43.6 1.5 %collective-permute-start.15 = (bf16[64,1024]{1,0:T(8,128)(2,1)S(1)}, bf16[64,1024]{1,0:T(8,128)(2,1)S(1)}, u32[]{:S(2)}, u32[]{:S(2)}) collective-permute-start(bf16[64,1024]{1,0:T(8,128)(2,1)S(1)} %get-tuple-element.49), channel_id=1, source_target_pairs={{0,2},{1,3},{2,0},{3,1},{4,6},{5,7},{6,4},{7,5},{8,10},{9,11},{10,... | collective-permute-start | bytes 393224 | tf_op jit(solution)/shard_map/ppermute | solution.py:38
  45.0 0.0 collective-permute-done.1.refs_1_
  45.0 5.9 %collective-permute-done.3.refs_3_ = bf16[98,1024]{1,0:T(8,128)(2,1)S(1)} collective-permute-done((bf16[98,1024]{1,0:T(8,128)(2,1)S(1)}, bf16[98,1024]{1,0:T(8,128)(2,1)S(1)}, u32[]{:S(2)}, u32[]{:S(2)}) %collective-permute-start.3) | collective-permute-done | bytes 200736 | tf_op jit(solution)/shard_map/ppermute | solution.py:38
  51.0 0.2 shard_map.159.refs_4_
  51.2 0.1 collective-permute-start.6
  51.3 0.5 collective-permute-start.9
  51.9 0.0 collective-permute-done.7.refs_9_
  51.9 0.6 collective-permute-start.14
  52.5 0.0 collective-permute-done.6.refs_5_
  52.5 1.2 %shard_map.160 = (f32[448,1024]{1,0:T(8,128)S(1)}, f32[2,1024]{1,0:T(2,128)S(1)}, f32[2,1024]{1,0:T(2,128)S(1)}) custom-call(bf16[98,1024]{1,0:T(8,128)(2,1)S(1)} %broadcast_select_fusion.refs_0_.rows, bf16[98,1024]{1,0:T(8,128)(2,1)S(1)} %collective-permute-done.1.refs_1_, bf16[98,1024]{1,0:T(8,128)(2,1)S(1)} %collective-permute-done.2.refs_2_, ...), custom_call_target="tpu_custom_call" | custom-call | flops 939524096 | bytes 4775936 | tf_op jit(solution)/shard_map/pallas_call | solution.py:82
  53.7 0.0 copy-start.6
  53.7 0.1 collective-permute-start.8
  53.9 0.0 collective-permute-done.15
  53.9 3.4 %collective-permute-start.16 = (bf16[64,1024]{1,0:T(8,128)(2,1)S(1)}, bf16[64,1024]{1,0:T(8,128)(2,1)S(1)}, u32[]{:S(2)}, u32[]{:S(2)}) collective-permute-start(bf16[64,1024]{1,0:T(8,128)(2,1)S(1)} %add_convert_fusion.2), channel_id=1, source_target_pairs={{0,4},{1,5},{2,6},{3,7},{4,0},{5,1},{6,2},{7,3},{8,12},{9,13},{10,... | collective-permute-start | bytes 393224 | tf_op jit(solution)/shard_map/ppermute | solution.py:38
  57.3 0.0 collective-permute-done.9.two
  57.3 0.0 collective-permute-done.10.weight_two
  57.3 0.0 collective-permute-done.8.got
  57.3 1.1 %shard_map.161 = (f32[98,1024]{1,0:T(8,128)S(1)}, bf16[98,1024]{1,0:T(8,128)(2,1)S(1)}, f32[98,1024]{1,0:T(8,128)S(1)}, bf16[98,1024]{1,0:T(8,128)(2,1)S(1)}) custom-call(f32[448,1024]{1,0:T(8,128)S(1)} %get-tuple-element.37.inner, f32[2,1024]{1,0:T(2,128)S(1)} %get-tuple-element.38.sums, f32[2,1024]{1,0:T(2,128)S(1)} %collective-permute-done.8.got, ...), custom_call_target="tpu_custom_call" | custom-call | flops 939524096 | bytes 5361664 | tf_op jit(solution)/shard_map/pallas_call | solution.py:82
  58.4 0.8 collective-permute-start.12
  59.2 0.0 collective-permute-done.14.refs_0_
  59.2 5.1 %collective-permute-done.16.refs_1_ = bf16[64,1024]{1,0:T(8,128)(2,1)S(1)} collective-permute-done((bf16[64,1024]{1,0:T(8,128)(2,1)S(1)}, bf16[64,1024]{1,0:T(8,128)(2,1)S(1)}, u32[]{:S(2)}, u32[]{:S(2)}) %collective-permute-start.16) | collective-permute-done | bytes 131104 | tf_op jit(solution)/shard_map/ppermute | solution.py:38
  64.3 0.1 shard_map.163.refs_0_
  64.4 0.3 collective-permute-start.18
  64.7 2.9 %collective-permute-start.11 = (bf16[98,1024]{1,0:T(8,128)(2,1)S(1)}, bf16[98,1024]{1,0:T(8,128)(2,1)S(1)}, u32[]{:S(2)}, u32[]{:S(2)}) collective-permute-start(bf16[98,1024]{1,0:T(8,128)(2,1)S(1)} %get-tuple-element.41), channel_id=1, source_target_pairs={{0,2},{1,3},{2,0},{3,1},{4,6},{5,7},{6,4},{7,5},{8,10},{9,11},{10,... | collective-permute-start | bytes 602120 | tf_op jit(solution)/shard_map/ppermute | solution.py:38
  67.7 0.0 collective-permute-start.17
  67.7 5.4 %collective-permute-done.18.refs_2_ = bf16[64,1024]{1,0:T(8,128)(2,1)S(1)} collective-permute-done((bf16[64,1024]{1,0:T(8,128)(2,1)S(1)}, bf16[64,1024]{1,0:T(8,128)(2,1)S(1)}, u32[]{:S(2)}, u32[]{:S(2)}) %collective-permute-start.18) | collective-permute-done | bytes 131104 | tf_op jit(solution)/shard_map/ppermute | solution.py:38
  73.0 0.0 collective-permute-start.19
  73.1 0.0 collective-permute-done.12
  73.1 0.1 add_convert_fusion.1
  73.1 2.8 %collective-permute-start.13 = (bf16[98,1024]{1,0:T(8,128)(2,1)S(1)}, bf16[98,1024]{1,0:T(8,128)(2,1)S(1)}, u32[]{:S(2)}, u32[]{:S(2)}) collective-permute-start(bf16[98,1024]{1,0:T(8,128)(2,1)S(1)} %add_convert_fusion.1), channel_id=1, source_target_pairs={{0,4},{1,5},{2,6},{3,7},{4,0},{5,1},{6,2},{7,3},{8,12},{9,13},{10,... | collective-permute-start | bytes 602120 | tf_op jit(solution)/shard_map/ppermute | solution.py:38
  75.9 0.0 collective-permute-start.20
  75.9 0.5 collective-permute-done.11.refs_0_
  76.5 0.0 collective-permute-start.22
  76.5 6.5 %collective-permute-done.17.refs_1_ = bf16[64,1024]{1,0:T(8,128)(2,1)S(1)} collective-permute-done((bf16[64,1024]{1,0:T(8,128)(2,1)S(1)}, bf16[64,1024]{1,0:T(8,128)(2,1)S(1)}, u32[]{:S(2)}, u32[]{:S(2)}) %collective-permute-start.17) | collective-permute-done | bytes 131104 | tf_op jit(solution)/shard_map/ppermute | solution.py:38
  83.0 0.0 collective-permute-start.21
  83.0 1.8 %collective-permute-done.19.refs_3_ = bf16[64,1024]{1,0:T(8,128)(2,1)S(1)} collective-permute-done((bf16[64,1024]{1,0:T(8,128)(2,1)S(1)}, bf16[64,1024]{1,0:T(8,128)(2,1)S(1)}, u32[]{:S(2)}, u32[]{:S(2)}) %collective-permute-start.19) | collective-permute-done | bytes 131104 | tf_op jit(solution)/shard_map/ppermute | solution.py:38
  84.8 0.0 collective-permute-start.23
  84.9 2.0 %fusion = bf16[1,1568,256]{2,1,0:T(8,128)(2,1)} fusion(bf16[1568,256]{1,0:T(8,128)(2,1)S(1)} %get-tuple-element.44, bf16[1568,1024]{1,0:T(8,128)(2,1)S(1)} %get-tuple-element.45, bf16[1,256,1024]{2,1,0:T(8,128)(2,1)S(1)} %copy-done.6), kind=kOutput, calls=%fused_computation.1 | convolution fusion | flops 823287808 | bytes 5341184 | tf_op jit(solution)/shard_map/dot_general | solution.py:358
  86.8 0.7 shard_map.162
  87.6 0.0 collective-permute-done.20.refs_4_
  87.6 0.0 collective-permute-done.22.refs_6_
  87.6 0.0 collective-permute-done.23.refs_7_
  87.6 2.0 %shard_map.164 = (f32[256,1024]{1,0:T(8,128)}, f32[1024,256]{1,0:T(8,128)}) custom-call(bf16[64,1024]{1,0:T(8,128)(2,1)S(1)} %shard_map.163.refs_0_, bf16[64,1024]{1,0:T(8,128)(2,1)S(1)} %collective-permute-done.17.refs_1_, bf16[64,1024]{1,0:T(8,128)(2,1)S(1)} %collective-permute-done.18.refs_2_, bf16[64,1024]{1,0:T(8,128)(2,1)S(1)} %collective-permute-done.19.refs_3_, ...), custom_call_target="tpu_custom_call" | custom-call | flops 3145728 | bytes 3145728 | tf_op jit(solution)/shard_map/pallas_call | solution.py:82
  (22 shorter events, 0.1 us)
Async XLA Ops:
  0.6 23.8 %collective-permute-start.4 = (bf16[1568,256]{1,0:T(8,128)(2,1)}, bf16[1568,256]{1,0:T(8,128)(2,1)S(1)}, u32[]{:S(2)}, u32[]{:S(2)}) collective-permute-start(bf16[1568,256]{1,0:T(8,128)(2,1)} %bitcast.28), channel_id=1, source_target_pairs={{8,0},{16,8},{24,16},{9,1},{17,9},{25,17},{10,2},{18,10},{26,18},{... | collective-permute-start | bytes 2408456 | tf_op jit(solution)/shard_map/ppermute | solution.py:19
  1.9 27.1 %collective-permute-start = (bf16[98,1024]{1,0:T(8,128)(2,1)}, bf16[98,1024]{1,0:T(8,128)(2,1)S(1)}, u32[]{:S(2)}, u32[]{:S(2)}) collective-permute-start(bf16[98,1024]{1,0:T(8,128)(2,1)} %bitcast.29), channel_id=1, source_target_pairs={{0,8},{8,16},{16,24},{1,9},{9,17},{17,25},{2,10},{10,18},{18,26},{... | collective-permute-start | bytes 602120 | tf_op jit(solution)/shard_map/ppermute | solution.py:19
  7.5 44.4 %collective-permute-start.7 = (bf16[1024,512]{1,0:T(8,128)(2,1)}, bf16[1024,512]{1,0:T(8,128)(2,1)S(1)}, u32[]{:S(2)}, u32[]{:S(2)}) collective-permute-start(bf16[1024,512]{1,0:T(8,128)(2,1)} %bitcast.22), channel_id=1, source_target_pairs={{0,1},{1,0},{2,3},{3,2},{4,5},{5,4},{6,7},{7,6},{8,9},{9,8},{10,11... | collective-permute-start | bytes 3145736 | tf_op jit(solution)/shard_map/ppermute | solution.py:23
  7.5 49.7 %collective-permute-start.10 = (bf16[512,1024]{1,0:T(8,128)(2,1)}, bf16[512,1024]{1,0:T(8,128)(2,1)S(1)}, u32[]{:S(2)}, u32[]{:S(2)}) collective-permute-start(bf16[512,1024]{1,0:T(8,128)(2,1)} %bitcast.17), channel_id=1, source_target_pairs={{0,1},{1,0},{2,3},{3,2},{4,5},{5,4},{6,7},{7,6},{8,9},{9,8},{10,11... | collective-permute-start | bytes 3145736 | tf_op jit(solution)/shard_map/ppermute | solution.py:23
  8.0 1.1 %copy-start.1 = (bf16[1,1568,256]{2,1,0:T(8,128)(2,1)S(1)}, bf16[1,1568,256]{2,1,0:T(8,128)(2,1)}, u32[]{:S(2)}) copy-start(bf16[1,1568,256]{2,1,0:T(8,128)(2,1)} %param.21) | copy-start | bytes 2408452
  9.2 1.0 %copy-start.5 = (bf16[1,256,1024]{2,1,0:T(8,128)(2,1)S(1)}, bf16[1,256,1024]{2,1,0:T(8,128)(2,1)}, u32[]{:S(2)}) copy-start(bf16[1,256,1024]{2,1,0:T(8,128)(2,1)} %param.24) | copy-start | bytes 1572868
  10.2 14.2 %copy-start.2 = (bf16[1568,256]{1,0:T(8,128)(2,1)S(1)}, bf16[1568,256]{1,0:T(8,128)(2,1)}, u32[]{:S(2)}) copy-start(bf16[1568,256]{1,0:T(8,128)(2,1)} %leaving.1) | copy-start | bytes 2408452
  10.2 14.2 %copy-start.3 = (bf16[1,1024,256]{2,1,0:T(8,128)(2,1)S(1)}, bf16[1,1024,256]{2,1,0:T(8,128)(2,1)}, u32[]{:S(2)}) copy-start(bf16[1,1024,256]{2,1,0:T(8,128)(2,1)} %param.25) | copy-start | bytes 1572868
  24.5 4.6 %copy-start.9 = (bf16[98,1024]{1,0:T(8,128)(2,1)S(1)}, bf16[98,1024]{1,0:T(8,128)(2,1)}, u32[]{:S(2)}) copy-start(bf16[98,1024]{1,0:T(8,128)(2,1)} %param.14) | copy-start | bytes 602116
  24.5 26.8 %copy-start.10 = (f32[1,512]{1,0:T(1,128)S(1)}, f32[1,512]{1,0:T(1,128)}, u32[]{:S(2)}) copy-start(f32[1,512]{1,0:T(1,128)} %param.19) | copy-start | bytes 6148
  24.5 26.8 %copy-start.11 = (f32[1,512]{1,0:T(1,128)S(1)}, f32[1,512]{1,0:T(1,128)}, u32[]{:S(2)}) copy-start(f32[1,512]{1,0:T(1,128)} %param.18) | copy-start | bytes 6148
  24.5 28.0 %copy-start.4 = (bf16[1,1024,512]{2,1,0:T(8,128)(2,1)S(1)}, bf16[1,1024,512]{2,1,0:T(8,128)(2,1)}, u32[]{:S(2)}) copy-start(bf16[1,1024,512]{2,1,0:T(8,128)(2,1)} %param.17) | copy-start | bytes 3145732
  24.5 28.0 %copy-start.7 = (f32[1,1024]{1,0:T(1,128)S(1)}, f32[1,1024]{1,0:T(1,128)}, u32[]{:S(2)}) copy-start(f32[1,1024]{1,0:T(1,128)} %refs_6_.1) | copy-start | bytes 12292
  24.5 28.0 %copy-start.8 = (f32[1,1024]{1,0:T(1,128)S(1)}, f32[1,1024]{1,0:T(1,128)}, u32[]{:S(2)}) copy-start(f32[1,1024]{1,0:T(1,128)} %refs_7_.1) | copy-start | bytes 12292
  29.0 14.5 %collective-permute-start.5 = (bf16[256,1024]{1,0:T(8,128)(2,1)S(1)}, bf16[256,1024]{1,0:T(8,128)(2,1)S(1)}, u32[]{:S(2)}, u32[]{:S(2)}) collective-permute-start(bf16[256,1024]{1,0:T(8,128)(2,1)S(1)} %get-tuple-element.31), channel_id=1, source_target_pairs={{0,1},{1,0},{2,3},{3,2},{4,5},{5,4},{6,7},{7,6},{8,9},{9,8},{10,11... | collective-permute-start | bytes 1572872 | tf_op jit(solution)/shard_map/ppermute | solution.py:23
  29.1 13.8 %collective-permute-start.2 = (bf16[98,1024]{1,0:T(8,128)(2,1)S(1)}, bf16[98,1024]{1,0:T(8,128)(2,1)S(1)}, u32[]{:S(2)}, u32[]{:S(2)}) collective-permute-start(bf16[98,1024]{1,0:T(8,128)(2,1)S(1)} %broadcast_select_fusion.refs_0_.rows), channel_id=1, source_target_pairs={{0,4},{1,5},{2,6},{3,7},{4,0},{5,1},{6,2},{7,3},{8,12},{9,13},{10,... | collective-permute-start | bytes 602120 | tf_op jit(solution)/shard_map/ppermute | solution.py:38
  32.3 12.7 %collective-permute-start.1 = (bf16[98,1024]{1,0:T(8,128)(2,1)S(1)}, bf16[98,1024]{1,0:T(8,128)(2,1)S(1)}, u32[]{:S(2)}, u32[]{:S(2)}) collective-permute-start(bf16[98,1024]{1,0:T(8,128)(2,1)S(1)} %broadcast_select_fusion.refs_0_.rows), channel_id=1, source_target_pairs={{0,2},{1,3},{2,0},{3,1},{4,6},{5,7},{6,4},{7,5},{8,10},{9,11},{10,... | collective-permute-start | bytes 602120 | tf_op jit(solution)/shard_map/ppermute | solution.py:38
  42.8 8.1 %collective-permute-start.3 = (bf16[98,1024]{1,0:T(8,128)(2,1)S(1)}, bf16[98,1024]{1,0:T(8,128)(2,1)S(1)}, u32[]{:S(2)}, u32[]{:S(2)}) collective-permute-start(bf16[98,1024]{1,0:T(8,128)(2,1)S(1)} %collective-permute-done.2.refs_2_), channel_id=1, source_target_pairs={{0,2},{1,3},{2,0},{3,1},{4,6},{5,7},{6,4},{7,5},{8,10},{9,11},{10,... | collective-permute-start | bytes 602120 | tf_op jit(solution)/shard_map/ppermute | solution.py:38
  43.5 13.8 %copy-start = (bf16[1,512,1024]{2,1,0:T(8,128)(2,1)S(1)}, bf16[1,512,1024]{2,1,0:T(8,128)(2,1)}, u32[]{:S(2)}) copy-start(bf16[1,512,1024]{2,1,0:T(8,128)(2,1)} %param.20) | copy-start | bytes 3145732
  43.6 10.3 %collective-permute-start.15 = (bf16[64,1024]{1,0:T(8,128)(2,1)S(1)}, bf16[64,1024]{1,0:T(8,128)(2,1)S(1)}, u32[]{:S(2)}, u32[]{:S(2)}) collective-permute-start(bf16[64,1024]{1,0:T(8,128)(2,1)S(1)} %get-tuple-element.49), channel_id=1, source_target_pairs={{0,2},{1,3},{2,0},{3,1},{4,6},{5,7},{6,4},{7,5},{8,10},{9,11},{10,... | collective-permute-start | bytes 393224 | tf_op jit(solution)/shard_map/ppermute | solution.py:38
  51.2 1.3 %collective-permute-start.6 = (f32[2,1024]{1,0:T(2,128)S(1)}, f32[2,1024]{1,0:T(2,128)S(1)}, u32[]{:S(2)}, u32[]{:S(2)}) collective-permute-start(f32[2,1024]{1,0:T(2,128)S(1)} %shard_map.159.refs_4_), channel_id=1, source_target_pairs={{0,1},{1,0},{2,3},{3,2},{4,5},{5,4},{6,7},{7,6},{8,9},{9,8},{10,11... | collective-permute-start | bytes 24584 | tf_op jit(solution)/shard_map/ppermute | solution.py:23
  51.3 5.9 %collective-permute-start.9 = (f32[2,512]{1,0:T(2,128)S(1)}, f32[2,512]{1,0:T(2,128)S(1)}, u32[]{:S(2)}, u32[]{:S(2)}) collective-permute-start(f32[2,512]{1,0:T(2,128)S(1)} %pad_maximum_fusion.one), channel_id=1, source_target_pairs={{0,1},{1,0},{2,3},{3,2},{4,5},{5,4},{6,7},{7,6},{8,9},{9,8},{10,11... | collective-permute-start | bytes 12296 | tf_op jit(solution)/shard_map/ppermute | solution.py:23
  51.9 7.3 %collective-permute-start.14 = (bf16[64,1024]{1,0:T(8,128)(2,1)S(1)}, bf16[64,1024]{1,0:T(8,128)(2,1)S(1)}, u32[]{:S(2)}, u32[]{:S(2)}) collective-permute-start(bf16[64,1024]{1,0:T(8,128)(2,1)S(1)} %get-tuple-element.47), channel_id=1, source_target_pairs={{0,2},{1,3},{2,0},{3,1},{4,6},{5,7},{6,4},{7,5},{8,10},{9,11},{10,... | collective-permute-start | bytes 393224 | tf_op jit(solution)/shard_map/ppermute | solution.py:38
  53.7 31.2 %copy-start.6 = (bf16[1,256,1024]{2,1,0:T(8,128)(2,1)S(1)}, bf16[1,256,1024]{2,1,0:T(8,128)(2,1)}, u32[]{:S(2)}) copy-start(bf16[1,256,1024]{2,1,0:T(8,128)(2,1)} %param.24) | copy-start | bytes 1572868
  53.7 3.6 %collective-permute-start.8 = (f32[2,1024]{1,0:T(2,128)S(1)}, f32[2,1024]{1,0:T(2,128)S(1)}, u32[]{:S(2)}, u32[]{:S(2)}) collective-permute-start(f32[2,1024]{1,0:T(2,128)S(1)} %get-tuple-element.39), channel_id=1, source_target_pairs={{0,1},{1,0},{2,3},{3,2},{4,5},{5,4},{6,7},{7,6},{8,9},{9,8},{10,11... | collective-permute-start | bytes 24584 | tf_op jit(solution)/shard_map/ppermute | solution.py:23
  53.9 10.4 %collective-permute-start.16 = (bf16[64,1024]{1,0:T(8,128)(2,1)S(1)}, bf16[64,1024]{1,0:T(8,128)(2,1)S(1)}, u32[]{:S(2)}, u32[]{:S(2)}) collective-permute-start(bf16[64,1024]{1,0:T(8,128)(2,1)S(1)} %add_convert_fusion.2), channel_id=1, source_target_pairs={{0,4},{1,5},{2,6},{3,7},{4,0},{5,1},{6,2},{7,3},{8,12},{9,13},{10,... | collective-permute-start | bytes 393224 | tf_op jit(solution)/shard_map/ppermute | solution.py:38
  58.4 14.6 %collective-permute-start.12 = (bf16[98,1024]{1,0:T(8,128)(2,1)S(1)}, bf16[98,1024]{1,0:T(8,128)(2,1)S(1)}, u32[]{:S(2)}, u32[]{:S(2)}) collective-permute-start(bf16[98,1024]{1,0:T(8,128)(2,1)S(1)} %get-tuple-element.43), channel_id=1, source_target_pairs={{0,2},{1,3},{2,0},{3,1},{4,6},{5,7},{6,4},{7,5},{8,10},{9,11},{10,... | collective-permute-start | bytes 602120 | tf_op jit(solution)/shard_map/ppermute | solution.py:38
  64.4 8.7 %collective-permute-start.18 = (bf16[64,1024]{1,0:T(8,128)(2,1)S(1)}, bf16[64,1024]{1,0:T(8,128)(2,1)S(1)}, u32[]{:S(2)}, u32[]{:S(2)}) collective-permute-start(bf16[64,1024]{1,0:T(8,128)(2,1)S(1)} %shard_map.163.refs_0_), channel_id=1, source_target_pairs={{0,4},{1,5},{2,6},{3,7},{4,0},{5,1},{6,2},{7,3},{8,12},{9,13},{10,... | collective-permute-start | bytes 393224 | tf_op jit(solution)/shard_map/ppermute | solution.py:38
  64.7 11.8 %collective-permute-start.11 = (bf16[98,1024]{1,0:T(8,128)(2,1)S(1)}, bf16[98,1024]{1,0:T(8,128)(2,1)S(1)}, u32[]{:S(2)}, u32[]{:S(2)}) collective-permute-start(bf16[98,1024]{1,0:T(8,128)(2,1)S(1)} %get-tuple-element.41), channel_id=1, source_target_pairs={{0,2},{1,3},{2,0},{3,1},{4,6},{5,7},{6,4},{7,5},{8,10},{9,11},{10,... | collective-permute-start | bytes 602120 | tf_op jit(solution)/shard_map/ppermute | solution.py:38
  67.7 15.4 %collective-permute-start.17 = (bf16[64,1024]{1,0:T(8,128)(2,1)S(1)}, bf16[64,1024]{1,0:T(8,128)(2,1)S(1)}, u32[]{:S(2)}, u32[]{:S(2)}) collective-permute-start(bf16[64,1024]{1,0:T(8,128)(2,1)S(1)} %shard_map.163.refs_0_), channel_id=1, source_target_pairs={{0,2},{1,3},{2,0},{3,1},{4,6},{5,7},{6,4},{7,5},{8,10},{9,11},{10,... | collective-permute-start | bytes 393224 | tf_op jit(solution)/shard_map/ppermute | solution.py:38
  73.0 11.8 %collective-permute-start.19 = (bf16[64,1024]{1,0:T(8,128)(2,1)S(1)}, bf16[64,1024]{1,0:T(8,128)(2,1)S(1)}, u32[]{:S(2)}, u32[]{:S(2)}) collective-permute-start(bf16[64,1024]{1,0:T(8,128)(2,1)S(1)} %collective-permute-done.18.refs_2_), channel_id=1, source_target_pairs={{0,2},{1,3},{2,0},{3,1},{4,6},{5,7},{6,4},{7,5},{8,10},{9,11},{10,... | collective-permute-start | bytes 393224 | tf_op jit(solution)/shard_map/ppermute | solution.py:38
  73.1 13.7 %collective-permute-start.13 = (bf16[98,1024]{1,0:T(8,128)(2,1)S(1)}, bf16[98,1024]{1,0:T(8,128)(2,1)S(1)}, u32[]{:S(2)}, u32[]{:S(2)}) collective-permute-start(bf16[98,1024]{1,0:T(8,128)(2,1)S(1)} %add_convert_fusion.1), channel_id=1, source_target_pairs={{0,4},{1,5},{2,6},{3,7},{4,0},{5,1},{6,2},{7,3},{8,12},{9,13},{10,... | collective-permute-start | bytes 602120 | tf_op jit(solution)/shard_map/ppermute | solution.py:38
  75.9 11.6 %collective-permute-start.20 = (bf16[64,1024]{1,0:T(8,128)(2,1)S(1)}, bf16[64,1024]{1,0:T(8,128)(2,1)S(1)}, u32[]{:S(2)}, u32[]{:S(2)}) collective-permute-start(bf16[64,1024]{1,0:T(8,128)(2,1)S(1)} %shard_map.163.refs_0_), channel_id=1, source_target_pairs={{0,1},{1,0},{2,3},{3,2},{4,5},{5,4},{6,7},{7,6},{8,9},{9,8},{10,11... | collective-permute-start | bytes 393224 | tf_op jit(solution)/shard_map/ppermute | solution.py:23
  76.5 11.1 %collective-permute-start.22 = (bf16[64,1024]{1,0:T(8,128)(2,1)S(1)}, bf16[64,1024]{1,0:T(8,128)(2,1)S(1)}, u32[]{:S(2)}, u32[]{:S(2)}) collective-permute-start(bf16[64,1024]{1,0:T(8,128)(2,1)S(1)} %collective-permute-done.18.refs_2_), channel_id=1, source_target_pairs={{0,1},{1,0},{2,3},{3,2},{4,5},{5,4},{6,7},{7,6},{8,9},{9,8},{10,11... | collective-permute-start | bytes 393224 | tf_op jit(solution)/shard_map/ppermute | solution.py:23
  83.0 4.6 %collective-permute-start.21 = (bf16[64,1024]{1,0:T(8,128)(2,1)S(1)}, bf16[64,1024]{1,0:T(8,128)(2,1)S(1)}, u32[]{:S(2)}, u32[]{:S(2)}) collective-permute-start(bf16[64,1024]{1,0:T(8,128)(2,1)S(1)} %collective-permute-done.17.refs_1_), channel_id=1, source_target_pairs={{0,1},{1,0},{2,3},{3,2},{4,5},{5,4},{6,7},{7,6},{8,9},{9,8},{10,11... | collective-permute-start | bytes 393224 | tf_op jit(solution)/shard_map/ppermute | solution.py:23
  84.8 2.7 %collective-permute-start.23 = (bf16[64,1024]{1,0:T(8,128)(2,1)S(1)}, bf16[64,1024]{1,0:T(8,128)(2,1)S(1)}, u32[]{:S(2)}, u32[]{:S(2)}) collective-permute-start(bf16[64,1024]{1,0:T(8,128)(2,1)S(1)} %collective-permute-done.19.refs_3_), channel_id=1, source_target_pairs={{0,1},{1,0},{2,3},{3,2},{4,5},{5,4},{6,7},{7,6},{8,9},{9,8},{10,11... | collective-permute-start | bytes 393224 | tf_op jit(solution)/shard_map/ppermute | solution.py:23

commit v3 on v2

--- a/solution.py
+++ b/solution.py
@@ -121,22 +121,42 @@
     return values * jax.nn.sigmoid(values)
 
 
-def early_pre_kernel(saved, weight, act, bend):
-    @tiles(saved.shape[0], tile_of(saved.shape[0], 256, 16))
-    def _(rows):
-        pre = jnp.dot(saved[rows, :], weight[...], preferred_element_type=f32)
-        sigma = jax.nn.sigmoid(pre)
-        act[rows, :] = (pre * sigma).astype(bf16)
-        bend[rows, :] = (sigma * (1.0 + pre * (1.0 - sigma))).astype(bf16)
-
-
-def early_grads_kernel(sections, saved, leaving, arrived, act, bend, weight, grad, slope, keep, send):
+def cut_kernel(starts, whole, *refs):
+    for part, ref in enumerate(refs):
+        ref[...] = whole[starts[part] : starts[part + 1], :]
+
+
+def early_pre_kernel(starts, saved, weight, *refs):
+    parts = len(starts) - 1
+    for part in range(parts):
+        act, bend = refs[2 * part : 2 * part + 2]
+        first, extent = starts[part], starts[part + 1] - starts[part]
+        tile = tile_of(extent, 256, 16)
+
+        @pl.loop(0, extent // tile)
+        def _(index):
+            here = pl.ds(pl.multiple_of(index * tile, tile), tile)
+            rows = pl.ds(pl.multiple_of(first + index * tile, 16), tile)
+            pre = jnp.dot(saved[rows, :], weight[...], preferred_element_type=f32)
+            sigma = jax.nn.sigmoid(pre)
+            act[here, :] = (pre * sigma).astype(bf16)
+            bend[here, :] = (sigma * (1.0 + pre * (1.0 - sigma))).astype(bf16)
+
+        if part:
+            refs[2 * parts + part - 1][...] = saved[first : first + extent, :]
+
+
+def early_grads_kernel(sections, first, last_part, saved, leaving, arrived, act, bend, weight, *refs):
     last = lax.axis_index("section") == sections - 1
-    first_core = lax.rem(lax.axis_index("dev"), 2) == 0
-
-    @tiles(saved.shape[0], tile_of(saved.shape[0], 256, 16))
-    def _(rows):
-        here = jnp.where(last, leaving[rows, :], arrived[rows, :])
+    extent = arrived.shape[0]
+    before, (grad, slope, one_out, two_out) = refs[:-4], refs[-4:]
+    tile = tile_of(extent, 672, 16)
+
+    @pl.loop(0, extent // tile)
+    def _(index):
+        rows = pl.ds(pl.multiple_of(index * tile, tile), tile)
+        whole = pl.ds(pl.multiple_of(first + index * tile, 16), tile)
+        here = jnp.where(last, leaving[whole, :], arrived[rows, :])
         grad[rows, :] = here
         back = lax.dot_general(
             here, weight[...], (((1,), (1,)), ((), ())), preferred_element_type=f32
@@ -144,10 +164,37 @@
         slope[rows, :] = (back * bend[rows, :].astype(f32)).astype(bf16)
 
     over_rows = (((0,), (0,)), ((), ()))
-    one = lax.dot_general(saved[...], slope[...], over_rows, preferred_element_type=f32)
+    one = lax.dot_general(saved[:extent, :], slope[...], over_rows, preferred_element_type=f32)
     two = lax.dot_general(grad[...], act[...], over_rows, preferred_element_type=f32)
-    keep[...] = jnp.where(first_core, one, two)
-    send[...] = jnp.where(first_core, two, one).astype(bf16)
+    if before:
+        one, two = one + before[0][...], two + before[1][...]
+    if last_part:
+        first_core = lax.rem(lax.axis_index("dev"), 2) == 0
+        one_out[...] = jnp.where(first_core, one, two)
+        two_out[...] = jnp.where(first_core, two, one).astype(bf16)
+    else:
+        one_out[...] = one
+        two_out[...] = two
+
+
+def input_grad_kernel(parts, weight, *refs):
+    out, start = refs[-1], 0
+    for part in range(parts):
+        grad, slope = refs[2 * part : 2 * part + 2]
+        extent = grad.shape[0]
+        tile = tile_of(extent, 1024, 16)
+        first = start
+
+        @pl.loop(0, extent // tile)
+        def _(index):
+            rows = pl.ds(pl.multiple_of(index * tile, tile), tile)
+            whole = pl.ds(pl.multiple_of(first + index * tile, 16), tile)
+            term = lax.dot_general(
+                slope[rows, :], weight[...], (((1,), (1,)), ((), ())), preferred_element_type=f32
+            )
+            out[whole, :] = (grad[rows, :].astype(f32) + term).astype(bf16)
+
+        start += extent
 
 
 def pieces_kernel(count, keep, got, own, *pieces):
@@ -286,7 +333,19 @@
     steps = range(1, count)
 
     late_arrived = from_behind(late_sent[0], "section", 1)
-    early_arrived = from_behind(upstream_grad[0], "section", -1)
+    pixels = upstream_grad.shape[1]
+    tail = 2 * tile_of(pixels, 256, 16)
+    starts = (0, pixels - tail, pixels) if tail < pixels else (0, pixels)
+    parts = len(starts) - 1
+    extents = [starts[part + 1] - starts[part] for part in range(parts)]
+    leaving = whole_arrays(
+        functools.partial(cut_kernel, starts),
+        [shape((extent, upstream_grad.shape[2]), bf16) for extent in extents],
+        [upstream_grad[0]],
+    )
+    early_arrived = []
+    for part in range(parts):
+        early_arrived.append(from_behind(leaving[part], "section", -1))
     expand_two, reduce_two = swap(expand_late[0]), swap(reduce_late[0])
     one = jnp.concatenate([gain_inner, shift_inner], axis=0)
     two = swap(one)
@@ -295,23 +354,38 @@
     blocks = gather(own_rows)
 
     saved = early_saved[0]
-    pixels, narrow = saved.shape
-    wide = expand_early.shape[2]
-    work = 2 * pixels * narrow * wide
-    act, bend = whole_arrays(
-        early_pre_kernel, [shape((pixels, wide), bf16)] * 2, [saved, expand_early[0]], work
-    )
-    grad, slope, keep, send = whole_arrays(
-        functools.partial(early_grads_kernel, sections),
-        [
-            shape((pixels, narrow), bf16),
-            shape((pixels, wide), bf16),
-            shape((narrow, wide), f32),
-            shape((narrow, wide), bf16),
-        ],
-        [saved, exit_grad, early_arrived, act, bend, reduce_early[0]],
-        3 * work,
-    )
+    narrow, wide = expand_early.shape[1:]
+    work = 2 * narrow * wide
+    pre = whole_arrays(
+        functools.partial(early_pre_kernel, starts),
+        [shape((extents[part // 2], wide), bf16) for part in range(2 * parts)]
+        + [shape((extent, narrow), bf16) for extent in extents[1:]],
+        [saved, expand_early[0]],
+        pixels * work,
+    )
+    grads, sums_so_far = [], []
+    for part in range(parts):
+        final = part == parts - 1
+        grad, slope, keep, send = whole_arrays(
+            functools.partial(early_grads_kernel, sections, starts[part], final),
+            [
+                shape((extents[part], narrow), bf16),
+                shape((extents[part], wide), bf16),
+                shape((narrow, wide), f32),
+                shape((narrow, wide), bf16 if final else f32),
+            ],
+            [
+                pre[2 * parts + part - 1] if part else saved,
+                exit_grad,
+                early_arrived[part],
+                *pre[2 * part : 2 * part + 2],
+                reduce_early[0],
+                *sums_so_far,
+            ],
+            3 * extents[part] * work,
+        )
+        grads += [grad, slope]
+        sums_so_far = [keep, send]
     got = swap(send)
     share = narrow // count
     own_share, *shares = whole_arrays(
@@ -327,8 +401,7 @@
     held = -(-rows // 16) * 16
     hidden = expand_late.shape[2]
     late_work = 4 * count * held * channels * hidden
-    listed = lax.optimization_barrier(tuple(blocks[step] for step in range(count)) + (own_share,))
-    listed, own_share = list(listed[:-1]), listed[-1]
+    listed = [blocks[step] for step in range(count)]
     (mine,) = whole_arrays(late_sums_kernel, [shape((2, channels), f32)], listed)
     others = swap(mine)
     inner, sums, swapped = whole_arrays(
@@ -355,10 +428,12 @@
     )
     gathered = gather(summed)
     theirs = {step: swap(gathered[step]) for step in gathered}
-    input_grad = grad.astype(f32) + lax.dot_general(
-        slope, expand_early[0], (((1,), (1,)), ((), ())), preferred_element_type=f32
-    )
-    input_grad = input_grad.astype(bf16)
+    (input_grad,) = whole_arrays(
+        functools.partial(input_grad_kernel, parts),
+        [shape((pixels, narrow), bf16)],
+        [expand_early[0], *grads],
+        pixels * work,
+    )
     grad_expand, grad_reduce = whole_arrays(
         functools.partial(assemble_kernel, count),
         [shape((narrow, wide), f32), shape((wide, narrow), f32)],

time: 89.9 us -> 90.4 us (level)
  the two profiles are of different devices: /device:TPU:0 before, /device:TPU:27 now
where the time goes in v3:
time: 90.4 us; the launch traced here: 90 us
  waiting for transfers between devices  36.3 us (40%)
  starting transfers between devices  31.7 us (35%)
  Pallas kernels  16.5 us (18%)
  local copies, waits for them, and re-layouts  3.47 us (4%)
  other arithmetic  1.04 us (1%)
  between operations  0.93 us (1%)
    ppermute x12, waiting for transfers between devices, across(): return lax.ppermute(x, 'dev', pairs)  32.2 us
    ppermute x10, starting transfers between devices, swap(): lax.ppermute(x, 'dev', [(i, i ^ 1) for i in range(lax.axis_size('dev'))])  19.8 us
    pallas_call x12, Pallas kernels, whole_arrays(): pl.pallas_call(body, out_shape=list(outs), in_specs=[pl.BlockSpec(memory_...  16.5 us
    ppermute x3, starting transfers between devices, from_behind(): return lax.ppermute(x, axis, pairs)  8.34 us
    ppermute x3, waiting for transfers between devices, from_behind(): return lax.ppermute(x, axis, pairs)  3.86 us
    ppermute x12, starting transfers between devices, across(): return lax.ppermute(x, 'dev', pairs)  3.63 us
    unnamed x26, local copies, waits for them, and re-layouts  3.47 us
  transfers between devices with their start and end apart: 25, of which 10 were waited for; matrix products, arithmetic and copies ran while one was open for 1% of the time, Pallas kernels for 15%

profile of v3, /device:TPU:27, one launch (start us, length us, event | category | flops | bytes accessed | tf_op | source)
XLA Modules:
  0.0 90.0 jit_solution(7715117922558050720)
XLA Ops:
  0.7 1.2 %copy-done.4 = bf16[1,1568,256]{2,1,0:T(8,128)(2,1)S(1)} copy-done((bf16[1,1568,256]{2,1,0:T(8,128)(2,1)S(1)}, bf16[1,1568,256]{2,1,0:T(8,128)(2,1)}, u32[]{:S(2)}) %copy-start.4) | copy-done | bytes 802840
  1.9 0.9 shard_map.160
  2.8 2.2 %collective-permute-start.12 = (bf16[1120,256]{1,0:T(8,128)(2,1)}, bf16[1120,256]{1,0:T(8,128)(2,1)S(1)}, u32[]{:S(2)}, u32[]{:S(2)}) collective-permute-start(bf16[1120,256]{1,0:T(8,128)(2,1)} %get-tuple-element.39), channel_id=1, source_target_pairs={{8,0},{16,8},{24,16},{9,1},{17,9},{25,17},{10,2},{18,10},{26,18},{... | collective-permute-start | bytes 1720328 | tf_op jit(solution)/shard_map/ppermute | solution.py:19
  4.9 1.9 %collective-permute-start.13 = (bf16[448,256]{1,0:T(8,128)(2,1)S(1)}, bf16[448,256]{1,0:T(8,128)(2,1)S(1)}, u32[]{:S(2)}, u32[]{:S(2)}) collective-permute-start(bf16[448,256]{1,0:T(8,128)(2,1)S(1)} %get-tuple-element.45), channel_id=1, source_target_pairs={{8,0},{16,8},{24,16},{9,1},{17,9},{25,17},{10,2},{18,10},{26,18},{... | collective-permute-start | bytes 688136 | tf_op jit(solution)/shard_map/ppermute | solution.py:19
  6.8 4.3 %collective-permute-start = (bf16[98,1024]{1,0:T(8,128)(2,1)}, bf16[98,1024]{1,0:T(8,128)(2,1)}, u32[]{:S(2)}, u32[]{:S(2)}) collective-permute-start(bf16[98,1024]{1,0:T(8,128)(2,1)} %bitcast.26), channel_id=1, source_target_pairs={{0,8},{8,16},{16,24},{1,9},{9,17},{17,25},{2,10},{10,18},{18,26},{... | collective-permute-start | bytes 602120 | tf_op jit(solution)/shard_map/ppermute | solution.py:19
  11.1 1.6 %collective-permute-start.5 = (bf16[1024,512]{1,0:T(8,128)(2,1)}, bf16[1024,512]{1,0:T(8,128)(2,1)}, u32[]{:S(2)}, u32[]{:S(2)}) collective-permute-start(bf16[1024,512]{1,0:T(8,128)(2,1)} %bitcast.20), channel_id=1, source_target_pairs={{0,1},{1,0},{2,3},{3,2},{4,5},{5,4},{6,7},{7,6},{8,9},{9,8},{10,11... | collective-permute-start | bytes 3145736 | tf_op jit(solution)/shard_map/ppermute | solution.py:23
  12.7 0.1 collective-permute-start.8
  12.8 1.1 %copy-done.3 = bf16[1,1568,256]{2,1,0:T(8,128)(2,1)S(1)} copy-done((bf16[1,1568,256]{2,1,0:T(8,128)(2,1)S(1)}, bf16[1,1568,256]{2,1,0:T(8,128)(2,1)}, u32[]{:S(2)}) %copy-start.3) | copy-done | bytes 802840
  13.9 1.0 %copy-done.5 = bf16[1,256,1024]{2,1,0:T(8,128)(2,1)S(1)} copy-done((bf16[1,256,1024]{2,1,0:T(8,128)(2,1)S(1)}, bf16[1,256,1024]{2,1,0:T(8,128)(2,1)}, u32[]{:S(2)}) %copy-start.5) | copy-done | bytes 524312
  15.0 3.1 %shard_map.161 = (bf16[1120,1024]{1,0:T(8,128)(2,1)S(1)}, bf16[1120,1024]{1,0:T(8,128)(2,1)S(1)}, bf16[448,1024]{1,0:T(8,128)(2,1)S(1)}, bf16[448,1024]{1,0:T(8,128)(2,1)S(1)}, bf16[448,256]{1,0:T(8,128)(2,1)S(1)}) custom-call(bf16[1568,256]{1,0:T(8,128)(2,1)S(1)} %bitcast.15, bf16[256,1024]{1,0:T(8,128)(2,1)S(1)} %bitcast.18), custom_call_target="tpu_custom_call" | custom-call | flops 822083584 | bytes 7979008 | tf_op jit(solution)/shard_map/pallas_call | solution.py:82
  18.1 1.5 %collective-permute-done.12.arrived = bf16[1120,256]{1,0:T(8,128)(2,1)S(1)} collective-permute-done((bf16[1120,256]{1,0:T(8,128)(2,1)}, bf16[1120,256]{1,0:T(8,128)(2,1)S(1)}, u32[]{:S(2)}, u32[]{:S(2)}) %collective-permute-start.12) | collective-permute-done | bytes 573472 | tf_op jit(solution)/shard_map/ppermute | solution.py:19
  19.6 2.5 %shard_map.162 = (bf16[1120,256]{1,0:T(8,128)(2,1)S(1)}, bf16[1120,1024]{1,0:T(8,128)(2,1)S(1)}, f32[256,1024]{1,0:T(8,128)S(1)}, f32[256,1024]{1,0:T(8,128)S(1)}) custom-call(bf16[1568,256]{1,0:T(8,128)(2,1)S(1)} %bitcast.16, bf16[1568,256]{1,0:T(8,128)(2,1)S(1)} %copy-done, bf16[1120,256]{1,0:T(8,128)(2,1)S(1)} %collective-permute-done.12.arrived, ...), custom_call_target="tpu_custom_call" | custom-call | flops 1761607680 | bytes 12255232 | tf_op jit(solution)/shard_map/pallas_call | solution.py:82
  22.2 2.4 %collective-permute-done.13.arrived = bf16[448,256]{1,0:T(8,128)(2,1)S(1)} collective-permute-done((bf16[448,256]{1,0:T(8,128)(2,1)S(1)}, bf16[448,256]{1,0:T(8,128)(2,1)S(1)}, u32[]{:S(2)}, u32[]{:S(2)}) %collective-permute-start.13) | collective-permute-done | bytes 229408 | tf_op jit(solution)/shard_map/ppermute | solution.py:19
  24.5 1.0 %shard_map.163 = (bf16[448,256]{1,0:T(8,128)(2,1)S(1)}, bf16[448,1024]{1,0:T(8,128)(2,1)S(1)}, f32[256,1024]{1,0:T(8,128)S(1)}, bf16[256,1024]{1,0:T(8,128)(2,1)S(1)}) custom-call(bf16[448,256]{1,0:T(8,128)(2,1)S(1)} %get-tuple-element.44.saved, bf16[1568,256]{1,0:T(8,128)(2,1)S(1)} %copy-done, bf16[448,256]{1,0:T(8,128)(2,1)S(1)} %collective-permute-done.13.arrived, ...), custom_call_target="tpu_custom_call" | custom-call | flops 704643072 | bytes 8437760 | tf_op jit(solution)/shard_map/pallas_call | solution.py:82
  25.5 0.0 copy-start.11
  25.6 0.0 copy-start.12
  25.6 0.0 copy-start.7
  25.6 0.0 copy-start.8
  25.6 0.0 copy-start.9
  25.6 2.7 %collective-permute-start.14 = (bf16[256,1024]{1,0:T(8,128)(2,1)S(1)}, bf16[256,1024]{1,0:T(8,128)(2,1)S(1)}, u32[]{:S(2)}, u32[]{:S(2)}) collective-permute-start(bf16[256,1024]{1,0:T(8,128)(2,1)S(1)} %get-tuple-element.53), channel_id=1, source_target_pairs={{0,1},{1,0},{2,3},{3,2},{4,5},{5,4},{6,7},{7,6},{8,9},{9,8},{10,11... | collective-permute-start | bytes 1572872 | tf_op jit(solution)/shard_map/ppermute | solution.py:23
  28.3 0.0 collective-permute-done
  28.3 1.0 %broadcast_select_fusion.refs_0_.rows = bf16[98,1024]{1,0:T(8,128)(2,1)S(1)} fusion(bf16[98,1024]{1,0:T(8,128)(2,1)S(1)} %copy-done.10, bf16[98,1024]{1,0:T(8,128)(2,1)} %collective-permute-done, pred[]{:T(512)S(6)} %eq.3), kind=kLoop, calls=%fused_computation.2 | loop fusion | flops 100352 | bytes 602113 | tf_op jit(solution)/shard_map/jit(_where)/select_n | solution.py:353
  29.3 0.1 collective-permute-start.2
  29.4 0.2 collective-permute-start.1
  29.6 12.3 %collective-permute-done.2.refs_2_ = bf16[98,1024]{1,0:T(8,128)(2,1)S(1)} collective-permute-done((bf16[98,1024]{1,0:T(8,128)(2,1)S(1)}, bf16[98,1024]{1,0:T(8,128)(2,1)S(1)}, u32[]{:S(2)}, u32[]{:S(2)}) %collective-permute-start.2) | collective-permute-done | bytes 200736 | tf_op jit(solution)/shard_map/ppermute | solution.py:38
  41.9 0.0 collective-permute-start.3
  41.9 6.4 %collective-permute-done.3.refs_3_ = bf16[98,1024]{1,0:T(8,128)(2,1)S(1)} collective-permute-done((bf16[98,1024]{1,0:T(8,128)(2,1)S(1)}, bf16[98,1024]{1,0:T(8,128)(2,1)S(1)}, u32[]{:S(2)}, u32[]{:S(2)}) %collective-permute-start.3) | collective-permute-done | bytes 200736 | tf_op jit(solution)/shard_map/ppermute | solution.py:38
  48.3 0.2 shard_map.156.refs_4_
  48.5 1.4 %collective-permute-start.4 = (f32[2,1024]{1,0:T(2,128)S(1)}, f32[2,1024]{1,0:T(2,128)S(1)}, u32[]{:S(2)}, u32[]{:S(2)}) collective-permute-start(f32[2,1024]{1,0:T(2,128)S(1)} %shard_map.156.refs_4_), channel_id=1, source_target_pairs={{0,1},{1,0},{2,3},{3,2},{4,5},{5,4},{6,7},{7,6},{8,9},{9,8},{10,11... | collective-permute-start | bytes 24584 | tf_op jit(solution)/shard_map/ppermute | solution.py:23
  49.9 0.0 collective-permute-done.14.got
  49.9 0.1 shard_map.165
  50.0 0.0 copy-start.2
  50.0 0.1 collective-permute-start.16
  50.2 0.3 collective-permute-start.7
  50.5 0.2 collective-permute-done.4.refs_5_
  50.7 2.4 %shard_map.157 = (f32[448,1024]{1,0:T(8,128)S(1)}, f32[2,1024]{1,0:T(2,128)S(1)}, f32[2,1024]{1,0:T(2,128)S(1)}) custom-call(bf16[98,1024]{1,0:T(8,128)(2,1)S(1)} %broadcast_select_fusion.refs_0_.rows, bf16[98,1024]{1,0:T(8,128)(2,1)S(1)} %collective-permute-done.1.refs_1_, bf16[98,1024]{1,0:T(8,128)(2,1)S(1)} %collective-permute-done.2.refs_2_, ...), custom_call_target="tpu_custom_call" | custom-call | flops 939524096 | bytes 4775936 | tf_op jit(solution)/shard_map/pallas_call | solution.py:82
  53.1 0.4 collective-permute-start.6
  53.6 1.1 %collective-permute-start.15 = (bf16[64,1024]{1,0:T(8,128)(2,1)S(1)}, bf16[64,1024]{1,0:T(8,128)(2,1)S(1)}, u32[]{:S(2)}, u32[]{:S(2)}) collective-permute-start(bf16[64,1024]{1,0:T(8,128)(2,1)S(1)} %get-tuple-element.55), channel_id=1, source_target_pairs={{0,2},{1,3},{2,0},{3,1},{4,6},{5,7},{6,4},{7,5},{8,10},{9,11},{10,... | collective-permute-start | bytes 393224 | tf_op jit(solution)/shard_map/ppermute | solution.py:38
  54.7 0.5 collective-permute-done.16
  55.2 0.1 collective-permute-start.17
  55.2 0.0 collective-permute-done.7.two
  55.3 0.0 collective-permute-done.6.got
  55.3 0.0 copy-start.6
  55.3 1.1 %shard_map.158 = (f32[98,1024]{1,0:T(8,128)S(1)}, bf16[98,1024]{1,0:T(8,128)(2,1)S(1)}, f32[98,1024]{1,0:T(8,128)S(1)}, bf16[98,1024]{1,0:T(8,128)(2,1)S(1)}) custom-call(f32[448,1024]{1,0:T(8,128)S(1)} %get-tuple-element.32.inner, f32[2,1024]{1,0:T(2,128)S(1)} %get-tuple-element.33.sums, f32[2,1024]{1,0:T(2,128)S(1)} %collective-permute-done.6.got, ...), custom_call_target="tpu_custom_call" | custom-call | flops 939524096 | bytes 5361664 | tf_op jit(solution)/shard_map/pallas_call | solution.py:82
  56.4 0.4 collective-permute-start.10
  56.9 1.6 %collective-permute-done.15.refs_0_ = bf16[64,1024]{1,0:T(8,128)(2,1)S(1)} collective-permute-done((bf16[64,1024]{1,0:T(8,128)(2,1)S(1)}, bf16[64,1024]{1,0:T(8,128)(2,1)S(1)}, u32[]{:S(2)}, u32[]{:S(2)}) %collective-permute-start.15) | collective-permute-done | bytes 131104 | tf_op jit(solution)/shard_map/ppermute | solution.py:38
  58.5 5.7 %collective-permute-done.17.refs_1_ = bf16[64,1024]{1,0:T(8,128)(2,1)S(1)} collective-permute-done((bf16[64,1024]{1,0:T(8,128)(2,1)S(1)}, bf16[64,1024]{1,0:T(8,128)(2,1)S(1)}, u32[]{:S(2)}, u32[]{:S(2)}) %collective-permute-start.17) | collective-permute-done | bytes 131104 | tf_op jit(solution)/shard_map/ppermute | solution.py:38
  64.1 0.1 shard_map.166.refs_0_
  64.2 0.1 collective-permute-start.19
  64.3 0.1 collective-permute-start.9
  64.3 1.5 %collective-permute-start.18 = (bf16[64,1024]{1,0:T(8,128)(2,1)S(1)}, bf16[64,1024]{1,0:T(8,128)(2,1)S(1)}, u32[]{:S(2)}, u32[]{:S(2)}) collective-permute-start(bf16[64,1024]{1,0:T(8,128)(2,1)S(1)} %shard_map.166.refs_0_), channel_id=1, source_target_pairs={{0,2},{1,3},{2,0},{3,1},{4,6},{5,7},{6,4},{7,5},{8,10},{9,11},{10,... | collective-permute-start | bytes 393224 | tf_op jit(solution)/shard_map/ppermute | solution.py:38
  65.8 5.7 %collective-permute-done.19.refs_2_ = bf16[64,1024]{1,0:T(8,128)(2,1)S(1)} collective-permute-done((bf16[64,1024]{1,0:T(8,128)(2,1)S(1)}, bf16[64,1024]{1,0:T(8,128)(2,1)S(1)}, u32[]{:S(2)}, u32[]{:S(2)}) %collective-permute-start.19) | collective-permute-done | bytes 131104 | tf_op jit(solution)/shard_map/ppermute | solution.py:38
  71.5 0.0 collective-permute-start.20
  71.5 0.0 collective-permute-done.10
  71.6 0.1 collective-permute-start.11
  71.7 1.2 %collective-permute-start.21 = (bf16[64,1024]{1,0:T(8,128)(2,1)S(1)}, bf16[64,1024]{1,0:T(8,128)(2,1)S(1)}, u32[]{:S(2)}, u32[]{:S(2)}) collective-permute-start(bf16[64,1024]{1,0:T(8,128)(2,1)S(1)} %shard_map.166.refs_0_), channel_id=1, source_target_pairs={{0,1},{1,0},{2,3},{3,2},{4,5},{5,4},{6,7},{7,6},{8,9},{9,8},{10,11... | collective-permute-start | bytes 393224 | tf_op jit(solution)/shard_map/ppermute | solution.py:23
  72.8 0.1 collective-permute-done.9.refs_0_
  72.9 6.6 %collective-permute-start.23 = (bf16[64,1024]{1,0:T(8,128)(2,1)S(1)}, bf16[64,1024]{1,0:T(8,128)(2,1)S(1)}, u32[]{:S(2)}, u32[]{:S(2)}) collective-permute-start(bf16[64,1024]{1,0:T(8,128)(2,1)S(1)} %collective-permute-done.19.refs_2_), channel_id=1, source_target_pairs={{0,1},{1,0},{2,3},{3,2},{4,5},{5,4},{6,7},{7,6},{8,9},{9,8},{10,11... | collective-permute-start | bytes 393224 | tf_op jit(solution)/shard_map/ppermute | solution.py:23
  79.5 0.0 collective-permute-done.18.refs_1_
  79.5 3.5 %collective-permute-start.22 = (bf16[64,1024]{1,0:T(8,128)(2,1)S(1)}, bf16[64,1024]{1,0:T(8,128)(2,1)S(1)}, u32[]{:S(2)}, u32[]{:S(2)}) collective-permute-start(bf16[64,1024]{1,0:T(8,128)(2,1)S(1)} %collective-permute-done.18.refs_1_), channel_id=1, source_target_pairs={{0,1},{1,0},{2,3},{3,2},{4,5},{5,4},{6,7},{7,6},{8,9},{9,8},{10,11... | collective-permute-start | bytes 393224 | tf_op jit(solution)/shard_map/ppermute | solution.py:23
  83.0 2.0 %collective-permute-start.24 = (bf16[64,1024]{1,0:T(8,128)(2,1)S(1)}, bf16[64,1024]{1,0:T(8,128)(2,1)S(1)}, u32[]{:S(2)}, u32[]{:S(2)}) collective-permute-start(bf16[64,1024]{1,0:T(8,128)(2,1)S(1)} %collective-permute-done.20.refs_3_), channel_id=1, source_target_pairs={{0,1},{1,0},{2,3},{3,2},{4,5},{5,4},{6,7},{7,6},{8,9},{9,8},{10,11... | collective-permute-start | bytes 393224 | tf_op jit(solution)/shard_map/ppermute | solution.py:23
  85.0 2.3 %shard_map.164 = bf16[1568,256]{1,0:T(8,128)(2,1)} custom-call(bf16[256,1024]{1,0:T(8,128)(2,1)S(1)} %bitcast.19, bf16[1120,256]{1,0:T(8,128)(2,1)S(1)} %get-tuple-element.42.refs_0_, bf16[1120,1024]{1,0:T(8,128)(2,1)S(1)} %get-tuple-element.43.refs_1_, bf16[448,256]{1,0:T(8,128)(2,1)S(1)} %get-tuple-element.50.refs_2_, ...), custom_call_target="tpu_custom_call" | custom-call | flops 822083584 | bytes 5341184 | tf_op jit(solution)/shard_map/pallas_call | solution.py:82
  87.3 0.7 shard_map.159
  88.1 2.0 %shard_map.167 = (f32[256,1024]{1,0:T(8,128)}, f32[1024,256]{1,0:T(8,128)}) custom-call(bf16[64,1024]{1,0:T(8,128)(2,1)S(1)} %shard_map.166.refs_0_, bf16[64,1024]{1,0:T(8,128)(2,1)S(1)} %collective-permute-done.18.refs_1_, bf16[64,1024]{1,0:T(8,128)(2,1)S(1)} %collective-permute-done.19.refs_2_, bf16[64,1024]{1,0:T(8,128)(2,1)S(1)} %collective-permute-done.20.refs_3_, ...), custom_call_target="tpu_custom_call" | custom-call | flops 3145728 | bytes 3145728 | tf_op jit(solution)/shard_map/pallas_call | solution.py:82
  (28 shorter events, 0.1 us)
Async XLA Ops:
  0.6 19.0 %copy-start.1 = (bf16[1,1024,256]{2,1,0:T(8,128)(2,1)S(1)}, bf16[1,1024,256]{2,1,0:T(8,128)(2,1)}, u32[]{:S(2)}) copy-start(bf16[1,1024,256]{2,1,0:T(8,128)(2,1)} %param.25) | copy-start | bytes 1572868
  0.6 19.0 %copy-start = (bf16[1568,256]{1,0:T(8,128)(2,1)S(1)}, bf16[1568,256]{1,0:T(8,128)(2,1)}, u32[]{:S(2)}) copy-start(bf16[1568,256]{1,0:T(8,128)(2,1)} %leaving.3) | copy-start | bytes 2408452
  0.7 1.2 %copy-start.4 = (bf16[1,1568,256]{2,1,0:T(8,128)(2,1)S(1)}, bf16[1,1568,256]{2,1,0:T(8,128)(2,1)}, u32[]{:S(2)}) copy-start(bf16[1,1568,256]{2,1,0:T(8,128)(2,1)} %param.22) | copy-start | bytes 2408452
  2.8 16.9 %collective-permute-start.12 = (bf16[1120,256]{1,0:T(8,128)(2,1)}, bf16[1120,256]{1,0:T(8,128)(2,1)S(1)}, u32[]{:S(2)}, u32[]{:S(2)}) collective-permute-start(bf16[1120,256]{1,0:T(8,128)(2,1)} %get-tuple-element.39), channel_id=1, source_target_pairs={{8,0},{16,8},{24,16},{9,1},{17,9},{25,17},{10,2},{18,10},{26,18},{... | collective-permute-start | bytes 1720328 | tf_op jit(solution)/shard_map/ppermute | solution.py:19
  4.9 19.6 %collective-permute-start.13 = (bf16[448,256]{1,0:T(8,128)(2,1)S(1)}, bf16[448,256]{1,0:T(8,128)(2,1)S(1)}, u32[]{:S(2)}, u32[]{:S(2)}) collective-permute-start(bf16[448,256]{1,0:T(8,128)(2,1)S(1)} %get-tuple-element.45), channel_id=1, source_target_pairs={{8,0},{16,8},{24,16},{9,1},{17,9},{25,17},{10,2},{18,10},{26,18},{... | collective-permute-start | bytes 688136 | tf_op jit(solution)/shard_map/ppermute | solution.py:19
  6.8 21.5 %collective-permute-start = (bf16[98,1024]{1,0:T(8,128)(2,1)}, bf16[98,1024]{1,0:T(8,128)(2,1)}, u32[]{:S(2)}, u32[]{:S(2)}) collective-permute-start(bf16[98,1024]{1,0:T(8,128)(2,1)} %bitcast.26), channel_id=1, source_target_pairs={{0,8},{8,16},{16,24},{1,9},{9,17},{17,25},{2,10},{10,18},{18,26},{... | collective-permute-start | bytes 602120 | tf_op jit(solution)/shard_map/ppermute | solution.py:19
  11.1 39.6 %collective-permute-start.5 = (bf16[1024,512]{1,0:T(8,128)(2,1)}, bf16[1024,512]{1,0:T(8,128)(2,1)}, u32[]{:S(2)}, u32[]{:S(2)}) collective-permute-start(bf16[1024,512]{1,0:T(8,128)(2,1)} %bitcast.20), channel_id=1, source_target_pairs={{0,1},{1,0},{2,3},{3,2},{4,5},{5,4},{6,7},{7,6},{8,9},{9,8},{10,11... | collective-permute-start | bytes 3145736 | tf_op jit(solution)/shard_map/ppermute | solution.py:23
  12.7 42.6 %collective-permute-start.8 = (bf16[512,1024]{1,0:T(8,128)(2,1)}, bf16[512,1024]{1,0:T(8,128)(2,1)S(1)}, u32[]{:S(2)}, u32[]{:S(2)}) collective-permute-start(bf16[512,1024]{1,0:T(8,128)(2,1)} %bitcast.13), channel_id=1, source_target_pairs={{0,1},{1,0},{2,3},{3,2},{4,5},{5,4},{6,7},{7,6},{8,9},{9,8},{10,11... | collective-permute-start | bytes 3145736 | tf_op jit(solution)/shard_map/ppermute | solution.py:23
  12.8 1.1 %copy-start.3 = (bf16[1,1568,256]{2,1,0:T(8,128)(2,1)S(1)}, bf16[1,1568,256]{2,1,0:T(8,128)(2,1)}, u32[]{:S(2)}) copy-start(bf16[1,1568,256]{2,1,0:T(8,128)(2,1)} %param.21) | copy-start | bytes 2408452
  13.9 1.0 %copy-start.5 = (bf16[1,256,1024]{2,1,0:T(8,128)(2,1)S(1)}, bf16[1,256,1024]{2,1,0:T(8,128)(2,1)}, u32[]{:S(2)}) copy-start(bf16[1,256,1024]{2,1,0:T(8,128)(2,1)} %param.24) | copy-start | bytes 1572868
  24.5 3.8 %copy-start.10 = (bf16[98,1024]{1,0:T(8,128)(2,1)S(1)}, bf16[98,1024]{1,0:T(8,128)(2,1)}, u32[]{:S(2)}) copy-start(bf16[98,1024]{1,0:T(8,128)(2,1)} %param.14) | copy-start | bytes 602116
  25.5 24.6 %copy-start.11 = (f32[1,512]{1,0:T(1,128)S(1)}, f32[1,512]{1,0:T(1,128)}, u32[]{:S(2)}) copy-start(f32[1,512]{1,0:T(1,128)} %param.19) | copy-start | bytes 6148
  25.6 24.6 %copy-start.12 = (f32[1,512]{1,0:T(1,128)S(1)}, f32[1,512]{1,0:T(1,128)}, u32[]{:S(2)}) copy-start(f32[1,512]{1,0:T(1,128)} %param.18) | copy-start | bytes 6148
  25.6 25.2 %copy-start.7 = (bf16[1,1024,512]{2,1,0:T(8,128)(2,1)S(1)}, bf16[1,1024,512]{2,1,0:T(8,128)(2,1)}, u32[]{:S(2)}) copy-start(bf16[1,1024,512]{2,1,0:T(8,128)(2,1)} %param.17) | copy-start | bytes 3145732
  25.6 25.2 %copy-start.8 = (f32[1,1024]{1,0:T(1,128)S(1)}, f32[1,1024]{1,0:T(1,128)}, u32[]{:S(2)}) copy-start(f32[1,1024]{1,0:T(1,128)} %refs_6_.1) | copy-start | bytes 12292
  25.6 25.1 %copy-start.9 = (f32[1,1024]{1,0:T(1,128)S(1)}, f32[1,1024]{1,0:T(1,128)}, u32[]{:S(2)}) copy-start(f32[1,1024]{1,0:T(1,128)} %refs_7_.1) | copy-start | bytes 12292
  25.6 24.3 %collective-permute-start.14 = (bf16[256,1024]{1,0:T(8,128)(2,1)S(1)}, bf16[256,1024]{1,0:T(8,128)(2,1)S(1)}, u32[]{:S(2)}, u32[]{:S(2)}) collective-permute-start(bf16[256,1024]{1,0:T(8,128)(2,1)S(1)} %get-tuple-element.53), channel_id=1, source_target_pairs={{0,1},{1,0},{2,3},{3,2},{4,5},{5,4},{6,7},{7,6},{8,9},{9,8},{10,11... | collective-permute-start | bytes 1572872 | tf_op jit(solution)/shard_map/ppermute | solution.py:23
  29.3 12.6 %collective-permute-start.2 = (bf16[98,1024]{1,0:T(8,128)(2,1)S(1)}, bf16[98,1024]{1,0:T(8,128)(2,1)S(1)}, u32[]{:S(2)}, u32[]{:S(2)}) collective-permute-start(bf16[98,1024]{1,0:T(8,128)(2,1)S(1)} %broadcast_select_fusion.refs_0_.rows), channel_id=1, source_target_pairs={{0,4},{1,5},{2,6},{3,7},{4,0},{5,1},{6,2},{7,3},{8,12},{9,13},{10,... | collective-permute-start | bytes 602120 | tf_op jit(solution)/shard_map/ppermute | solution.py:38
  29.4 12.5 %collective-permute-start.1 = (bf16[98,1024]{1,0:T(8,128)(2,1)S(1)}, bf16[98,1024]{1,0:T(8,128)(2,1)S(1)}, u32[]{:S(2)}, u32[]{:S(2)}) collective-permute-start(bf16[98,1024]{1,0:T(8,128)(2,1)S(1)} %broadcast_select_fusion.refs_0_.rows), channel_id=1, source_target_pairs={{0,2},{1,3},{2,0},{3,1},{4,6},{5,7},{6,4},{7,5},{8,10},{9,11},{10,... | collective-permute-start | bytes 602120 | tf_op jit(solution)/shard_map/ppermute | solution.py:38
  41.9 6.4 %collective-permute-start.3 = (bf16[98,1024]{1,0:T(8,128)(2,1)S(1)}, bf16[98,1024]{1,0:T(8,128)(2,1)S(1)}, u32[]{:S(2)}, u32[]{:S(2)}) collective-permute-start(bf16[98,1024]{1,0:T(8,128)(2,1)S(1)} %collective-permute-done.2.refs_2_), channel_id=1, source_target_pairs={{0,2},{1,3},{2,0},{3,1},{4,6},{5,7},{6,4},{7,5},{8,10},{9,11},{10,... | collective-permute-start | bytes 602120 | tf_op jit(solution)/shard_map/ppermute | solution.py:38
  48.5 2.2 %collective-permute-start.4 = (f32[2,1024]{1,0:T(2,128)S(1)}, f32[2,1024]{1,0:T(2,128)S(1)}, u32[]{:S(2)}, u32[]{:S(2)}) collective-permute-start(f32[2,1024]{1,0:T(2,128)S(1)} %shard_map.156.refs_4_), channel_id=1, source_target_pairs={{0,1},{1,0},{2,3},{3,2},{4,5},{5,4},{6,7},{7,6},{8,9},{9,8},{10,11... | collective-permute-start | bytes 24584 | tf_op jit(solution)/shard_map/ppermute | solution.py:23
  50.0 5.2 %copy-start.2 = (bf16[1,512,1024]{2,1,0:T(8,128)(2,1)S(1)}, bf16[1,512,1024]{2,1,0:T(8,128)(2,1)}, u32[]{:S(2)}) copy-start(bf16[1,512,1024]{2,1,0:T(8,128)(2,1)} %param.20) | copy-start | bytes 3145732
  50.0 5.1 %collective-permute-start.16 = (bf16[64,1024]{1,0:T(8,128)(2,1)S(1)}, bf16[64,1024]{1,0:T(8,128)(2,1)S(1)}, u32[]{:S(2)}, u32[]{:S(2)}) collective-permute-start(bf16[64,1024]{1,0:T(8,128)(2,1)S(1)} %get-tuple-element.57), channel_id=1, source_target_pairs={{0,2},{1,3},{2,0},{3,1},{4,6},{5,7},{6,4},{7,5},{8,10},{9,11},{10,... | collective-permute-start | bytes 393224 | tf_op jit(solution)/shard_map/ppermute | solution.py:38
  50.2 5.1 %collective-permute-start.7 = (f32[2,512]{1,0:T(2,128)S(1)}, f32[2,512]{1,0:T(2,128)S(1)}, u32[]{:S(2)}, u32[]{:S(2)}) collective-permute-start(f32[2,512]{1,0:T(2,128)S(1)} %pad_maximum_fusion.one), channel_id=1, source_target_pairs={{0,1},{1,0},{2,3},{3,2},{4,5},{5,4},{6,7},{7,6},{8,9},{9,8},{10,11... | collective-permute-start | bytes 12296 | tf_op jit(solution)/shard_map/ppermute | solution.py:23
  53.1 2.1 %collective-permute-start.6 = (f32[2,1024]{1,0:T(2,128)S(1)}, f32[2,1024]{1,0:T(2,128)S(1)}, u32[]{:S(2)}, u32[]{:S(2)}) collective-permute-start(f32[2,1024]{1,0:T(2,128)S(1)} %get-tuple-element.34), channel_id=1, source_target_pairs={{0,1},{1,0},{2,3},{3,2},{4,5},{5,4},{6,7},{7,6},{8,9},{9,8},{10,11... | collective-permute-start | bytes 24584 | tf_op jit(solution)/shard_map/ppermute | solution.py:23
  53.6 4.9 %collective-permute-start.15 = (bf16[64,1024]{1,0:T(8,128)(2,1)S(1)}, bf16[64,1024]{1,0:T(8,128)(2,1)S(1)}, u32[]{:S(2)}, u32[]{:S(2)}) collective-permute-start(bf16[64,1024]{1,0:T(8,128)(2,1)S(1)} %get-tuple-element.55), channel_id=1, source_target_pairs={{0,2},{1,3},{2,0},{3,1},{4,6},{5,7},{6,4},{7,5},{8,10},{9,11},{10,... | collective-permute-start | bytes 393224 | tf_op jit(solution)/shard_map/ppermute | solution.py:38
  55.2 9.0 %collective-permute-start.17 = (bf16[64,1024]{1,0:T(8,128)(2,1)S(1)}, bf16[64,1024]{1,0:T(8,128)(2,1)S(1)}, u32[]{:S(2)}, u32[]{:S(2)}) collective-permute-start(bf16[64,1024]{1,0:T(8,128)(2,1)S(1)} %add_convert_fusion.1), channel_id=1, source_target_pairs={{0,4},{1,5},{2,6},{3,7},{4,0},{5,1},{6,2},{7,3},{8,12},{9,13},{10,... | collective-permute-start | bytes 393224 | tf_op jit(solution)/shard_map/ppermute | solution.py:38
  55.3 29.7 %copy-start.6 = (bf16[1,256,1024]{2,1,0:T(8,128)(2,1)S(1)}, bf16[1,256,1024]{2,1,0:T(8,128)(2,1)}, u32[]{:S(2)}) copy-start(bf16[1,256,1024]{2,1,0:T(8,128)(2,1)} %param.24) | copy-start | bytes 1572868
  56.4 15.1 %collective-permute-start.10 = (bf16[98,1024]{1,0:T(8,128)(2,1)S(1)}, bf16[98,1024]{1,0:T(8,128)(2,1)S(1)}, u32[]{:S(2)}, u32[]{:S(2)}) collective-permute-start(bf16[98,1024]{1,0:T(8,128)(2,1)S(1)} %get-tuple-element.38), channel_id=1, source_target_pairs={{0,2},{1,3},{2,0},{3,1},{4,6},{5,7},{6,4},{7,5},{8,10},{9,11},{10,... | collective-permute-start | bytes 602120 | tf_op jit(solution)/shard_map/ppermute | solution.py:38
  64.2 7.4 %collective-permute-start.19 = (bf16[64,1024]{1,0:T(8,128)(2,1)S(1)}, bf16[64,1024]{1,0:T(8,128)(2,1)S(1)}, u32[]{:S(2)}, u32[]{:S(2)}) collective-permute-start(bf16[64,1024]{1,0:T(8,128)(2,1)S(1)} %shard_map.166.refs_0_), channel_id=1, source_target_pairs={{0,4},{1,5},{2,6},{3,7},{4,0},{5,1},{6,2},{7,3},{8,12},{9,13},{10,... | collective-permute-start | bytes 393224 | tf_op jit(solution)/shard_map/ppermute | solution.py:38
  64.3 8.6 %collective-permute-start.9 = (bf16[98,1024]{1,0:T(8,128)(2,1)S(1)}, bf16[98,1024]{1,0:T(8,128)(2,1)S(1)}, u32[]{:S(2)}, u32[]{:S(2)}) collective-permute-start(bf16[98,1024]{1,0:T(8,128)(2,1)S(1)} %get-tuple-element.36), channel_id=1, source_target_pairs={{0,2},{1,3},{2,0},{3,1},{4,6},{5,7},{6,4},{7,5},{8,10},{9,11},{10,... | collective-permute-start | bytes 602120 | tf_op jit(solution)/shard_map/ppermute | solution.py:38
  64.3 15.2 %collective-permute-start.18 = (bf16[64,1024]{1,0:T(8,128)(2,1)S(1)}, bf16[64,1024]{1,0:T(8,128)(2,1)S(1)}, u32[]{:S(2)}, u32[]{:S(2)}) collective-permute-start(bf16[64,1024]{1,0:T(8,128)(2,1)S(1)} %shard_map.166.refs_0_), channel_id=1, source_target_pairs={{0,2},{1,3},{2,0},{3,1},{4,6},{5,7},{6,4},{7,5},{8,10},{9,11},{10,... | collective-permute-start | bytes 393224 | tf_op jit(solution)/shard_map/ppermute | solution.py:38
  71.5 11.5 %collective-permute-start.20 = (bf16[64,1024]{1,0:T(8,128)(2,1)S(1)}, bf16[64,1024]{1,0:T(8,128)(2,1)S(1)}, u32[]{:S(2)}, u32[]{:S(2)}) collective-permute-start(bf16[64,1024]{1,0:T(8,128)(2,1)S(1)} %collective-permute-done.19.refs_2_), channel_id=1, source_target_pairs={{0,2},{1,3},{2,0},{3,1},{4,6},{5,7},{6,4},{7,5},{8,10},{9,11},{10,... | collective-permute-start | bytes 393224 | tf_op jit(solution)/shard_map/ppermute | solution.py:38
  71.6 15.7 %collective-permute-start.11 = (bf16[98,1024]{1,0:T(8,128)(2,1)S(1)}, bf16[98,1024]{1,0:T(8,128)(2,1)S(1)}, u32[]{:S(2)}, u32[]{:S(2)}) collective-permute-start(bf16[98,1024]{1,0:T(8,128)(2,1)S(1)} %add_convert_fusion), channel_id=1, source_target_pairs={{0,4},{1,5},{2,6},{3,7},{4,0},{5,1},{6,2},{7,3},{8,12},{9,13},{10,... | collective-permute-start | bytes 602120 | tf_op jit(solution)/shard_map/ppermute | solution.py:38
  71.7 16.4 %collective-permute-start.21 = (bf16[64,1024]{1,0:T(8,128)(2,1)S(1)}, bf16[64,1024]{1,0:T(8,128)(2,1)S(1)}, u32[]{:S(2)}, u32[]{:S(2)}) collective-permute-start(bf16[64,1024]{1,0:T(8,128)(2,1)S(1)} %shard_map.166.refs_0_), channel_id=1, source_target_pairs={{0,1},{1,0},{2,3},{3,2},{4,5},{5,4},{6,7},{7,6},{8,9},{9,8},{10,11... | collective-permute-start | bytes 393224 | tf_op jit(solution)/shard_map/ppermute | solution.py:23
  72.9 15.2 %collective-permute-start.23 = (bf16[64,1024]{1,0:T(8,128)(2,1)S(1)}, bf16[64,1024]{1,0:T(8,128)(2,1)S(1)}, u32[]{:S(2)}, u32[]{:S(2)}) collective-permute-start(bf16[64,1024]{1,0:T(8,128)(2,1)S(1)} %collective-permute-done.19.refs_2_), channel_id=1, source_target_pairs={{0,1},{1,0},{2,3},{3,2},{4,5},{5,4},{6,7},{7,6},{8,9},{9,8},{10,11... | collective-permute-start | bytes 393224 | tf_op jit(solution)/shard_map/ppermute | solution.py:23
  79.5 8.5 %collective-permute-start.22 = (bf16[64,1024]{1,0:T(8,128)(2,1)S(1)}, bf16[64,1024]{1,0:T(8,128)(2,1)S(1)}, u32[]{:S(2)}, u32[]{:S(2)}) collective-permute-start(bf16[64,1024]{1,0:T(8,128)(2,1)S(1)} %collective-permute-done.18.refs_1_), channel_id=1, source_target_pairs={{0,1},{1,0},{2,3},{3,2},{4,5},{5,4},{6,7},{7,6},{8,9},{9,8},{10,11... | collective-permute-start | bytes 393224 | tf_op jit(solution)/shard_map/ppermute | solution.py:23
  83.0 5.0 %collective-permute-start.24 = (bf16[64,1024]{1,0:T(8,128)(2,1)S(1)}, bf16[64,1024]{1,0:T(8,128)(2,1)S(1)}, u32[]{:S(2)}, u32[]{:S(2)}) collective-permute-start(bf16[64,1024]{1,0:T(8,128)(2,1)S(1)} %collective-permute-done.20.refs_3_), channel_id=1, source_target_pairs={{0,1},{1,0},{2,3},{3,2},{4,5},{5,4},{6,7},{7,6},{8,9},{9,8},{10,11... | collective-permute-start | bytes 393224 | tf_op jit(solution)/shard_map/ppermute | solution.py:23

commit v4 on v3

--- a/solution.py
+++ b/solution.py
@@ -73,6 +73,10 @@
     return terms
 
 
+def inner_steps(count):
+    return list(range(count - 1, 2, -2)) if in_pairs(count) else []
+
+
 def piece_type(step, count):
     return f32 if in_pairs(count) and step % 2 == 0 else bf16
 
@@ -146,10 +150,11 @@
             refs[2 * parts + part - 1][...] = saved[first : first + extent, :]
 
 
-def early_grads_kernel(sections, first, last_part, saved, leaving, arrived, act, bend, weight, *refs):
+def early_grads_kernel(sections, count, first, last_part, saved, leaving, arrived, act, bend, weight, *refs):
     last = lax.axis_index("section") == sections - 1
     extent = arrived.shape[0]
-    before, (grad, slope, one_out, two_out) = refs[:-4], refs[-4:]
+    outs = 4 + len(inner_steps(count)) if last_part else 4
+    before, (grad, slope, one_out, two_out, *urgent) = refs[:-outs], refs[-outs:]
     tile = tile_of(extent, 672, 16)
 
     @pl.loop(0, extent // tile)
@@ -172,6 +177,8 @@
         first_core = lax.rem(lax.axis_index("dev"), 2) == 0
         one_out[...] = jnp.where(first_core, one, two)
         two_out[...] = jnp.where(first_core, two, one).astype(bf16)
+        for step, out in zip(inner_steps(count), urgent):
+            out[...] = two_out[rows_of(step, count, out.shape[0]), :]
     else:
         one_out[...] = one
         two_out[...] = two
@@ -197,18 +204,23 @@
         start += extent
 
 
-def pieces_kernel(count, keep, got, own, *pieces):
+def rows_of(step, count, extent):
     chip = lax.div(lax.axis_index("dev"), 2)
-    extent = own.shape[0]
-
-    def piece(index):
-        rows = pl.ds(pl.multiple_of(index * extent, extent), extent)
-        return keep[rows, :] + got[rows, :].astype(f32)
-
-    own[...] = piece(chip)
-    for step in range(1, count):
-        out = pieces[step - 1]
-        out[...] = piece(partner(chip, step, count)).astype(out.dtype)
+    index = partner(chip, step, count) if step else chip
+    return pl.ds(pl.multiple_of(index * extent, extent), extent)
+
+
+def urgent_kernel(count, keep, *refs):
+    steps = inner_steps(count)
+    for step, got, out in zip(steps, refs[: len(steps)], refs[len(steps) :]):
+        rows = rows_of(step, count, out.shape[0])
+        out[...] = (keep[rows, :] + got[...].astype(f32)).astype(bf16)
+
+
+def pieces_kernel(count, steps, keep, got, *pieces):
+    for step, out in zip(steps, pieces):
+        rows = rows_of(step, count, out.shape[0])
+        out[...] = (keep[rows, :] + got[rows, :].astype(f32)).astype(out.dtype)
 
 
 def total_kernel(factor, own, *refs):
@@ -363,17 +375,20 @@
         [saved, expand_early[0]],
         pixels * work,
     )
+    share = narrow // count
+    urgent_steps = inner_steps(count)
     grads, sums_so_far = [], []
     for part in range(parts):
         final = part == parts - 1
-        grad, slope, keep, send = whole_arrays(
-            functools.partial(early_grads_kernel, sections, starts[part], final),
+        grad, slope, keep, send, *urgent = whole_arrays(
+            functools.partial(early_grads_kernel, sections, count, starts[part], final),
             [
                 shape((extents[part], narrow), bf16),
                 shape((extents[part], wide), bf16),
                 shape((narrow, wide), f32),
                 shape((narrow, wide), bf16 if final else f32),
-            ],
+            ]
+            + [shape((share, wide), bf16)] * (len(urgent_steps) if final else 0),
             [
                 pre[2 * parts + part - 1] if part else saved,
                 exit_grad,
@@ -386,15 +401,25 @@
         )
         grads += [grad, slope]
         sums_so_far = [keep, send]
+    shares = {}
+    if urgent_steps:
+        got_urgent = [swap(piece) for piece in urgent]
+        added = whole_arrays(
+            functools.partial(urgent_kernel, count),
+            [shape((share, wide), bf16)] * len(urgent),
+            [keep, *got_urgent],
+        )
+        shares.update(zip(urgent_steps, added))
     got = swap(send)
-    share = narrow // count
-    own_share, *shares = whole_arrays(
-        functools.partial(pieces_kernel, count),
-        [shape((share, wide), f32)]
-        + [shape((share, wide), piece_type(step, count)) for step in steps],
+    other_steps = [step for step in range(count) if step not in shares]
+    added = whole_arrays(
+        functools.partial(pieces_kernel, count, other_steps),
+        [shape((share, wide), piece_type(step, count) if step else f32) for step in other_steps],
         [keep, got],
     )
-    terms = scatter(dict(zip(steps, shares)))
+    shares.update(zip(other_steps, added))
+    own_share = shares[0]
+    terms = scatter(shares)
 
     rows, channels = own_rows.shape
     total_rows = rows * lax.axis_size("dev")

time: 90.4 us -> 86.8 us (0.960)
  the two profiles are of different devices: /device:TPU:27 before, /device:TPU:5 now
where the time goes in v4:
time: 86.8 us; the launch traced here: 86.4 us
  starting transfers between devices  48.4 us (56%)
  Pallas kernels  16.5 us (19%)
  waiting for transfers between devices  16.1 us (19%)
  local copies, waits for them, and re-layouts  3.47 us (4%)
  other arithmetic  1.05 us (1%)
  between operations  0.88 us (1%)
    ppermute x11, starting transfers between devices, swap(): lax.ppermute(x, 'dev', [(i, i ^ 1) for i in range(lax.axis_size('dev'))])  19.8 us
    ppermute x12, starting transfers between devices, across(): return lax.ppermute(x, 'dev', pairs)  19.5 us
    pallas_call x13, Pallas kernels, whole_arrays(): pl.pallas_call(body, out_shape=list(outs), in_specs=[pl.BlockSpec(memory_...  16.5 us
    ppermute x12, waiting for transfers between devices, across(): return lax.ppermute(x, 'dev', pairs)  11.5 us
    ppermute x3, starting transfers between devices, from_behind(): return lax.ppermute(x, axis, pairs)  9.22 us
    ppermute x3, waiting for transfers between devices, from_behind(): return lax.ppermute(x, axis, pairs)  4.35 us
    unnamed x26, local copies, waits for them, and re-layouts  3.47 us
  transfers between devices with their start and end apart: 26, of which 9 were waited for; matrix products, arithmetic and copies ran while one was open for 1% of the time, Pallas kernels for 16%

profile of v4, /device:TPU:5, one launch (start us, length us, event | category | flops | bytes accessed | tf_op | source)
XLA Modules:
  0.0 86.4 jit_solution(327402602903765330)
XLA Ops:
  0.7 1.2 %copy-done.4 = bf16[1,1568,256]{2,1,0:T(8,128)(2,1)S(1)} copy-done((bf16[1,1568,256]{2,1,0:T(8,128)(2,1)S(1)}, bf16[1,1568,256]{2,1,0:T(8,128)(2,1)}, u32[]{:S(2)}) %copy-start.4) | copy-done | bytes 802840
  1.9 0.9 shard_map.160
  2.8 3.0 %collective-permute-start.12 = (bf16[1120,256]{1,0:T(8,128)(2,1)}, bf16[1120,256]{1,0:T(8,128)(2,1)S(1)}, u32[]{:S(2)}, u32[]{:S(2)}) collective-permute-start(bf16[1120,256]{1,0:T(8,128)(2,1)} %get-tuple-element.39), channel_id=1, source_target_pairs={{8,0},{16,8},{24,16},{9,1},{17,9},{25,17},{10,2},{18,10},{26,18},{... | collective-permute-start | bytes 1720328 | tf_op jit(solution)/shard_map/ppermute | solution.py:19
  5.8 2.3 %collective-permute-start = (bf16[98,1024]{1,0:T(8,128)(2,1)}, bf16[98,1024]{1,0:T(8,128)(2,1)}, u32[]{:S(2)}, u32[]{:S(2)}) collective-permute-start(bf16[98,1024]{1,0:T(8,128)(2,1)} %bitcast.26), channel_id=1, source_target_pairs={{0,8},{8,16},{16,24},{1,9},{9,17},{17,25},{2,10},{10,18},{18,26},{... | collective-permute-start | bytes 602120 | tf_op jit(solution)/shard_map/ppermute | solution.py:19
  8.1 1.3 %collective-permute-start.5 = (bf16[1024,512]{1,0:T(8,128)(2,1)}, bf16[1024,512]{1,0:T(8,128)(2,1)}, u32[]{:S(2)}, u32[]{:S(2)}) collective-permute-start(bf16[1024,512]{1,0:T(8,128)(2,1)} %bitcast.20), channel_id=1, source_target_pairs={{0,1},{1,0},{2,3},{3,2},{4,5},{5,4},{6,7},{7,6},{8,9},{9,8},{10,11... | collective-permute-start | bytes 3145736 | tf_op jit(solution)/shard_map/ppermute | solution.py:23
  9.4 3.9 %collective-permute-start.13 = (bf16[448,256]{1,0:T(8,128)(2,1)S(1)}, bf16[448,256]{1,0:T(8,128)(2,1)S(1)}, u32[]{:S(2)}, u32[]{:S(2)}) collective-permute-start(bf16[448,256]{1,0:T(8,128)(2,1)S(1)} %get-tuple-element.45), channel_id=1, source_target_pairs={{8,0},{16,8},{24,16},{9,1},{17,9},{25,17},{10,2},{18,10},{26,18},{... | collective-permute-start | bytes 688136 | tf_op jit(solution)/shard_map/ppermute | solution.py:19
  13.3 0.4 collective-permute-start.8
  13.7 1.1 %copy-done.3 = bf16[1,1568,256]{2,1,0:T(8,128)(2,1)S(1)} copy-done((bf16[1,1568,256]{2,1,0:T(8,128)(2,1)S(1)}, bf16[1,1568,256]{2,1,0:T(8,128)(2,1)}, u32[]{:S(2)}) %copy-start.3) | copy-done | bytes 802840
  14.8 1.0 %copy-done.5 = bf16[1,256,1024]{2,1,0:T(8,128)(2,1)S(1)} copy-done((bf16[1,256,1024]{2,1,0:T(8,128)(2,1)S(1)}, bf16[1,256,1024]{2,1,0:T(8,128)(2,1)}, u32[]{:S(2)}) %copy-start.5) | copy-done | bytes 524312
  15.9 3.1 %shard_map.161 = (bf16[1120,1024]{1,0:T(8,128)(2,1)S(1)}, bf16[1120,1024]{1,0:T(8,128)(2,1)S(1)}, bf16[448,1024]{1,0:T(8,128)(2,1)S(1)}, bf16[448,1024]{1,0:T(8,128)(2,1)S(1)}, bf16[448,256]{1,0:T(8,128)(2,1)S(1)}) custom-call(bf16[1568,256]{1,0:T(8,128)(2,1)S(1)} %bitcast.15, bf16[256,1024]{1,0:T(8,128)(2,1)S(1)} %bitcast.18), custom_call_target="tpu_custom_call" | custom-call | flops 822083584 | bytes 7979008 | tf_op jit(solution)/shard_map/pallas_call | solution.py:86
  19.0 4.3 %collective-permute-done = bf16[98,1024]{1,0:T(8,128)(2,1)} collective-permute-done((bf16[98,1024]{1,0:T(8,128)(2,1)}, bf16[98,1024]{1,0:T(8,128)(2,1)}, u32[]{:S(2)}, u32[]{:S(2)}) %collective-permute-start) | collective-permute-done | bytes 200736 | tf_op jit(solution)/shard_map/ppermute | solution.py:19
  23.4 1.0 %broadcast_select_fusion.refs_0_.rows = bf16[98,1024]{1,0:T(8,128)(2,1)S(1)} fusion(bf16[98,1024]{1,0:T(8,128)(2,1)S(1)} %copy-done.10, bf16[98,1024]{1,0:T(8,128)(2,1)} %collective-permute-done, pred[]{:T(512)S(6)} %eq.3), kind=kLoop, calls=%fused_computation.2 | loop fusion | flops 100352 | bytes 602113 | tf_op jit(solution)/shard_map/jit(_where)/select_n | solution.py:365
  24.3 2.3 %collective-permute-start.2 = (bf16[98,1024]{1,0:T(8,128)(2,1)S(1)}, bf16[98,1024]{1,0:T(8,128)(2,1)S(1)}, u32[]{:S(2)}, u32[]{:S(2)}) collective-permute-start(bf16[98,1024]{1,0:T(8,128)(2,1)S(1)} %broadcast_select_fusion.refs_0_.rows), channel_id=1, source_target_pairs={{0,4},{1,5},{2,6},{3,7},{4,0},{5,1},{6,2},{7,3},{8,12},{9,13},{10,... | collective-permute-start | bytes 602120 | tf_op jit(solution)/shard_map/ppermute | solution.py:38
  26.7 1.3 %collective-permute-start.1 = (bf16[98,1024]{1,0:T(8,128)(2,1)S(1)}, bf16[98,1024]{1,0:T(8,128)(2,1)S(1)}, u32[]{:S(2)}, u32[]{:S(2)}) collective-permute-start(bf16[98,1024]{1,0:T(8,128)(2,1)S(1)} %broadcast_select_fusion.refs_0_.rows), channel_id=1, source_target_pairs={{0,2},{1,3},{2,0},{3,1},{4,6},{5,7},{6,4},{7,5},{8,10},{9,11},{10,... | collective-permute-start | bytes 602120 | tf_op jit(solution)/shard_map/ppermute | solution.py:38
  28.0 2.5 %shard_map.162 = (bf16[1120,256]{1,0:T(8,128)(2,1)S(1)}, bf16[1120,1024]{1,0:T(8,128)(2,1)S(1)}, f32[256,1024]{1,0:T(8,128)S(1)}, f32[256,1024]{1,0:T(8,128)S(1)}) custom-call(bf16[1568,256]{1,0:T(8,128)(2,1)S(1)} %bitcast.16, bf16[1568,256]{1,0:T(8,128)(2,1)S(1)} %copy-done, bf16[1120,256]{1,0:T(8,128)(2,1)S(1)} %collective-permute-done.12.arrived, ...), custom_call_target="tpu_custom_call" | custom-call | flops 1761607680 | bytes 12255232 | tf_op jit(solution)/shard_map/pallas_call | solution.py:86
  30.5 0.0 collective-permute-done.13.arrived
  30.5 0.0 copy-start.11
  30.5 0.0 copy-start.12
  30.6 0.0 copy-start.7
  30.6 0.0 copy-start.8
  30.6 0.0 copy-start.9
  30.6 1.0 %shard_map.163 = (bf16[448,256]{1,0:T(8,128)(2,1)S(1)}, bf16[448,1024]{1,0:T(8,128)(2,1)S(1)}, f32[256,1024]{1,0:T(8,128)S(1)}, bf16[256,1024]{1,0:T(8,128)(2,1)S(1)}, bf16[64,1024]{1,0:T(8,128)(2,1)S(1)}) custom-call(bf16[448,256]{1,0:T(8,128)(2,1)S(1)} %get-tuple-element.44.saved, bf16[1568,256]{1,0:T(8,128)(2,1)S(1)} %copy-done, ...), custom_call_target="tpu_custom_call" | custom-call | flops 704643072 | bytes 8568832 | tf_op jit(solution)/shard_map/pallas_call | solution.py:86
  31.6 3.3 %collective-permute-start.14 = (bf16[256,1024]{1,0:T(8,128)(2,1)S(1)}, bf16[256,1024]{1,0:T(8,128)(2,1)S(1)}, u32[]{:S(2)}, u32[]{:S(2)}) collective-permute-start(bf16[256,1024]{1,0:T(8,128)(2,1)S(1)} %get-tuple-element.53), channel_id=1, source_target_pairs={{0,1},{1,0},{2,3},{3,2},{4,5},{5,4},{6,7},{7,6},{8,9},{9,8},{10,11... | collective-permute-start | bytes 1572872 | tf_op jit(solution)/shard_map/ppermute | solution.py:23
  34.9 1.1 %collective-permute-done.2.refs_2_ = bf16[98,1024]{1,0:T(8,128)(2,1)S(1)} collective-permute-done((bf16[98,1024]{1,0:T(8,128)(2,1)S(1)}, bf16[98,1024]{1,0:T(8,128)(2,1)S(1)}, u32[]{:S(2)}, u32[]{:S(2)}) %collective-permute-start.2) | collective-permute-done | bytes 200736 | tf_op jit(solution)/shard_map/ppermute | solution.py:38
  36.0 0.5 collective-permute-start.3
  36.6 1.6 %collective-permute-start.16 = (bf16[64,1024]{1,0:T(8,128)(2,1)S(1)}, bf16[64,1024]{1,0:T(8,128)(2,1)S(1)}, u32[]{:S(2)}, u32[]{:S(2)}) collective-permute-start(bf16[64,1024]{1,0:T(8,128)(2,1)S(1)} %get-tuple-element.57), channel_id=1, source_target_pairs={{0,1},{1,0},{2,3},{3,2},{4,5},{5,4},{6,7},{7,6},{8,9},{9,8},{10,11... | collective-permute-start | bytes 393224 | tf_op jit(solution)/shard_map/ppermute | solution.py:23
  38.2 3.1 %collective-permute-done.3.refs_3_ = bf16[98,1024]{1,0:T(8,128)(2,1)S(1)} collective-permute-done((bf16[98,1024]{1,0:T(8,128)(2,1)S(1)}, bf16[98,1024]{1,0:T(8,128)(2,1)S(1)}, u32[]{:S(2)}, u32[]{:S(2)}) %collective-permute-start.3) | collective-permute-done | bytes 200736 | tf_op jit(solution)/shard_map/ppermute | solution.py:38
  41.3 0.2 shard_map.156.refs_4_
  41.5 2.5 %collective-permute-start.4 = (f32[2,1024]{1,0:T(2,128)S(1)}, f32[2,1024]{1,0:T(2,128)S(1)}, u32[]{:S(2)}, u32[]{:S(2)}) collective-permute-start(f32[2,1024]{1,0:T(2,128)S(1)} %shard_map.156.refs_4_), channel_id=1, source_target_pairs={{0,1},{1,0},{2,3},{3,2},{4,5},{5,4},{6,7},{7,6},{8,9},{9,8},{10,11... | collective-permute-start | bytes 24584 | tf_op jit(solution)/shard_map/ppermute | solution.py:23
  44.1 0.6 collective-permute-start.17
  44.7 0.0 copy-start.2
  44.7 0.2 collective-permute-done.4.refs_5_
  44.8 0.3 collective-permute-start.7
  45.2 2.4 %shard_map.157 = (f32[448,1024]{1,0:T(8,128)S(1)}, f32[2,1024]{1,0:T(2,128)S(1)}, f32[2,1024]{1,0:T(2,128)S(1)}) custom-call(bf16[98,1024]{1,0:T(8,128)(2,1)S(1)} %broadcast_select_fusion.refs_0_.rows, bf16[98,1024]{1,0:T(8,128)(2,1)S(1)} %collective-permute-done.1.refs_1_, bf16[98,1024]{1,0:T(8,128)(2,1)S(1)} %collective-permute-done.2.refs_2_, ...), custom_call_target="tpu_custom_call" | custom-call | flops 939524096 | bytes 4775936 | tf_op jit(solution)/shard_map/pallas_call | solution.py:86
  47.6 0.2 collective-permute-start.6
  47.8 0.1 shard_map.165
  47.9 1.2 %collective-permute-done.17 = bf16[64,1024]{1,0:T(8,128)(2,1)S(1)} collective-permute-done((bf16[64,1024]{1,0:T(8,128)(2,1)S(1)}, bf16[64,1024]{1,0:T(8,128)(2,1)S(1)}, u32[]{:S(2)}, u32[]{:S(2)}) %collective-permute-start.17) | collective-permute-done | bytes 131104 | tf_op jit(solution)/shard_map/ppermute | solution.py:38
  49.2 2.2 %collective-permute-start.18 = (bf16[64,1024]{1,0:T(8,128)(2,1)S(1)}, bf16[64,1024]{1,0:T(8,128)(2,1)S(1)}, u32[]{:S(2)}, u32[]{:S(2)}) collective-permute-start(bf16[64,1024]{1,0:T(8,128)(2,1)S(1)} %add_convert_fusion.1), channel_id=1, source_target_pairs={{0,4},{1,5},{2,6},{3,7},{4,0},{5,1},{6,2},{7,3},{8,12},{9,13},{10,... | collective-permute-start | bytes 393224 | tf_op jit(solution)/shard_map/ppermute | solution.py:38
  51.4 1.5 %collective-permute-start.15 = (bf16[64,1024]{1,0:T(8,128)(2,1)S(1)}, bf16[64,1024]{1,0:T(8,128)(2,1)S(1)}, u32[]{:S(2)}, u32[]{:S(2)}) collective-permute-start(bf16[64,1024]{1,0:T(8,128)(2,1)S(1)} %get-tuple-element.55), channel_id=1, source_target_pairs={{0,2},{1,3},{2,0},{3,1},{4,6},{5,7},{6,4},{7,5},{8,10},{9,11},{10,... | collective-permute-start | bytes 393224 | tf_op jit(solution)/shard_map/ppermute | solution.py:38
  52.9 0.0 collective-permute-done.7.two
  52.9 0.0 copy-start.6
  52.9 1.1 %shard_map.158 = (f32[98,1024]{1,0:T(8,128)S(1)}, bf16[98,1024]{1,0:T(8,128)(2,1)S(1)}, f32[98,1024]{1,0:T(8,128)S(1)}, bf16[98,1024]{1,0:T(8,128)(2,1)S(1)}) custom-call(f32[448,1024]{1,0:T(8,128)S(1)} %get-tuple-element.32.inner, f32[2,1024]{1,0:T(2,128)S(1)} %get-tuple-element.33.sums, f32[2,1024]{1,0:T(2,128)S(1)} %collective-permute-done.6.got, ...), custom_call_target="tpu_custom_call" | custom-call | flops 939524096 | bytes 5361664 | tf_op jit(solution)/shard_map/pallas_call | solution.py:86
  54.1 0.1 collective-permute-start.10
  54.2 2.9 %collective-permute-done.18.refs_1_ = bf16[64,1024]{1,0:T(8,128)(2,1)S(1)} collective-permute-done((bf16[64,1024]{1,0:T(8,128)(2,1)S(1)}, bf16[64,1024]{1,0:T(8,128)(2,1)S(1)}, u32[]{:S(2)}, u32[]{:S(2)}) %collective-permute-start.18) | collective-permute-done | bytes 131104 | tf_op jit(solution)/shard_map/ppermute | solution.py:38
  57.0 0.1 shard_map.167.refs_0_
  57.1 1.8 %collective-permute-start.20 = (bf16[64,1024]{1,0:T(8,128)(2,1)S(1)}, bf16[64,1024]{1,0:T(8,128)(2,1)S(1)}, u32[]{:S(2)}, u32[]{:S(2)}) collective-permute-start(bf16[64,1024]{1,0:T(8,128)(2,1)S(1)} %shard_map.167.refs_0_), channel_id=1, source_target_pairs={{0,4},{1,5},{2,6},{3,7},{4,0},{5,1},{6,2},{7,3},{8,12},{9,13},{10,... | collective-permute-start | bytes 393224 | tf_op jit(solution)/shard_map/ppermute | solution.py:38
  58.9 3.0 %collective-permute-start.9 = (bf16[98,1024]{1,0:T(8,128)(2,1)S(1)}, bf16[98,1024]{1,0:T(8,128)(2,1)S(1)}, u32[]{:S(2)}, u32[]{:S(2)}) collective-permute-start(bf16[98,1024]{1,0:T(8,128)(2,1)S(1)} %get-tuple-element.36), channel_id=1, source_target_pairs={{0,2},{1,3},{2,0},{3,1},{4,6},{5,7},{6,4},{7,5},{8,10},{9,11},{10,... | collective-permute-start | bytes 602120 | tf_op jit(solution)/shard_map/ppermute | solution.py:38
  61.9 0.0 collective-permute-start.19
  61.9 1.7 %collective-permute-done.20.refs_2_ = bf16[64,1024]{1,0:T(8,128)(2,1)S(1)} collective-permute-done((bf16[64,1024]{1,0:T(8,128)(2,1)S(1)}, bf16[64,1024]{1,0:T(8,128)(2,1)S(1)}, u32[]{:S(2)}, u32[]{:S(2)}) %collective-permute-start.20) | collective-permute-done | bytes 131104 | tf_op jit(solution)/shard_map/ppermute | solution.py:38
  63.6 2.4 %collective-permute-start.21 = (bf16[64,1024]{1,0:T(8,128)(2,1)S(1)}, bf16[64,1024]{1,0:T(8,128)(2,1)S(1)}, u32[]{:S(2)}, u32[]{:S(2)}) collective-permute-start(bf16[64,1024]{1,0:T(8,128)(2,1)S(1)} %collective-permute-done.20.refs_2_), channel_id=1, source_target_pairs={{0,2},{1,3},{2,0},{3,1},{4,6},{5,7},{6,4},{7,5},{8,10},{9,11},{10,... | collective-permute-start | bytes 393224 | tf_op jit(solution)/shard_map/ppermute | solution.py:38
  66.0 0.1 add_convert_fusion
  66.1 3.7 %collective-permute-start.11 = (bf16[98,1024]{1,0:T(8,128)(2,1)S(1)}, bf16[98,1024]{1,0:T(8,128)(2,1)S(1)}, u32[]{:S(2)}, u32[]{:S(2)}) collective-permute-start(bf16[98,1024]{1,0:T(8,128)(2,1)S(1)} %add_convert_fusion), channel_id=1, source_target_pairs={{0,4},{1,5},{2,6},{3,7},{4,0},{5,1},{6,2},{7,3},{8,12},{9,13},{10,... | collective-permute-start | bytes 602120 | tf_op jit(solution)/shard_map/ppermute | solution.py:38
  69.7 2.3 %collective-permute-start.22 = (bf16[64,1024]{1,0:T(8,128)(2,1)S(1)}, bf16[64,1024]{1,0:T(8,128)(2,1)S(1)}, u32[]{:S(2)}, u32[]{:S(2)}) collective-permute-start(bf16[64,1024]{1,0:T(8,128)(2,1)S(1)} %shard_map.167.refs_0_), channel_id=1, source_target_pairs={{0,1},{1,0},{2,3},{3,2},{4,5},{5,4},{6,7},{7,6},{8,9},{9,8},{10,11... | collective-permute-start | bytes 393224 | tf_op jit(solution)/shard_map/ppermute | solution.py:23
  72.0 0.0 collective-permute-done.9.refs_0_
  72.0 4.6 %collective-permute-start.24 = (bf16[64,1024]{1,0:T(8,128)(2,1)S(1)}, bf16[64,1024]{1,0:T(8,128)(2,1)S(1)}, u32[]{:S(2)}, u32[]{:S(2)}) collective-permute-start(bf16[64,1024]{1,0:T(8,128)(2,1)S(1)} %collective-permute-done.20.refs_2_), channel_id=1, source_target_pairs={{0,1},{1,0},{2,3},{3,2},{4,5},{5,4},{6,7},{7,6},{8,9},{9,8},{10,11... | collective-permute-start | bytes 393224 | tf_op jit(solution)/shard_map/ppermute | solution.py:23
  76.6 0.8 collective-permute-done.19.refs_1_
  77.3 2.1 %collective-permute-start.23 = (bf16[64,1024]{1,0:T(8,128)(2,1)S(1)}, bf16[64,1024]{1,0:T(8,128)(2,1)S(1)}, u32[]{:S(2)}, u32[]{:S(2)}) collective-permute-start(bf16[64,1024]{1,0:T(8,128)(2,1)S(1)} %collective-permute-done.19.refs_1_), channel_id=1, source_target_pairs={{0,1},{1,0},{2,3},{3,2},{4,5},{5,4},{6,7},{7,6},{8,9},{9,8},{10,11... | collective-permute-start | bytes 393224 | tf_op jit(solution)/shard_map/ppermute | solution.py:23
  79.4 0.8 collective-permute-done.21.refs_3_
  80.2 1.2 %collective-permute-start.25 = (bf16[64,1024]{1,0:T(8,128)(2,1)S(1)}, bf16[64,1024]{1,0:T(8,128)(2,1)S(1)}, u32[]{:S(2)}, u32[]{:S(2)}) collective-permute-start(bf16[64,1024]{1,0:T(8,128)(2,1)S(1)} %collective-permute-done.21.refs_3_), channel_id=1, source_target_pairs={{0,1},{1,0},{2,3},{3,2},{4,5},{5,4},{6,7},{7,6},{8,9},{9,8},{10,11... | collective-permute-start | bytes 393224 | tf_op jit(solution)/shard_map/ppermute | solution.py:23
  81.4 2.3 %shard_map.164 = bf16[1568,256]{1,0:T(8,128)(2,1)} custom-call(bf16[256,1024]{1,0:T(8,128)(2,1)S(1)} %bitcast.19, bf16[1120,256]{1,0:T(8,128)(2,1)S(1)} %get-tuple-element.42.refs_0_, bf16[1120,1024]{1,0:T(8,128)(2,1)S(1)} %get-tuple-element.43.refs_1_, bf16[448,256]{1,0:T(8,128)(2,1)S(1)} %get-tuple-element.50.refs_2_, ...), custom_call_target="tpu_custom_call" | custom-call | flops 822083584 | bytes 5341184 | tf_op jit(solution)/shard_map/pallas_call | solution.py:86
  83.7 0.7 shard_map.159
  84.5 0.0 collective-permute-done.22.refs_4_
  84.5 0.0 collective-permute-done.25.refs_7_
  84.5 2.0 %shard_map.168 = (f32[256,1024]{1,0:T(8,128)}, f32[1024,256]{1,0:T(8,128)}) custom-call(bf16[64,1024]{1,0:T(8,128)(2,1)S(1)} %shard_map.167.refs_0_, bf16[64,1024]{1,0:T(8,128)(2,1)S(1)} %collective-permute-done.19.refs_1_, bf16[64,1024]{1,0:T(8,128)(2,1)S(1)} %collective-permute-done.20.refs_2_, bf16[64,1024]{1,0:T(8,128)(2,1)S(1)} %collective-permute-done.21.refs_3_, ...), custom_call_target="tpu_custom_call" | custom-call | flops 3145728 | bytes 3145728 | tf_op jit(solution)/shard_map/pallas_call | solution.py:86
  (31 shorter events, 0.1 us)
Async XLA Ops:
  0.6 27.3 %copy-start.1 = (bf16[1,1024,256]{2,1,0:T(8,128)(2,1)S(1)}, bf16[1,1024,256]{2,1,0:T(8,128)(2,1)}, u32[]{:S(2)}) copy-start(bf16[1,1024,256]{2,1,0:T(8,128)(2,1)} %param.25) | copy-start | bytes 1572868
  0.6 27.3 %copy-start = (bf16[1568,256]{1,0:T(8,128)(2,1)S(1)}, bf16[1568,256]{1,0:T(8,128)(2,1)}, u32[]{:S(2)}) copy-start(bf16[1568,256]{1,0:T(8,128)(2,1)} %leaving.3) | copy-start | bytes 2408452
  0.7 1.2 %copy-start.4 = (bf16[1,1568,256]{2,1,0:T(8,128)(2,1)S(1)}, bf16[1,1568,256]{2,1,0:T(8,128)(2,1)}, u32[]{:S(2)}) copy-start(bf16[1,1568,256]{2,1,0:T(8,128)(2,1)} %param.22) | copy-start | bytes 2408452
  2.8 23.9 %collective-permute-start.12 = (bf16[1120,256]{1,0:T(8,128)(2,1)}, bf16[1120,256]{1,0:T(8,128)(2,1)S(1)}, u32[]{:S(2)}, u32[]{:S(2)}) collective-permute-start(bf16[1120,256]{1,0:T(8,128)(2,1)} %get-tuple-element.39), channel_id=1, source_target_pairs={{8,0},{16,8},{24,16},{9,1},{17,9},{25,17},{10,2},{18,10},{26,18},{... | collective-permute-start | bytes 1720328 | tf_op jit(solution)/shard_map/ppermute | solution.py:19
  5.8 17.5 %collective-permute-start = (bf16[98,1024]{1,0:T(8,128)(2,1)}, bf16[98,1024]{1,0:T(8,128)(2,1)}, u32[]{:S(2)}, u32[]{:S(2)}) collective-permute-start(bf16[98,1024]{1,0:T(8,128)(2,1)} %bitcast.26), channel_id=1, source_target_pairs={{0,8},{8,16},{16,24},{1,9},{9,17},{17,25},{2,10},{10,18},{18,26},{... | collective-permute-start | bytes 602120 | tf_op jit(solution)/shard_map/ppermute | solution.py:19
  8.1 37.1 %collective-permute-start.5 = (bf16[1024,512]{1,0:T(8,128)(2,1)}, bf16[1024,512]{1,0:T(8,128)(2,1)}, u32[]{:S(2)}, u32[]{:S(2)}) collective-permute-start(bf16[1024,512]{1,0:T(8,128)(2,1)} %bitcast.20), channel_id=1, source_target_pairs={{0,1},{1,0},{2,3},{3,2},{4,5},{5,4},{6,7},{7,6},{8,9},{9,8},{10,11... | collective-permute-start | bytes 3145736 | tf_op jit(solution)/shard_map/ppermute | solution.py:23
  9.4 21.1 %collective-permute-start.13 = (bf16[448,256]{1,0:T(8,128)(2,1)S(1)}, bf16[448,256]{1,0:T(8,128)(2,1)S(1)}, u32[]{:S(2)}, u32[]{:S(2)}) collective-permute-start(bf16[448,256]{1,0:T(8,128)(2,1)S(1)} %get-tuple-element.45), channel_id=1, source_target_pairs={{8,0},{16,8},{24,16},{9,1},{17,9},{25,17},{10,2},{18,10},{26,18},{... | collective-permute-start | bytes 688136 | tf_op jit(solution)/shard_map/ppermute | solution.py:19
  13.3 39.6 %collective-permute-start.8 = (bf16[512,1024]{1,0:T(8,128)(2,1)}, bf16[512,1024]{1,0:T(8,128)(2,1)S(1)}, u32[]{:S(2)}, u32[]{:S(2)}) collective-permute-start(bf16[512,1024]{1,0:T(8,128)(2,1)} %bitcast.13), channel_id=1, source_target_pairs={{0,1},{1,0},{2,3},{3,2},{4,5},{5,4},{6,7},{7,6},{8,9},{9,8},{10,11... | collective-permute-start | bytes 3145736 | tf_op jit(solution)/shard_map/ppermute | solution.py:23
  13.7 1.1 %copy-start.3 = (bf16[1,1568,256]{2,1,0:T(8,128)(2,1)S(1)}, bf16[1,1568,256]{2,1,0:T(8,128)(2,1)}, u32[]{:S(2)}) copy-start(bf16[1,1568,256]{2,1,0:T(8,128)(2,1)} %param.21) | copy-start | bytes 2408452
  14.8 1.0 %copy-start.5 = (bf16[1,256,1024]{2,1,0:T(8,128)(2,1)S(1)}, bf16[1,256,1024]{2,1,0:T(8,128)(2,1)}, u32[]{:S(2)}) copy-start(bf16[1,256,1024]{2,1,0:T(8,128)(2,1)} %param.24) | copy-start | bytes 1572868
  15.9 7.5 %copy-start.10 = (bf16[98,1024]{1,0:T(8,128)(2,1)S(1)}, bf16[98,1024]{1,0:T(8,128)(2,1)}, u32[]{:S(2)}) copy-start(bf16[98,1024]{1,0:T(8,128)(2,1)} %param.14) | copy-start | bytes 602116
  24.3 11.7 %collective-permute-start.2 = (bf16[98,1024]{1,0:T(8,128)(2,1)S(1)}, bf16[98,1024]{1,0:T(8,128)(2,1)S(1)}, u32[]{:S(2)}, u32[]{:S(2)}) collective-permute-start(bf16[98,1024]{1,0:T(8,128)(2,1)S(1)} %broadcast_select_fusion.refs_0_.rows), channel_id=1, source_target_pairs={{0,4},{1,5},{2,6},{3,7},{4,0},{5,1},{6,2},{7,3},{8,12},{9,13},{10,... | collective-permute-start | bytes 602120 | tf_op jit(solution)/shard_map/ppermute | solution.py:38
  26.7 9.9 %collective-permute-start.1 = (bf16[98,1024]{1,0:T(8,128)(2,1)S(1)}, bf16[98,1024]{1,0:T(8,128)(2,1)S(1)}, u32[]{:S(2)}, u32[]{:S(2)}) collective-permute-start(bf16[98,1024]{1,0:T(8,128)(2,1)S(1)} %broadcast_select_fusion.refs_0_.rows), channel_id=1, source_target_pairs={{0,2},{1,3},{2,0},{3,1},{4,6},{5,7},{6,4},{7,5},{8,10},{9,11},{10,... | collective-permute-start | bytes 602120 | tf_op jit(solution)/shard_map/ppermute | solution.py:38
  30.5 14.1 %copy-start.11 = (f32[1,512]{1,0:T(1,128)S(1)}, f32[1,512]{1,0:T(1,128)}, u32[]{:S(2)}) copy-start(f32[1,512]{1,0:T(1,128)} %param.19) | copy-start | bytes 6148
  30.5 14.1 %copy-start.12 = (f32[1,512]{1,0:T(1,128)S(1)}, f32[1,512]{1,0:T(1,128)}, u32[]{:S(2)}) copy-start(f32[1,512]{1,0:T(1,128)} %param.18) | copy-start | bytes 6148
  30.6 14.6 %copy-start.7 = (bf16[1,1024,512]{2,1,0:T(8,128)(2,1)S(1)}, bf16[1,1024,512]{2,1,0:T(8,128)(2,1)}, u32[]{:S(2)}) copy-start(bf16[1,1024,512]{2,1,0:T(8,128)(2,1)} %param.17) | copy-start | bytes 3145732
  30.6 14.6 %copy-start.8 = (f32[1,1024]{1,0:T(1,128)S(1)}, f32[1,1024]{1,0:T(1,128)}, u32[]{:S(2)}) copy-start(f32[1,1024]{1,0:T(1,128)} %refs_6_.1) | copy-start | bytes 12292
  30.6 14.6 %copy-start.9 = (f32[1,1024]{1,0:T(1,128)S(1)}, f32[1,1024]{1,0:T(1,128)}, u32[]{:S(2)}) copy-start(f32[1,1024]{1,0:T(1,128)} %refs_7_.1) | copy-start | bytes 12292
  31.6 16.2 %collective-permute-start.14 = (bf16[256,1024]{1,0:T(8,128)(2,1)S(1)}, bf16[256,1024]{1,0:T(8,128)(2,1)S(1)}, u32[]{:S(2)}, u32[]{:S(2)}) collective-permute-start(bf16[256,1024]{1,0:T(8,128)(2,1)S(1)} %get-tuple-element.53), channel_id=1, source_target_pairs={{0,1},{1,0},{2,3},{3,2},{4,5},{5,4},{6,7},{7,6},{8,9},{9,8},{10,11... | collective-permute-start | bytes 1572872 | tf_op jit(solution)/shard_map/ppermute | solution.py:23
  36.0 5.2 %collective-permute-start.3 = (bf16[98,1024]{1,0:T(8,128)(2,1)S(1)}, bf16[98,1024]{1,0:T(8,128)(2,1)S(1)}, u32[]{:S(2)}, u32[]{:S(2)}) collective-permute-start(bf16[98,1024]{1,0:T(8,128)(2,1)S(1)} %collective-permute-done.2.refs_2_), channel_id=1, source_target_pairs={{0,2},{1,3},{2,0},{3,1},{4,6},{5,7},{6,4},{7,5},{8,10},{9,11},{10,... | collective-permute-start | bytes 602120 | tf_op jit(solution)/shard_map/ppermute | solution.py:38
  36.6 7.4 %collective-permute-start.16 = (bf16[64,1024]{1,0:T(8,128)(2,1)S(1)}, bf16[64,1024]{1,0:T(8,128)(2,1)S(1)}, u32[]{:S(2)}, u32[]{:S(2)}) collective-permute-start(bf16[64,1024]{1,0:T(8,128)(2,1)S(1)} %get-tuple-element.57), channel_id=1, source_target_pairs={{0,1},{1,0},{2,3},{3,2},{4,5},{5,4},{6,7},{7,6},{8,9},{9,8},{10,11... | collective-permute-start | bytes 393224 | tf_op jit(solution)/shard_map/ppermute | solution.py:23
  41.5 3.3 %collective-permute-start.4 = (f32[2,1024]{1,0:T(2,128)S(1)}, f32[2,1024]{1,0:T(2,128)S(1)}, u32[]{:S(2)}, u32[]{:S(2)}) collective-permute-start(f32[2,1024]{1,0:T(2,128)S(1)} %shard_map.156.refs_4_), channel_id=1, source_target_pairs={{0,1},{1,0},{2,3},{3,2},{4,5},{5,4},{6,7},{7,6},{8,9},{9,8},{10,11... | collective-permute-start | bytes 24584 | tf_op jit(solution)/shard_map/ppermute | solution.py:23
  44.1 5.1 %collective-permute-start.17 = (bf16[64,1024]{1,0:T(8,128)(2,1)S(1)}, bf16[64,1024]{1,0:T(8,128)(2,1)S(1)}, u32[]{:S(2)}, u32[]{:S(2)}) collective-permute-start(bf16[64,1024]{1,0:T(8,128)(2,1)S(1)} %shard_map.166), channel_id=1, source_target_pairs={{0,2},{1,3},{2,0},{3,1},{4,6},{5,7},{6,4},{7,5},{8,10},{9,11},{10,... | collective-permute-start | bytes 393224 | tf_op jit(solution)/shard_map/ppermute | solution.py:38
  44.7 8.2 %copy-start.2 = (bf16[1,512,1024]{2,1,0:T(8,128)(2,1)S(1)}, bf16[1,512,1024]{2,1,0:T(8,128)(2,1)}, u32[]{:S(2)}) copy-start(bf16[1,512,1024]{2,1,0:T(8,128)(2,1)} %param.20) | copy-start | bytes 3145732
  44.8 8.0 %collective-permute-start.7 = (f32[2,512]{1,0:T(2,128)S(1)}, f32[2,512]{1,0:T(2,128)S(1)}, u32[]{:S(2)}, u32[]{:S(2)}) collective-permute-start(f32[2,512]{1,0:T(2,128)S(1)} %pad_maximum_fusion.one), channel_id=1, source_target_pairs={{0,1},{1,0},{2,3},{3,2},{4,5},{5,4},{6,7},{7,6},{8,9},{9,8},{10,11... | collective-permute-start | bytes 12296 | tf_op jit(solution)/shard_map/ppermute | solution.py:23
  47.6 5.3 %collective-permute-start.6 = (f32[2,1024]{1,0:T(2,128)S(1)}, f32[2,1024]{1,0:T(2,128)S(1)}, u32[]{:S(2)}, u32[]{:S(2)}) collective-permute-start(f32[2,1024]{1,0:T(2,128)S(1)} %get-tuple-element.34), channel_id=1, source_target_pairs={{0,1},{1,0},{2,3},{3,2},{4,5},{5,4},{6,7},{7,6},{8,9},{9,8},{10,11... | collective-permute-start | bytes 24584 | tf_op jit(solution)/shard_map/ppermute | solution.py:23
  49.2 7.8 %collective-permute-start.18 = (bf16[64,1024]{1,0:T(8,128)(2,1)S(1)}, bf16[64,1024]{1,0:T(8,128)(2,1)S(1)}, u32[]{:S(2)}, u32[]{:S(2)}) collective-permute-start(bf16[64,1024]{1,0:T(8,128)(2,1)S(1)} %add_convert_fusion.1), channel_id=1, source_target_pairs={{0,4},{1,5},{2,6},{3,7},{4,0},{5,1},{6,2},{7,3},{8,12},{9,13},{10,... | collective-permute-start | bytes 393224 | tf_op jit(solution)/shard_map/ppermute | solution.py:38
  51.4 5.6 %collective-permute-start.15 = (bf16[64,1024]{1,0:T(8,128)(2,1)S(1)}, bf16[64,1024]{1,0:T(8,128)(2,1)S(1)}, u32[]{:S(2)}, u32[]{:S(2)}) collective-permute-start(bf16[64,1024]{1,0:T(8,128)(2,1)S(1)} %get-tuple-element.55), channel_id=1, source_target_pairs={{0,2},{1,3},{2,0},{3,1},{4,6},{5,7},{6,4},{7,5},{8,10},{9,11},{10,... | collective-permute-start | bytes 393224 | tf_op jit(solution)/shard_map/ppermute | solution.py:38
  52.9 28.5 %copy-start.6 = (bf16[1,256,1024]{2,1,0:T(8,128)(2,1)S(1)}, bf16[1,256,1024]{2,1,0:T(8,128)(2,1)}, u32[]{:S(2)}) copy-start(bf16[1,256,1024]{2,1,0:T(8,128)(2,1)} %param.24) | copy-start | bytes 1572868
  54.1 11.9 %collective-permute-start.10 = (bf16[98,1024]{1,0:T(8,128)(2,1)S(1)}, bf16[98,1024]{1,0:T(8,128)(2,1)S(1)}, u32[]{:S(2)}, u32[]{:S(2)}) collective-permute-start(bf16[98,1024]{1,0:T(8,128)(2,1)S(1)} %get-tuple-element.38), channel_id=1, source_target_pairs={{0,2},{1,3},{2,0},{3,1},{4,6},{5,7},{6,4},{7,5},{8,10},{9,11},{10,... | collective-permute-start | bytes 602120 | tf_op jit(solution)/shard_map/ppermute | solution.py:38
  57.1 6.5 %collective-permute-start.20 = (bf16[64,1024]{1,0:T(8,128)(2,1)S(1)}, bf16[64,1024]{1,0:T(8,128)(2,1)S(1)}, u32[]{:S(2)}, u32[]{:S(2)}) collective-permute-start(bf16[64,1024]{1,0:T(8,128)(2,1)S(1)} %shard_map.167.refs_0_), channel_id=1, source_target_pairs={{0,4},{1,5},{2,6},{3,7},{4,0},{5,1},{6,2},{7,3},{8,12},{9,13},{10,... | collective-permute-start | bytes 393224 | tf_op jit(solution)/shard_map/ppermute | solution.py:38
  58.9 13.1 %collective-permute-start.9 = (bf16[98,1024]{1,0:T(8,128)(2,1)S(1)}, bf16[98,1024]{1,0:T(8,128)(2,1)S(1)}, u32[]{:S(2)}, u32[]{:S(2)}) collective-permute-start(bf16[98,1024]{1,0:T(8,128)(2,1)S(1)} %get-tuple-element.36), channel_id=1, source_target_pairs={{0,2},{1,3},{2,0},{3,1},{4,6},{5,7},{6,4},{7,5},{8,10},{9,11},{10,... | collective-permute-start | bytes 602120 | tf_op jit(solution)/shard_map/ppermute | solution.py:38
  61.9 15.4 %collective-permute-start.19 = (bf16[64,1024]{1,0:T(8,128)(2,1)S(1)}, bf16[64,1024]{1,0:T(8,128)(2,1)S(1)}, u32[]{:S(2)}, u32[]{:S(2)}) collective-permute-start(bf16[64,1024]{1,0:T(8,128)(2,1)S(1)} %shard_map.167.refs_0_), channel_id=1, source_target_pairs={{0,2},{1,3},{2,0},{3,1},{4,6},{5,7},{6,4},{7,5},{8,10},{9,11},{10,... | collective-permute-start | bytes 393224 | tf_op jit(solution)/shard_map/ppermute | solution.py:38
  63.6 16.6 %collective-permute-start.21 = (bf16[64,1024]{1,0:T(8,128)(2,1)S(1)}, bf16[64,1024]{1,0:T(8,128)(2,1)S(1)}, u32[]{:S(2)}, u32[]{:S(2)}) collective-permute-start(bf16[64,1024]{1,0:T(8,128)(2,1)S(1)} %collective-permute-done.20.refs_2_), channel_id=1, source_target_pairs={{0,2},{1,3},{2,0},{3,1},{4,6},{5,7},{6,4},{7,5},{8,10},{9,11},{10,... | collective-permute-start | bytes 393224 | tf_op jit(solution)/shard_map/ppermute | solution.py:38
  66.1 17.6 %collective-permute-start.11 = (bf16[98,1024]{1,0:T(8,128)(2,1)S(1)}, bf16[98,1024]{1,0:T(8,128)(2,1)S(1)}, u32[]{:S(2)}, u32[]{:S(2)}) collective-permute-start(bf16[98,1024]{1,0:T(8,128)(2,1)S(1)} %add_convert_fusion), channel_id=1, source_target_pairs={{0,4},{1,5},{2,6},{3,7},{4,0},{5,1},{6,2},{7,3},{8,12},{9,13},{10,... | collective-permute-start | bytes 602120 | tf_op jit(solution)/shard_map/ppermute | solution.py:38
  69.7 14.7 %collective-permute-start.22 = (bf16[64,1024]{1,0:T(8,128)(2,1)S(1)}, bf16[64,1024]{1,0:T(8,128)(2,1)S(1)}, u32[]{:S(2)}, u32[]{:S(2)}) collective-permute-start(bf16[64,1024]{1,0:T(8,128)(2,1)S(1)} %shard_map.167.refs_0_), channel_id=1, source_target_pairs={{0,1},{1,0},{2,3},{3,2},{4,5},{5,4},{6,7},{7,6},{8,9},{9,8},{10,11... | collective-permute-start | bytes 393224 | tf_op jit(solution)/shard_map/ppermute | solution.py:23
  72.0 12.5 %collective-permute-start.24 = (bf16[64,1024]{1,0:T(8,128)(2,1)S(1)}, bf16[64,1024]{1,0:T(8,128)(2,1)S(1)}, u32[]{:S(2)}, u32[]{:S(2)}) collective-permute-start(bf16[64,1024]{1,0:T(8,128)(2,1)S(1)} %collective-permute-done.20.refs_2_), channel_id=1, source_target_pairs={{0,1},{1,0},{2,3},{3,2},{4,5},{5,4},{6,7},{7,6},{8,9},{9,8},{10,11... | collective-permute-start | bytes 393224 | tf_op jit(solution)/shard_map/ppermute | solution.py:23
  77.3 7.1 %collective-permute-start.23 = (bf16[64,1024]{1,0:T(8,128)(2,1)S(1)}, bf16[64,1024]{1,0:T(8,128)(2,1)S(1)}, u32[]{:S(2)}, u32[]{:S(2)}) collective-permute-start(bf16[64,1024]{1,0:T(8,128)(2,1)S(1)} %collective-permute-done.19.refs_1_), channel_id=1, source_target_pairs={{0,1},{1,0},{2,3},{3,2},{4,5},{5,4},{6,7},{7,6},{8,9},{9,8},{10,11... | collective-permute-start | bytes 393224 | tf_op jit(solution)/shard_map/ppermute | solution.py:23
  80.2 4.3 %collective-permute-start.25 = (bf16[64,1024]{1,0:T(8,128)(2,1)S(1)}, bf16[64,1024]{1,0:T(8,128)(2,1)S(1)}, u32[]{:S(2)}, u32[]{:S(2)}) collective-permute-start(bf16[64,1024]{1,0:T(8,128)(2,1)S(1)} %collective-permute-done.21.refs_3_), channel_id=1, source_target_pairs={{0,1},{1,0},{2,3},{3,2},{4,5},{5,4},{6,7},{7,6},{8,9},{9,8},{10,11... | collective-permute-start | bytes 393224 | tf_op jit(solution)/shard_map/ppermute | solution.py:23

commit v5 on v4

--- a/solution.py
+++ b/solution.py
@@ -105,15 +105,6 @@
     return fitting[-1] if fitting else extent
 
 
-def tiles(extent, tile):
-    def each(body):
-        @pl.loop(0, extent // tile)
-        def _(index):
-            body(pl.ds(pl.multiple_of(index * tile, tile), tile))
-
-    return each
-
-
 def affine(sums, squares, count, gain, shift):
     average = sums / count
     second = squares / count
@@ -232,20 +223,47 @@
 
 def assemble_kernel(count, *refs):
     mine, theirs = refs[:count], refs[count : 2 * count]
-    expand, reduce, held = refs[2 * count :]
-    chip = lax.div(lax.axis_index("dev"), 2)
+    expand, reduce, one_held, two_held, turned, done = refs[2 * count :]
     first_core = lax.rem(lax.axis_index("dev"), 2) == 0
-    extent = mine[0].shape[0]
     for step in range(count):
-        index = partner(chip, step, count) if step else chip
-        rows = pl.ds(pl.multiple_of(index * extent, extent), extent)
-        one, two = mine[step][...].astype(f32), theirs[step][...].astype(f32)
-        expand[rows, :] = jnp.where(first_core, one, two)
-        held[rows, :] = jnp.where(first_core, two, one)
-
-    @tiles(held.shape[1], tile_of(held.shape[1], 256, 128))
-    def _(columns):
-        reduce[columns, :] = held[:, columns].T
+        here = rows_of(step, count, mine[step].shape[0])
+        one, two = mine[step][...], theirs[step][...]
+        one_held[here, :] = jnp.where(first_core, one, two).astype(f32)
+        two_held[here, :] = jnp.where(first_core, two, one)
+    copies = [pltpu.make_async_copy(one_held, expand, done.at[0])]
+    copies[0].start()
+    columns = reduce.shape[0]
+    extent = columns // (done.shape[0] - 1)
+    for index in range(columns // extent):
+        here = slice(index * extent, (index + 1) * extent)
+        turned[here, :] = two_held[:, here].T.astype(f32)
+        copies.append(
+            pltpu.make_async_copy(turned.at[here, :], reduce.at[here, :], done.at[index + 1])
+        )
+        copies[-1].start()
+    for copy in copies:
+        copy.wait()
+
+
+def assemble(count, pieces, dims):
+    rows, columns = dims
+    extent = tile_of(columns, 256, 128)
+    moved = 8 * rows * columns
+    return pl.pallas_call(
+        functools.partial(assemble_kernel, count),
+        name="assemble",
+        out_shape=[shape((rows, columns), f32), shape((columns, rows), f32)],
+        in_specs=[pl.BlockSpec(memory_space=pltpu.VMEM)] * len(pieces),
+        out_specs=[pl.BlockSpec(memory_space=pl.ANY)] * 2,
+        scratch_shapes=[
+            pltpu.VMEM((rows, columns), f32),
+            pltpu.VMEM((rows, columns), bf16),
+            pltpu.VMEM((columns, rows), f32),
+            pltpu.SemaphoreType.DMA((1 + columns // extent,)),
+        ],
+        compiler_params=pltpu.CompilerParams(vmem_limit_bytes=24 * 2**20),
+        cost_estimate=pl.CostEstimate(flops=moved, bytes_accessed=moved, transcendentals=0),
+    )(*pieces)
 
 
 def late_sums_kernel(*refs):
@@ -459,11 +477,10 @@
         [expand_early[0], *grads],
         pixels * work,
     )
-    grad_expand, grad_reduce = whole_arrays(
-        functools.partial(assemble_kernel, count),
-        [shape((narrow, wide), f32), shape((wide, narrow), f32)],
+    grad_expand, grad_reduce = assemble(
+        count,
         [gathered[step] for step in range(count)] + [theirs[step] for step in range(count)],
-        scratch=[pltpu.VMEM((narrow, wide), f32)],
+        (narrow, wide),
     )
     (late_out,) = whole_arrays(
         late_total_kernel, [shape((rows, channels), bf16)], [own_late] + late_terms

time: 86.8 us -> 86.3 us (level)
    pallas_call x13 -> x12, Pallas kernels: 16.5 us -> 14.6 us  [whole_arrays(): pl.pallas_call(body, out_shape=list(outs), in_specs=[pl.BlockSpec(memory_...]
    pallas_call x0 -> x1, Pallas kernels: none -> 1.52 us  [assemble(): pl.pallas_call(functools.partial(assemble_kernel, count), name='assemble'...]
where the time goes in v5:
time: 86.3 us; the launch traced here: 86 us
  starting transfers between devices  48.4 us (56%)
  Pallas kernels  16.1 us (19%)
  waiting for transfers between devices  16.1 us (19%)
  local copies, waits for them, and re-layouts  3.47 us (4%)
  other arithmetic  1.05 us (1%)
  between operations  0.88 us (1%)
    ppermute x11, starting transfers between devices, swap(): lax.ppermute(x, 'dev', [(i, i ^ 1) for i in range(lax.axis_size('dev'))])  19.8 us
    ppermute x12, starting transfers between devices, across(): return lax.ppermute(x, 'dev', pairs)  19.5 us
    pallas_call x12, Pallas kernels, whole_arrays(): pl.pallas_call(body, out_shape=list(outs), in_specs=[pl.BlockSpec(memory_...  14.6 us
    ppermute x12, waiting for transfers between devices, across(): return lax.ppermute(x, 'dev', pairs)  11.5 us
    ppermute x3, starting transfers between devices, from_behind(): return lax.ppermute(x, axis, pairs)  9.22 us
    ppermute x3, waiting for transfers between devices, from_behind(): return lax.ppermute(x, axis, pairs)  4.35 us
    unnamed x26, local copies, waits for them, and re-layouts  3.47 us
  transfers between devices with their start and end apart: 26, of which 9 were waited for; matrix products, arithmetic and copies ran while one was open for 1% of the time, Pallas kernels for 16%

profile of v5, /device:TPU:5, one launch (start us, length us, event | category | flops | bytes accessed | tf_op | source)
XLA Modules:
  0.0 86.0 jit_solution(16299708545927160370)
XLA Ops:
  0.7 1.2 %copy-done.4 = bf16[1,1568,256]{2,1,0:T(8,128)(2,1)S(1)} copy-done((bf16[1,1568,256]{2,1,0:T(8,128)(2,1)S(1)}, bf16[1,1568,256]{2,1,0:T(8,128)(2,1)}, u32[]{:S(2)}) %copy-start.4) | copy-done | bytes 802840
  1.9 0.9 %shard_map.160 = (bf16[1120,256]{1,0:T(8,128)(2,1)}, bf16[448,256]{1,0:T(8,128)(2,1)S(1)}) custom-call(bf16[1568,256]{1,0:T(8,128)(2,1)S(1)} %bitcast.17), custom_call_target="tpu_custom_call" | custom-call | flops 1605632 | bytes 1605632 | tf_op jit(solution)/shard_map/pallas_call | solution.py:86
  2.8 3.0 %collective-permute-start.12 = (bf16[1120,256]{1,0:T(8,128)(2,1)}, bf16[1120,256]{1,0:T(8,128)(2,1)S(1)}, u32[]{:S(2)}, u32[]{:S(2)}) collective-permute-start(bf16[1120,256]{1,0:T(8,128)(2,1)} %get-tuple-element.39), channel_id=1, source_target_pairs={{8,0},{16,8},{24,16},{9,1},{17,9},{25,17},{10,2},{18,10},{26,18},{... | collective-permute-start | bytes 1720328 | tf_op jit(solution)/shard_map/ppermute | solution.py:19
  5.8 2.3 %collective-permute-start = (bf16[98,1024]{1,0:T(8,128)(2,1)}, bf16[98,1024]{1,0:T(8,128)(2,1)}, u32[]{:S(2)}, u32[]{:S(2)}) collective-permute-start(bf16[98,1024]{1,0:T(8,128)(2,1)} %bitcast.26), channel_id=1, source_target_pairs={{0,8},{8,16},{16,24},{1,9},{9,17},{17,25},{2,10},{10,18},{18,26},{... | collective-permute-start | bytes 602120 | tf_op jit(solution)/shard_map/ppermute | solution.py:19
  8.1 1.3 %collective-permute-start.5 = (bf16[1024,512]{1,0:T(8,128)(2,1)}, bf16[1024,512]{1,0:T(8,128)(2,1)}, u32[]{:S(2)}, u32[]{:S(2)}) collective-permute-start(bf16[1024,512]{1,0:T(8,128)(2,1)} %bitcast.20), channel_id=1, source_target_pairs={{0,1},{1,0},{2,3},{3,2},{4,5},{5,4},{6,7},{7,6},{8,9},{9,8},{10,11... | collective-permute-start | bytes 3145736 | tf_op jit(solution)/shard_map/ppermute | solution.py:23
  9.4 3.9 %collective-permute-start.13 = (bf16[448,256]{1,0:T(8,128)(2,1)S(1)}, bf16[448,256]{1,0:T(8,128)(2,1)S(1)}, u32[]{:S(2)}, u32[]{:S(2)}) collective-permute-start(bf16[448,256]{1,0:T(8,128)(2,1)S(1)} %get-tuple-element.45), channel_id=1, source_target_pairs={{8,0},{16,8},{24,16},{9,1},{17,9},{25,17},{10,2},{18,10},{26,18},{... | collective-permute-start | bytes 688136 | tf_op jit(solution)/shard_map/ppermute | solution.py:19
  13.3 0.4 collective-permute-start.8
  13.7 1.1 %copy-done.3 = bf16[1,1568,256]{2,1,0:T(8,128)(2,1)S(1)} copy-done((bf16[1,1568,256]{2,1,0:T(8,128)(2,1)S(1)}, bf16[1,1568,256]{2,1,0:T(8,128)(2,1)}, u32[]{:S(2)}) %copy-start.3) | copy-done | bytes 802840
  14.8 1.0 %copy-done.5 = bf16[1,256,1024]{2,1,0:T(8,128)(2,1)S(1)} copy-done((bf16[1,256,1024]{2,1,0:T(8,128)(2,1)S(1)}, bf16[1,256,1024]{2,1,0:T(8,128)(2,1)}, u32[]{:S(2)}) %copy-start.5) | copy-done | bytes 524312
  15.9 3.1 %shard_map.161 = (bf16[1120,1024]{1,0:T(8,128)(2,1)S(1)}, bf16[1120,1024]{1,0:T(8,128)(2,1)S(1)}, bf16[448,1024]{1,0:T(8,128)(2,1)S(1)}, bf16[448,1024]{1,0:T(8,128)(2,1)S(1)}, bf16[448,256]{1,0:T(8,128)(2,1)S(1)}) custom-call(bf16[1568,256]{1,0:T(8,128)(2,1)S(1)} %bitcast.15, bf16[256,1024]{1,0:T(8,128)(2,1)S(1)} %bitcast.18), custom_call_target="tpu_custom_call" | custom-call | flops 822083584 | bytes 7979008 | tf_op jit(solution)/shard_map/pallas_call | solution.py:86
  19.0 4.3 %collective-permute-done = bf16[98,1024]{1,0:T(8,128)(2,1)} collective-permute-done((bf16[98,1024]{1,0:T(8,128)(2,1)}, bf16[98,1024]{1,0:T(8,128)(2,1)}, u32[]{:S(2)}, u32[]{:S(2)}) %collective-permute-start) | collective-permute-done | bytes 200736 | tf_op jit(solution)/shard_map/ppermute | solution.py:19
  23.4 1.0 %broadcast_select_fusion.refs_0_.rows = bf16[98,1024]{1,0:T(8,128)(2,1)S(1)} fusion(bf16[98,1024]{1,0:T(8,128)(2,1)S(1)} %copy-done.10, bf16[98,1024]{1,0:T(8,128)(2,1)} %collective-permute-done, pred[]{:T(512)S(6)} %eq.3), kind=kLoop, calls=%fused_computation.2 | loop fusion | flops 100352 | bytes 602113 | tf_op jit(solution)/shard_map/jit(_where)/select_n | solution.py:383
  24.3 2.3 %collective-permute-start.2 = (bf16[98,1024]{1,0:T(8,128)(2,1)S(1)}, bf16[98,1024]{1,0:T(8,128)(2,1)S(1)}, u32[]{:S(2)}, u32[]{:S(2)}) collective-permute-start(bf16[98,1024]{1,0:T(8,128)(2,1)S(1)} %broadcast_select_fusion.refs_0_.rows), channel_id=1, source_target_pairs={{0,4},{1,5},{2,6},{3,7},{4,0},{5,1},{6,2},{7,3},{8,12},{9,13},{10,... | collective-permute-start | bytes 602120 | tf_op jit(solution)/shard_map/ppermute | solution.py:38
  26.7 1.3 %collective-permute-start.1 = (bf16[98,1024]{1,0:T(8,128)(2,1)S(1)}, bf16[98,1024]{1,0:T(8,128)(2,1)S(1)}, u32[]{:S(2)}, u32[]{:S(2)}) collective-permute-start(bf16[98,1024]{1,0:T(8,128)(2,1)S(1)} %broadcast_select_fusion.refs_0_.rows), channel_id=1, source_target_pairs={{0,2},{1,3},{2,0},{3,1},{4,6},{5,7},{6,4},{7,5},{8,10},{9,11},{10,... | collective-permute-start | bytes 602120 | tf_op jit(solution)/shard_map/ppermute | solution.py:38
  28.0 2.5 %shard_map.162 = (bf16[1120,256]{1,0:T(8,128)(2,1)S(1)}, bf16[1120,1024]{1,0:T(8,128)(2,1)S(1)}, f32[256,1024]{1,0:T(8,128)S(1)}, f32[256,1024]{1,0:T(8,128)S(1)}) custom-call(bf16[1568,256]{1,0:T(8,128)(2,1)S(1)} %bitcast.16, bf16[1568,256]{1,0:T(8,128)(2,1)S(1)} %copy-done, bf16[1120,256]{1,0:T(8,128)(2,1)S(1)} %collective-permute-done.12.arrived, ...), custom_call_target="tpu_custom_call" | custom-call | flops 1761607680 | bytes 12255232 | tf_op jit(solution)/shard_map/pallas_call | solution.py:86
  30.5 0.0 collective-permute-done.13.arrived
  30.5 0.0 copy-start.11
  30.5 0.0 copy-start.12
  30.6 0.0 copy-start.7
  30.6 0.0 copy-start.8
  30.6 0.0 copy-start.9
  30.6 1.0 %shard_map.163 = (bf16[448,256]{1,0:T(8,128)(2,1)S(1)}, bf16[448,1024]{1,0:T(8,128)(2,1)S(1)}, f32[256,1024]{1,0:T(8,128)S(1)}, bf16[256,1024]{1,0:T(8,128)(2,1)S(1)}, bf16[64,1024]{1,0:T(8,128)(2,1)S(1)}) custom-call(bf16[448,256]{1,0:T(8,128)(2,1)S(1)} %get-tuple-element.44.saved, bf16[1568,256]{1,0:T(8,128)(2,1)S(1)} %copy-done, ...), custom_call_target="tpu_custom_call" | custom-call | flops 704643072 | bytes 8568832 | tf_op jit(solution)/shard_map/pallas_call | solution.py:86
  31.6 3.3 %collective-permute-start.14 = (bf16[256,1024]{1,0:T(8,128)(2,1)S(1)}, bf16[256,1024]{1,0:T(8,128)(2,1)S(1)}, u32[]{:S(2)}, u32[]{:S(2)}) collective-permute-start(bf16[256,1024]{1,0:T(8,128)(2,1)S(1)} %get-tuple-element.53), channel_id=1, source_target_pairs={{0,1},{1,0},{2,3},{3,2},{4,5},{5,4},{6,7},{7,6},{8,9},{9,8},{10,11... | collective-permute-start | bytes 1572872 | tf_op jit(solution)/shard_map/ppermute | solution.py:23
  34.9 1.1 %collective-permute-done.2.refs_2_ = bf16[98,1024]{1,0:T(8,128)(2,1)S(1)} collective-permute-done((bf16[98,1024]{1,0:T(8,128)(2,1)S(1)}, bf16[98,1024]{1,0:T(8,128)(2,1)S(1)}, u32[]{:S(2)}, u32[]{:S(2)}) %collective-permute-start.2) | collective-permute-done | bytes 200736 | tf_op jit(solution)/shard_map/ppermute | solution.py:38
  36.0 0.5 collective-permute-start.3
  36.6 1.6 %collective-permute-start.16 = (bf16[64,1024]{1,0:T(8,128)(2,1)S(1)}, bf16[64,1024]{1,0:T(8,128)(2,1)S(1)}, u32[]{:S(2)}, u32[]{:S(2)}) collective-permute-start(bf16[64,1024]{1,0:T(8,128)(2,1)S(1)} %get-tuple-element.57), channel_id=1, source_target_pairs={{0,1},{1,0},{2,3},{3,2},{4,5},{5,4},{6,7},{7,6},{8,9},{9,8},{10,11... | collective-permute-start | bytes 393224 | tf_op jit(solution)/shard_map/ppermute | solution.py:23
  38.2 3.1 %collective-permute-done.3.refs_3_ = bf16[98,1024]{1,0:T(8,128)(2,1)S(1)} collective-permute-done((bf16[98,1024]{1,0:T(8,128)(2,1)S(1)}, bf16[98,1024]{1,0:T(8,128)(2,1)S(1)}, u32[]{:S(2)}, u32[]{:S(2)}) %collective-permute-start.3) | collective-permute-done | bytes 200736 | tf_op jit(solution)/shard_map/ppermute | solution.py:38
  41.3 0.2 shard_map.156.refs_4_
  41.5 2.5 %collective-permute-start.4 = (f32[2,1024]{1,0:T(2,128)S(1)}, f32[2,1024]{1,0:T(2,128)S(1)}, u32[]{:S(2)}, u32[]{:S(2)}) collective-permute-start(f32[2,1024]{1,0:T(2,128)S(1)} %shard_map.156.refs_4_), channel_id=1, source_target_pairs={{0,1},{1,0},{2,3},{3,2},{4,5},{5,4},{6,7},{7,6},{8,9},{9,8},{10,11... | collective-permute-start | bytes 24584 | tf_op jit(solution)/shard_map/ppermute | solution.py:23
  44.1 0.6 collective-permute-start.17
  44.7 0.0 copy-start.2
  44.7 0.2 collective-permute-done.4.refs_5_
  44.8 0.3 collective-permute-start.7
  45.2 2.4 %shard_map.157 = (f32[448,1024]{1,0:T(8,128)S(1)}, f32[2,1024]{1,0:T(2,128)S(1)}, f32[2,1024]{1,0:T(2,128)S(1)}) custom-call(bf16[98,1024]{1,0:T(8,128)(2,1)S(1)} %broadcast_select_fusion.refs_0_.rows, bf16[98,1024]{1,0:T(8,128)(2,1)S(1)} %collective-permute-done.1.refs_1_, bf16[98,1024]{1,0:T(8,128)(2,1)S(1)} %collective-permute-done.2.refs_2_, ...), custom_call_target="tpu_custom_call" | custom-call | flops 939524096 | bytes 4775936 | tf_op jit(solution)/shard_map/pallas_call | solution.py:86
  47.6 0.2 collective-permute-start.6
  47.8 0.1 shard_map.165
  47.9 1.2 %collective-permute-done.17 = bf16[64,1024]{1,0:T(8,128)(2,1)S(1)} collective-permute-done((bf16[64,1024]{1,0:T(8,128)(2,1)S(1)}, bf16[64,1024]{1,0:T(8,128)(2,1)S(1)}, u32[]{:S(2)}, u32[]{:S(2)}) %collective-permute-start.17) | collective-permute-done | bytes 131104 | tf_op jit(solution)/shard_map/ppermute | solution.py:38
  49.2 2.2 %collective-permute-start.18 = (bf16[64,1024]{1,0:T(8,128)(2,1)S(1)}, bf16[64,1024]{1,0:T(8,128)(2,1)S(1)}, u32[]{:S(2)}, u32[]{:S(2)}) collective-permute-start(bf16[64,1024]{1,0:T(8,128)(2,1)S(1)} %add_convert_fusion.1), channel_id=1, source_target_pairs={{0,4},{1,5},{2,6},{3,7},{4,0},{5,1},{6,2},{7,3},{8,12},{9,13},{10,... | collective-permute-start | bytes 393224 | tf_op jit(solution)/shard_map/ppermute | solution.py:38
  51.4 1.5 %collective-permute-start.15 = (bf16[64,1024]{1,0:T(8,128)(2,1)S(1)}, bf16[64,1024]{1,0:T(8,128)(2,1)S(1)}, u32[]{:S(2)}, u32[]{:S(2)}) collective-permute-start(bf16[64,1024]{1,0:T(8,128)(2,1)S(1)} %get-tuple-element.55), channel_id=1, source_target_pairs={{0,2},{1,3},{2,0},{3,1},{4,6},{5,7},{6,4},{7,5},{8,10},{9,11},{10,... | collective-permute-start | bytes 393224 | tf_op jit(solution)/shard_map/ppermute | solution.py:38
  52.9 0.0 collective-permute-done.7.two
  52.9 0.0 copy-start.6
  52.9 1.1 %shard_map.158 = (f32[98,1024]{1,0:T(8,128)S(1)}, bf16[98,1024]{1,0:T(8,128)(2,1)S(1)}, f32[98,1024]{1,0:T(8,128)S(1)}, bf16[98,1024]{1,0:T(8,128)(2,1)S(1)}) custom-call(f32[448,1024]{1,0:T(8,128)S(1)} %get-tuple-element.32.inner, f32[2,1024]{1,0:T(2,128)S(1)} %get-tuple-element.33.sums, f32[2,1024]{1,0:T(2,128)S(1)} %collective-permute-done.6.got, ...), custom_call_target="tpu_custom_call" | custom-call | flops 939524096 | bytes 5361664 | tf_op jit(solution)/shard_map/pallas_call | solution.py:86
  54.1 0.1 collective-permute-start.10
  54.2 2.9 %collective-permute-done.18.refs_1_ = bf16[64,1024]{1,0:T(8,128)(2,1)S(1)} collective-permute-done((bf16[64,1024]{1,0:T(8,128)(2,1)S(1)}, bf16[64,1024]{1,0:T(8,128)(2,1)S(1)}, u32[]{:S(2)}, u32[]{:S(2)}) %collective-permute-start.18) | collective-permute-done | bytes 131104 | tf_op jit(solution)/shard_map/ppermute | solution.py:38
  57.0 0.1 shard_map.167.refs_0_
  57.1 1.8 %collective-permute-start.20 = (bf16[64,1024]{1,0:T(8,128)(2,1)S(1)}, bf16[64,1024]{1,0:T(8,128)(2,1)S(1)}, u32[]{:S(2)}, u32[]{:S(2)}) collective-permute-start(bf16[64,1024]{1,0:T(8,128)(2,1)S(1)} %shard_map.167.refs_0_), channel_id=1, source_target_pairs={{0,4},{1,5},{2,6},{3,7},{4,0},{5,1},{6,2},{7,3},{8,12},{9,13},{10,... | collective-permute-start | bytes 393224 | tf_op jit(solution)/shard_map/ppermute | solution.py:38
  58.9 3.0 %collective-permute-start.9 = (bf16[98,1024]{1,0:T(8,128)(2,1)S(1)}, bf16[98,1024]{1,0:T(8,128)(2,1)S(1)}, u32[]{:S(2)}, u32[]{:S(2)}) collective-permute-start(bf16[98,1024]{1,0:T(8,128)(2,1)S(1)} %get-tuple-element.36), channel_id=1, source_target_pairs={{0,2},{1,3},{2,0},{3,1},{4,6},{5,7},{6,4},{7,5},{8,10},{9,11},{10,... | collective-permute-start | bytes 602120 | tf_op jit(solution)/shard_map/ppermute | solution.py:38
  61.9 0.0 collective-permute-start.19
  61.9 1.7 %collective-permute-done.20.refs_2_ = bf16[64,1024]{1,0:T(8,128)(2,1)S(1)} collective-permute-done((bf16[64,1024]{1,0:T(8,128)(2,1)S(1)}, bf16[64,1024]{1,0:T(8,128)(2,1)S(1)}, u32[]{:S(2)}, u32[]{:S(2)}) %collective-permute-start.20) | collective-permute-done | bytes 131104 | tf_op jit(solution)/shard_map/ppermute | solution.py:38
  63.6 2.4 %collective-permute-start.21 = (bf16[64,1024]{1,0:T(8,128)(2,1)S(1)}, bf16[64,1024]{1,0:T(8,128)(2,1)S(1)}, u32[]{:S(2)}, u32[]{:S(2)}) collective-permute-start(bf16[64,1024]{1,0:T(8,128)(2,1)S(1)} %collective-permute-done.20.refs_2_), channel_id=1, source_target_pairs={{0,2},{1,3},{2,0},{3,1},{4,6},{5,7},{6,4},{7,5},{8,10},{9,11},{10,... | collective-permute-start | bytes 393224 | tf_op jit(solution)/shard_map/ppermute | solution.py:38
  66.0 0.1 add_convert_fusion
  66.1 3.7 %collective-permute-start.11 = (bf16[98,1024]{1,0:T(8,128)(2,1)S(1)}, bf16[98,1024]{1,0:T(8,128)(2,1)S(1)}, u32[]{:S(2)}, u32[]{:S(2)}) collective-permute-start(bf16[98,1024]{1,0:T(8,128)(2,1)S(1)} %add_convert_fusion), channel_id=1, source_target_pairs={{0,4},{1,5},{2,6},{3,7},{4,0},{5,1},{6,2},{7,3},{8,12},{9,13},{10,... | collective-permute-start | bytes 602120 | tf_op jit(solution)/shard_map/ppermute | solution.py:38
  69.7 2.3 %collective-permute-start.22 = (bf16[64,1024]{1,0:T(8,128)(2,1)S(1)}, bf16[64,1024]{1,0:T(8,128)(2,1)S(1)}, u32[]{:S(2)}, u32[]{:S(2)}) collective-permute-start(bf16[64,1024]{1,0:T(8,128)(2,1)S(1)} %shard_map.167.refs_0_), channel_id=1, source_target_pairs={{0,1},{1,0},{2,3},{3,2},{4,5},{5,4},{6,7},{7,6},{8,9},{9,8},{10,11... | collective-permute-start | bytes 393224 | tf_op jit(solution)/shard_map/ppermute | solution.py:23
  72.0 0.0 collective-permute-done.9.refs_0_
  72.0 4.6 %collective-permute-start.24 = (bf16[64,1024]{1,0:T(8,128)(2,1)S(1)}, bf16[64,1024]{1,0:T(8,128)(2,1)S(1)}, u32[]{:S(2)}, u32[]{:S(2)}) collective-permute-start(bf16[64,1024]{1,0:T(8,128)(2,1)S(1)} %collective-permute-done.20.refs_2_), channel_id=1, source_target_pairs={{0,1},{1,0},{2,3},{3,2},{4,5},{5,4},{6,7},{7,6},{8,9},{9,8},{10,11... | collective-permute-start | bytes 393224 | tf_op jit(solution)/shard_map/ppermute | solution.py:23
  76.6 0.8 collective-permute-done.19.refs_1_
  77.3 2.1 %collective-permute-start.23 = (bf16[64,1024]{1,0:T(8,128)(2,1)S(1)}, bf16[64,1024]{1,0:T(8,128)(2,1)S(1)}, u32[]{:S(2)}, u32[]{:S(2)}) collective-permute-start(bf16[64,1024]{1,0:T(8,128)(2,1)S(1)} %collective-permute-done.19.refs_1_), channel_id=1, source_target_pairs={{0,1},{1,0},{2,3},{3,2},{4,5},{5,4},{6,7},{7,6},{8,9},{9,8},{10,11... | collective-permute-start | bytes 393224 | tf_op jit(solution)/shard_map/ppermute | solution.py:23
  79.4 0.8 collective-permute-done.21.refs_3_
  80.2 1.2 %collective-permute-start.25 = (bf16[64,1024]{1,0:T(8,128)(2,1)S(1)}, bf16[64,1024]{1,0:T(8,128)(2,1)S(1)}, u32[]{:S(2)}, u32[]{:S(2)}) collective-permute-start(bf16[64,1024]{1,0:T(8,128)(2,1)S(1)} %collective-permute-done.21.refs_3_), channel_id=1, source_target_pairs={{0,1},{1,0},{2,3},{3,2},{4,5},{5,4},{6,7},{7,6},{8,9},{9,8},{10,11... | collective-permute-start | bytes 393224 | tf_op jit(solution)/shard_map/ppermute | solution.py:23
  81.4 2.3 %shard_map.164 = bf16[1568,256]{1,0:T(8,128)(2,1)} custom-call(bf16[256,1024]{1,0:T(8,128)(2,1)S(1)} %bitcast.19, bf16[1120,256]{1,0:T(8,128)(2,1)S(1)} %get-tuple-element.42.refs_0_, bf16[1120,1024]{1,0:T(8,128)(2,1)S(1)} %get-tuple-element.43.refs_1_, bf16[448,256]{1,0:T(8,128)(2,1)S(1)} %get-tuple-element.50.refs_2_, ...), custom_call_target="tpu_custom_call" | custom-call | flops 822083584 | bytes 5341184 | tf_op jit(solution)/shard_map/pallas_call | solution.py:86
  83.7 0.7 shard_map.159
  84.5 0.0 collective-permute-done.22.refs_4_
  84.5 0.0 collective-permute-done.25.refs_7_
  84.5 1.5 %assemble.1 = (f32[256,1024]{1,0:T(8,128)}, f32[1024,256]{1,0:T(8,128)}) custom-call(bf16[64,1024]{1,0:T(8,128)(2,1)S(1)} %shard_map.167.refs_0_, bf16[64,1024]{1,0:T(8,128)(2,1)S(1)} %collective-permute-done.19.refs_1_, bf16[64,1024]{1,0:T(8,128)(2,1)S(1)} %collective-permute-done.20.refs_2_, bf16[64,1024]{1,0:T(8,128)(2,1)S(1)} %collective-permute-done.21.refs_3_, ...), custom_call_target="tpu_custom_call" | custom-call | flops 2097152 | bytes 2097152 | tf_op jit(solution)/shard_map/assemble/pallas_call | solution.py:252
  (31 shorter events, 0.1 us)
Async XLA Ops:
  0.6 27.3 %copy-start.1 = (bf16[1,1024,256]{2,1,0:T(8,128)(2,1)S(1)}, bf16[1,1024,256]{2,1,0:T(8,128)(2,1)}, u32[]{:S(2)}) copy-start(bf16[1,1024,256]{2,1,0:T(8,128)(2,1)} %param.25) | copy-start | bytes 1572868
  0.6 27.3 %copy-start = (bf16[1568,256]{1,0:T(8,128)(2,1)S(1)}, bf16[1568,256]{1,0:T(8,128)(2,1)}, u32[]{:S(2)}) copy-start(bf16[1568,256]{1,0:T(8,128)(2,1)} %leaving.3) | copy-start | bytes 2408452
  0.7 1.2 %copy-start.4 = (bf16[1,1568,256]{2,1,0:T(8,128)(2,1)S(1)}, bf16[1,1568,256]{2,1,0:T(8,128)(2,1)}, u32[]{:S(2)}) copy-start(bf16[1,1568,256]{2,1,0:T(8,128)(2,1)} %param.22) | copy-start | bytes 2408452
  2.8 23.9 %collective-permute-start.12 = (bf16[1120,256]{1,0:T(8,128)(2,1)}, bf16[1120,256]{1,0:T(8,128)(2,1)S(1)}, u32[]{:S(2)}, u32[]{:S(2)}) collective-permute-start(bf16[1120,256]{1,0:T(8,128)(2,1)} %get-tuple-element.39), channel_id=1, source_target_pairs={{8,0},{16,8},{24,16},{9,1},{17,9},{25,17},{10,2},{18,10},{26,18},{... | collective-permute-start | bytes 1720328 | tf_op jit(solution)/shard_map/ppermute | solution.py:19
  5.8 17.5 %collective-permute-start = (bf16[98,1024]{1,0:T(8,128)(2,1)}, bf16[98,1024]{1,0:T(8,128)(2,1)}, u32[]{:S(2)}, u32[]{:S(2)}) collective-permute-start(bf16[98,1024]{1,0:T(8,128)(2,1)} %bitcast.26), channel_id=1, source_target_pairs={{0,8},{8,16},{16,24},{1,9},{9,17},{17,25},{2,10},{10,18},{18,26},{... | collective-permute-start | bytes 602120 | tf_op jit(solution)/shard_map/ppermute | solution.py:19
  8.1 37.1 %collective-permute-start.5 = (bf16[1024,512]{1,0:T(8,128)(2,1)}, bf16[1024,512]{1,0:T(8,128)(2,1)}, u32[]{:S(2)}, u32[]{:S(2)}) collective-permute-start(bf16[1024,512]{1,0:T(8,128)(2,1)} %bitcast.20), channel_id=1, source_target_pairs={{0,1},{1,0},{2,3},{3,2},{4,5},{5,4},{6,7},{7,6},{8,9},{9,8},{10,11... | collective-permute-start | bytes 3145736 | tf_op jit(solution)/shard_map/ppermute | solution.py:23
  9.4 21.1 %collective-permute-start.13 = (bf16[448,256]{1,0:T(8,128)(2,1)S(1)}, bf16[448,256]{1,0:T(8,128)(2,1)S(1)}, u32[]{:S(2)}, u32[]{:S(2)}) collective-permute-start(bf16[448,256]{1,0:T(8,128)(2,1)S(1)} %get-tuple-element.45), channel_id=1, source_target_pairs={{8,0},{16,8},{24,16},{9,1},{17,9},{25,17},{10,2},{18,10},{26,18},{... | collective-permute-start | bytes 688136 | tf_op jit(solution)/shard_map/ppermute | solution.py:19
  13.3 39.6 %collective-permute-start.8 = (bf16[512,1024]{1,0:T(8,128)(2,1)}, bf16[512,1024]{1,0:T(8,128)(2,1)S(1)}, u32[]{:S(2)}, u32[]{:S(2)}) collective-permute-start(bf16[512,1024]{1,0:T(8,128)(2,1)} %bitcast.13), channel_id=1, source_target_pairs={{0,1},{1,0},{2,3},{3,2},{4,5},{5,4},{6,7},{7,6},{8,9},{9,8},{10,11... | collective-permute-start | bytes 3145736 | tf_op jit(solution)/shard_map/ppermute | solution.py:23
  13.7 1.1 %copy-start.3 = (bf16[1,1568,256]{2,1,0:T(8,128)(2,1)S(1)}, bf16[1,1568,256]{2,1,0:T(8,128)(2,1)}, u32[]{:S(2)}) copy-start(bf16[1,1568,256]{2,1,0:T(8,128)(2,1)} %param.21) | copy-start | bytes 2408452
  14.8 1.0 %copy-start.5 = (bf16[1,256,1024]{2,1,0:T(8,128)(2,1)S(1)}, bf16[1,256,1024]{2,1,0:T(8,128)(2,1)}, u32[]{:S(2)}) copy-start(bf16[1,256,1024]{2,1,0:T(8,128)(2,1)} %param.24) | copy-start | bytes 1572868
  15.9 7.5 %copy-start.10 = (bf16[98,1024]{1,0:T(8,128)(2,1)S(1)}, bf16[98,1024]{1,0:T(8,128)(2,1)}, u32[]{:S(2)}) copy-start(bf16[98,1024]{1,0:T(8,128)(2,1)} %param.14) | copy-start | bytes 602116
  24.3 11.7 %collective-permute-start.2 = (bf16[98,1024]{1,0:T(8,128)(2,1)S(1)}, bf16[98,1024]{1,0:T(8,128)(2,1)S(1)}, u32[]{:S(2)}, u32[]{:S(2)}) collective-permute-start(bf16[98,1024]{1,0:T(8,128)(2,1)S(1)} %broadcast_select_fusion.refs_0_.rows), channel_id=1, source_target_pairs={{0,4},{1,5},{2,6},{3,7},{4,0},{5,1},{6,2},{7,3},{8,12},{9,13},{10,... | collective-permute-start | bytes 602120 | tf_op jit(solution)/shard_map/ppermute | solution.py:38
  26.7 9.9 %collective-permute-start.1 = (bf16[98,1024]{1,0:T(8,128)(2,1)S(1)}, bf16[98,1024]{1,0:T(8,128)(2,1)S(1)}, u32[]{:S(2)}, u32[]{:S(2)}) collective-permute-start(bf16[98,1024]{1,0:T(8,128)(2,1)S(1)} %broadcast_select_fusion.refs_0_.rows), channel_id=1, source_target_pairs={{0,2},{1,3},{2,0},{3,1},{4,6},{5,7},{6,4},{7,5},{8,10},{9,11},{10,... | collective-permute-start | bytes 602120 | tf_op jit(solution)/shard_map/ppermute | solution.py:38
  30.5 14.1 %copy-start.11 = (f32[1,512]{1,0:T(1,128)S(1)}, f32[1,512]{1,0:T(1,128)}, u32[]{:S(2)}) copy-start(f32[1,512]{1,0:T(1,128)} %param.19) | copy-start | bytes 6148
  30.5 14.1 %copy-start.12 = (f32[1,512]{1,0:T(1,128)S(1)}, f32[1,512]{1,0:T(1,128)}, u32[]{:S(2)}) copy-start(f32[1,512]{1,0:T(1,128)} %param.18) | copy-start | bytes 6148
  30.6 14.6 %copy-start.7 = (bf16[1,1024,512]{2,1,0:T(8,128)(2,1)S(1)}, bf16[1,1024,512]{2,1,0:T(8,128)(2,1)}, u32[]{:S(2)}) copy-start(bf16[1,1024,512]{2,1,0:T(8,128)(2,1)} %param.17) | copy-start | bytes 3145732
  30.6 14.6 %copy-start.8 = (f32[1,1024]{1,0:T(1,128)S(1)}, f32[1,1024]{1,0:T(1,128)}, u32[]{:S(2)}) copy-start(f32[1,1024]{1,0:T(1,128)} %refs_6_.1) | copy-start | bytes 12292
  30.6 14.6 %copy-start.9 = (f32[1,1024]{1,0:T(1,128)S(1)}, f32[1,1024]{1,0:T(1,128)}, u32[]{:S(2)}) copy-start(f32[1,1024]{1,0:T(1,128)} %refs_7_.1) | copy-start | bytes 12292
  31.6 16.2 %collective-permute-start.14 = (bf16[256,1024]{1,0:T(8,128)(2,1)S(1)}, bf16[256,1024]{1,0:T(8,128)(2,1)S(1)}, u32[]{:S(2)}, u32[]{:S(2)}) collective-permute-start(bf16[256,1024]{1,0:T(8,128)(2,1)S(1)} %get-tuple-element.53), channel_id=1, source_target_pairs={{0,1},{1,0},{2,3},{3,2},{4,5},{5,4},{6,7},{7,6},{8,9},{9,8},{10,11... | collective-permute-start | bytes 1572872 | tf_op jit(solution)/shard_map/ppermute | solution.py:23
  36.0 5.2 %collective-permute-start.3 = (bf16[98,1024]{1,0:T(8,128)(2,1)S(1)}, bf16[98,1024]{1,0:T(8,128)(2,1)S(1)}, u32[]{:S(2)}, u32[]{:S(2)}) collective-permute-start(bf16[98,1024]{1,0:T(8,128)(2,1)S(1)} %collective-permute-done.2.refs_2_), channel_id=1, source_target_pairs={{0,2},{1,3},{2,0},{3,1},{4,6},{5,7},{6,4},{7,5},{8,10},{9,11},{10,... | collective-permute-start | bytes 602120 | tf_op jit(solution)/shard_map/ppermute | solution.py:38
  36.6 7.4 %collective-permute-start.16 = (bf16[64,1024]{1,0:T(8,128)(2,1)S(1)}, bf16[64,1024]{1,0:T(8,128)(2,1)S(1)}, u32[]{:S(2)}, u32[]{:S(2)}) collective-permute-start(bf16[64,1024]{1,0:T(8,128)(2,1)S(1)} %get-tuple-element.57), channel_id=1, source_target_pairs={{0,1},{1,0},{2,3},{3,2},{4,5},{5,4},{6,7},{7,6},{8,9},{9,8},{10,11... | collective-permute-start | bytes 393224 | tf_op jit(solution)/shard_map/ppermute | solution.py:23
  41.5 3.3 %collective-permute-start.4 = (f32[2,1024]{1,0:T(2,128)S(1)}, f32[2,1024]{1,0:T(2,128)S(1)}, u32[]{:S(2)}, u32[]{:S(2)}) collective-permute-start(f32[2,1024]{1,0:T(2,128)S(1)} %shard_map.156.refs_4_), channel_id=1, source_target_pairs={{0,1},{1,0},{2,3},{3,2},{4,5},{5,4},{6,7},{7,6},{8,9},{9,8},{10,11... | collective-permute-start | bytes 24584 | tf_op jit(solution)/shard_map/ppermute | solution.py:23
  44.1 5.1 %collective-permute-start.17 = (bf16[64,1024]{1,0:T(8,128)(2,1)S(1)}, bf16[64,1024]{1,0:T(8,128)(2,1)S(1)}, u32[]{:S(2)}, u32[]{:S(2)}) collective-permute-start(bf16[64,1024]{1,0:T(8,128)(2,1)S(1)} %shard_map.166), channel_id=1, source_target_pairs={{0,2},{1,3},{2,0},{3,1},{4,6},{5,7},{6,4},{7,5},{8,10},{9,11},{10,... | collective-permute-start | bytes 393224 | tf_op jit(solution)/shard_map/ppermute | solution.py:38
  44.7 8.2 %copy-start.2 = (bf16[1,512,1024]{2,1,0:T(8,128)(2,1)S(1)}, bf16[1,512,1024]{2,1,0:T(8,128)(2,1)}, u32[]{:S(2)}) copy-start(bf16[1,512,1024]{2,1,0:T(8,128)(2,1)} %param.20) | copy-start | bytes 3145732
  44.8 8.0 %collective-permute-start.7 = (f32[2,512]{1,0:T(2,128)S(1)}, f32[2,512]{1,0:T(2,128)S(1)}, u32[]{:S(2)}, u32[]{:S(2)}) collective-permute-start(f32[2,512]{1,0:T(2,128)S(1)} %pad_maximum_fusion.one), channel_id=1, source_target_pairs={{0,1},{1,0},{2,3},{3,2},{4,5},{5,4},{6,7},{7,6},{8,9},{9,8},{10,11... | collective-permute-start | bytes 12296 | tf_op jit(solution)/shard_map/ppermute | solution.py:23
  47.6 5.3 %collective-permute-start.6 = (f32[2,1024]{1,0:T(2,128)S(1)}, f32[2,1024]{1,0:T(2,128)S(1)}, u32[]{:S(2)}, u32[]{:S(2)}) collective-permute-start(f32[2,1024]{1,0:T(2,128)S(1)} %get-tuple-element.34), channel_id=1, source_target_pairs={{0,1},{1,0},{2,3},{3,2},{4,5},{5,4},{6,7},{7,6},{8,9},{9,8},{10,11... | collective-permute-start | bytes 24584 | tf_op jit(solution)/shard_map/ppermute | solution.py:23
  49.2 7.8 %collective-permute-start.18 = (bf16[64,1024]{1,0:T(8,128)(2,1)S(1)}, bf16[64,1024]{1,0:T(8,128)(2,1)S(1)}, u32[]{:S(2)}, u32[]{:S(2)}) collective-permute-start(bf16[64,1024]{1,0:T(8,128)(2,1)S(1)} %add_convert_fusion.1), channel_id=1, source_target_pairs={{0,4},{1,5},{2,6},{3,7},{4,0},{5,1},{6,2},{7,3},{8,12},{9,13},{10,... | collective-permute-start | bytes 393224 | tf_op jit(solution)/shard_map/ppermute | solution.py:38
  51.4 5.6 %collective-permute-start.15 = (bf16[64,1024]{1,0:T(8,128)(2,1)S(1)}, bf16[64,1024]{1,0:T(8,128)(2,1)S(1)}, u32[]{:S(2)}, u32[]{:S(2)}) collective-permute-start(bf16[64,1024]{1,0:T(8,128)(2,1)S(1)} %get-tuple-element.55), channel_id=1, source_target_pairs={{0,2},{1,3},{2,0},{3,1},{4,6},{5,7},{6,4},{7,5},{8,10},{9,11},{10,... | collective-permute-start | bytes 393224 | tf_op jit(solution)/shard_map/ppermute | solution.py:38
  52.9 28.5 %copy-start.6 = (bf16[1,256,1024]{2,1,0:T(8,128)(2,1)S(1)}, bf16[1,256,1024]{2,1,0:T(8,128)(2,1)}, u32[]{:S(2)}) copy-start(bf16[1,256,1024]{2,1,0:T(8,128)(2,1)} %param.24) | copy-start | bytes 1572868
  54.1 11.9 %collective-permute-start.10 = (bf16[98,1024]{1,0:T(8,128)(2,1)S(1)}, bf16[98,1024]{1,0:T(8,128)(2,1)S(1)}, u32[]{:S(2)}, u32[]{:S(2)}) collective-permute-start(bf16[98,1024]{1,0:T(8,128)(2,1)S(1)} %get-tuple-element.38), channel_id=1, source_target_pairs={{0,2},{1,3},{2,0},{3,1},{4,6},{5,7},{6,4},{7,5},{8,10},{9,11},{10,... | collective-permute-start | bytes 602120 | tf_op jit(solution)/shard_map/ppermute | solution.py:38
  57.1 6.5 %collective-permute-start.20 = (bf16[64,1024]{1,0:T(8,128)(2,1)S(1)}, bf16[64,1024]{1,0:T(8,128)(2,1)S(1)}, u32[]{:S(2)}, u32[]{:S(2)}) collective-permute-start(bf16[64,1024]{1,0:T(8,128)(2,1)S(1)} %shard_map.167.refs_0_), channel_id=1, source_target_pairs={{0,4},{1,5},{2,6},{3,7},{4,0},{5,1},{6,2},{7,3},{8,12},{9,13},{10,... | collective-permute-start | bytes 393224 | tf_op jit(solution)/shard_map/ppermute | solution.py:38
  58.9 13.1 %collective-permute-start.9 = (bf16[98,1024]{1,0:T(8,128)(2,1)S(1)}, bf16[98,1024]{1,0:T(8,128)(2,1)S(1)}, u32[]{:S(2)}, u32[]{:S(2)}) collective-permute-start(bf16[98,1024]{1,0:T(8,128)(2,1)S(1)} %get-tuple-element.36), channel_id=1, source_target_pairs={{0,2},{1,3},{2,0},{3,1},{4,6},{5,7},{6,4},{7,5},{8,10},{9,11},{10,... | collective-permute-start | bytes 602120 | tf_op jit(solution)/shard_map/ppermute | solution.py:38
  61.9 15.4 %collective-permute-start.19 = (bf16[64,1024]{1,0:T(8,128)(2,1)S(1)}, bf16[64,1024]{1,0:T(8,128)(2,1)S(1)}, u32[]{:S(2)}, u32[]{:S(2)}) collective-permute-start(bf16[64,1024]{1,0:T(8,128)(2,1)S(1)} %shard_map.167.refs_0_), channel_id=1, source_target_pairs={{0,2},{1,3},{2,0},{3,1},{4,6},{5,7},{6,4},{7,5},{8,10},{9,11},{10,... | collective-permute-start | bytes 393224 | tf_op jit(solution)/shard_map/ppermute | solution.py:38
  63.6 16.6 %collective-permute-start.21 = (bf16[64,1024]{1,0:T(8,128)(2,1)S(1)}, bf16[64,1024]{1,0:T(8,128)(2,1)S(1)}, u32[]{:S(2)}, u32[]{:S(2)}) collective-permute-start(bf16[64,1024]{1,0:T(8,128)(2,1)S(1)} %collective-permute-done.20.refs_2_), channel_id=1, source_target_pairs={{0,2},{1,3},{2,0},{3,1},{4,6},{5,7},{6,4},{7,5},{8,10},{9,11},{10,... | collective-permute-start | bytes 393224 | tf_op jit(solution)/shard_map/ppermute | solution.py:38
  66.1 17.6 %collective-permute-start.11 = (bf16[98,1024]{1,0:T(8,128)(2,1)S(1)}, bf16[98,1024]{1,0:T(8,128)(2,1)S(1)}, u32[]{:S(2)}, u32[]{:S(2)}) collective-permute-start(bf16[98,1024]{1,0:T(8,128)(2,1)S(1)} %add_convert_fusion), channel_id=1, source_target_pairs={{0,4},{1,5},{2,6},{3,7},{4,0},{5,1},{6,2},{7,3},{8,12},{9,13},{10,... | collective-permute-start | bytes 602120 | tf_op jit(solution)/shard_map/ppermute | solution.py:38
  69.7 14.7 %collective-permute-start.22 = (bf16[64,1024]{1,0:T(8,128)(2,1)S(1)}, bf16[64,1024]{1,0:T(8,128)(2,1)S(1)}, u32[]{:S(2)}, u32[]{:S(2)}) collective-permute-start(bf16[64,1024]{1,0:T(8,128)(2,1)S(1)} %shard_map.167.refs_0_), channel_id=1, source_target_pairs={{0,1},{1,0},{2,3},{3,2},{4,5},{5,4},{6,7},{7,6},{8,9},{9,8},{10,11... | collective-permute-start | bytes 393224 | tf_op jit(solution)/shard_map/ppermute | solution.py:23
  72.0 12.5 %collective-permute-start.24 = (bf16[64,1024]{1,0:T(8,128)(2,1)S(1)}, bf16[64,1024]{1,0:T(8,128)(2,1)S(1)}, u32[]{:S(2)}, u32[]{:S(2)}) collective-permute-start(bf16[64,1024]{1,0:T(8,128)(2,1)S(1)} %collective-permute-done.20.refs_2_), channel_id=1, source_target_pairs={{0,1},{1,0},{2,3},{3,2},{4,5},{5,4},{6,7},{7,6},{8,9},{9,8},{10,11... | collective-permute-start | bytes 393224 | tf_op jit(solution)/shard_map/ppermute | solution.py:23
  77.3 7.1 %collective-permute-start.23 = (bf16[64,1024]{1,0:T(8,128)(2,1)S(1)}, bf16[64,1024]{1,0:T(8,128)(2,1)S(1)}, u32[]{:S(2)}, u32[]{:S(2)}) collective-permute-start(bf16[64,1024]{1,0:T(8,128)(2,1)S(1)} %collective-permute-done.19.refs_1_), channel_id=1, source_target_pairs={{0,1},{1,0},{2,3},{3,2},{4,5},{5,4},{6,7},{7,6},{8,9},{9,8},{10,11... | collective-permute-start | bytes 393224 | tf_op jit(solution)/shard_map/ppermute | solution.py:23
  80.2 4.3 %collective-permute-start.25 = (bf16[64,1024]{1,0:T(8,128)(2,1)S(1)}, bf16[64,1024]{1,0:T(8,128)(2,1)S(1)}, u32[]{:S(2)}, u32[]{:S(2)}) collective-permute-start(bf16[64,1024]{1,0:T(8,128)(2,1)S(1)} %collective-permute-done.21.refs_3_), channel_id=1, source_target_pairs={{0,1},{1,0},{2,3},{3,2},{4,5},{5,4},{6,7},{7,6},{8,9},{9,8},{10,11... | collective-permute-start | bytes 393224 | tf_op jit(solution)/shard_map/ppermute | solution.py:23

commit v6 on v5

--- a/solution.py
+++ b/solution.py
@@ -58,11 +58,11 @@
     return got
 
 
-def scatter(pieces):
+def scatter(pieces, far=None):
     count = lax.axis_size("dev") // 2
     if not in_pairs(count):
         return [across(pieces[step].astype(bf16), step) for step in range(count - 1, 0, -1)]
-    far = range(count - 2, 0, -2)
+    far = far or range(count - 2, 0, -2)
     inner = {}
     for step in far:
         inner[step] = across(pieces[step ^ 1], 1)
@@ -458,12 +458,14 @@
     own_late, *partials = whole_arrays(
         functools.partial(late_hidden_kernel, count, total_rows),
         [shape((rows, channels), f32)]
-        + [shape((rows, channels), piece_type(step, count)) for step in steps],
+        + [
+            shape((rows, channels), f32 if step > 1 and step % 2 else bf16) for step in steps
+        ],
         [inner, sums, got_sums, one, two, reduce_late[0], reduce_two, own_rows],
         late_work,
         [pltpu.VMEM((count * held, 2 * hidden), bf16)],
     )
-    late_terms = scatter(dict(zip(steps, partials)))
+    late_terms = scatter(dict(zip(steps, partials)), range(count - 1, 2, -2))
 
     factor = 1.0 / math.sqrt(pixels * lax.axis_size("dev"))
     (summed,) = whole_arrays(

time: 86.3 us -> 84 us (0.973)
  the two profiles are of different devices: /device:TPU:5 before, /device:TPU:4 now
where the time goes in v6:
time: 84 us; the launch traced here: 83.6 us
  waiting for transfers between devices  33 us (39%)
  starting transfers between devices  29.1 us (35%)
  Pallas kernels  16.1 us (19%)
  local copies, waits for them, and re-layouts  3.47 us (4%)
  other arithmetic  1.05 us (1%)
  between operations  0.9 us (1%)
    ppermute x12, waiting for transfers between devices, across(): return lax.ppermute(x, 'dev', pairs)  26.5 us
    ppermute x12, starting transfers between devices, across(): return lax.ppermute(x, 'dev', pairs)  17.9 us
    pallas_call x12, Pallas kernels, whole_arrays(): pl.pallas_call(body, out_shape=list(outs), in_specs=[pl.BlockSpec(memory_...  14.6 us
    ppermute x3, starting transfers between devices, from_behind(): return lax.ppermute(x, axis, pairs)  10.1 us
    ppermute x3, waiting for transfers between devices, from_behind(): return lax.ppermute(x, axis, pairs)  6.25 us
    unnamed x26, local copies, waits for them, and re-layouts  3.47 us
  transfers between devices with their start and end apart: 26, of which 12 were waited for; matrix products, arithmetic and copies ran while one was open for 1% of the time, Pallas kernels for 16%

profile of v6, /device:TPU:4, one launch (start us, length us, event | category | flops | bytes accessed | tf_op | source)
XLA Modules:
  0.0 83.6 jit_solution(17276109113152449525)
XLA Ops:
  0.7 1.2 %copy-done.4 = bf16[1,1568,256]{2,1,0:T(8,128)(2,1)S(1)} copy-done((bf16[1,1568,256]{2,1,0:T(8,128)(2,1)S(1)}, bf16[1,1568,256]{2,1,0:T(8,128)(2,1)}, u32[]{:S(2)}) %copy-start.4) | copy-done | bytes 802840
  1.9 0.9 %shard_map.160 = (bf16[1120,256]{1,0:T(8,128)(2,1)}, bf16[448,256]{1,0:T(8,128)(2,1)S(1)}) custom-call(bf16[1568,256]{1,0:T(8,128)(2,1)S(1)} %bitcast.17), custom_call_target="tpu_custom_call" | custom-call | flops 1605632 | bytes 1605632 | tf_op jit(solution)/shard_map/pallas_call | solution.py:86
  2.8 3.3 %collective-permute-start.12 = (bf16[1120,256]{1,0:T(8,128)(2,1)}, bf16[1120,256]{1,0:T(8,128)(2,1)S(1)}, u32[]{:S(2)}, u32[]{:S(2)}) collective-permute-start(bf16[1120,256]{1,0:T(8,128)(2,1)} %get-tuple-element.39), channel_id=1, source_target_pairs={{8,0},{16,8},{24,16},{9,1},{17,9},{25,17},{10,2},{18,10},{26,18},{... | collective-permute-start | bytes 1720328 | tf_op jit(solution)/shard_map/ppermute | solution.py:19
  6.1 2.5 %collective-permute-start = (bf16[98,1024]{1,0:T(8,128)(2,1)}, bf16[98,1024]{1,0:T(8,128)(2,1)}, u32[]{:S(2)}, u32[]{:S(2)}) collective-permute-start(bf16[98,1024]{1,0:T(8,128)(2,1)} %bitcast.26), channel_id=1, source_target_pairs={{0,8},{8,16},{16,24},{1,9},{9,17},{17,25},{2,10},{10,18},{18,26},{... | collective-permute-start | bytes 602120 | tf_op jit(solution)/shard_map/ppermute | solution.py:19
  8.6 0.1 collective-permute-start.5
  8.7 4.2 %collective-permute-start.13 = (bf16[448,256]{1,0:T(8,128)(2,1)S(1)}, bf16[448,256]{1,0:T(8,128)(2,1)S(1)}, u32[]{:S(2)}, u32[]{:S(2)}) collective-permute-start(bf16[448,256]{1,0:T(8,128)(2,1)S(1)} %get-tuple-element.45), channel_id=1, source_target_pairs={{8,0},{16,8},{24,16},{9,1},{17,9},{25,17},{10,2},{18,10},{26,18},{... | collective-permute-start | bytes 688136 | tf_op jit(solution)/shard_map/ppermute | solution.py:19
  12.9 0.3 collective-permute-start.8
  13.2 1.1 %copy-done.3 = bf16[1,1568,256]{2,1,0:T(8,128)(2,1)S(1)} copy-done((bf16[1,1568,256]{2,1,0:T(8,128)(2,1)S(1)}, bf16[1,1568,256]{2,1,0:T(8,128)(2,1)}, u32[]{:S(2)}) %copy-start.3) | copy-done | bytes 802840
  14.3 1.0 %copy-done.5 = bf16[1,256,1024]{2,1,0:T(8,128)(2,1)S(1)} copy-done((bf16[1,256,1024]{2,1,0:T(8,128)(2,1)S(1)}, bf16[1,256,1024]{2,1,0:T(8,128)(2,1)}, u32[]{:S(2)}) %copy-start.5) | copy-done | bytes 524312
  15.4 3.1 %shard_map.161 = (bf16[1120,1024]{1,0:T(8,128)(2,1)S(1)}, bf16[1120,1024]{1,0:T(8,128)(2,1)S(1)}, bf16[448,1024]{1,0:T(8,128)(2,1)S(1)}, bf16[448,1024]{1,0:T(8,128)(2,1)S(1)}, bf16[448,256]{1,0:T(8,128)(2,1)S(1)}) custom-call(bf16[1568,256]{1,0:T(8,128)(2,1)S(1)} %bitcast.15, bf16[256,1024]{1,0:T(8,128)(2,1)S(1)} %bitcast.18), custom_call_target="tpu_custom_call" | custom-call | flops 822083584 | bytes 7979008 | tf_op jit(solution)/shard_map/pallas_call | solution.py:86
  18.5 6.2 %collective-permute-done = bf16[98,1024]{1,0:T(8,128)(2,1)} collective-permute-done((bf16[98,1024]{1,0:T(8,128)(2,1)}, bf16[98,1024]{1,0:T(8,128)(2,1)}, u32[]{:S(2)}, u32[]{:S(2)}) %collective-permute-start) | collective-permute-done | bytes 200736 | tf_op jit(solution)/shard_map/ppermute | solution.py:19
  24.8 1.0 %broadcast_select_fusion.refs_0_.rows = bf16[98,1024]{1,0:T(8,128)(2,1)S(1)} fusion(bf16[98,1024]{1,0:T(8,128)(2,1)S(1)} %copy-done.10, bf16[98,1024]{1,0:T(8,128)(2,1)} %collective-permute-done, pred[]{:T(512)S(6)} %eq.3), kind=kLoop, calls=%fused_computation.2 | loop fusion | flops 100352 | bytes 602113 | tf_op jit(solution)/shard_map/jit(_where)/select_n | solution.py:383
  25.7 3.2 %collective-permute-start.2 = (bf16[98,1024]{1,0:T(8,128)(2,1)S(1)}, bf16[98,1024]{1,0:T(8,128)(2,1)S(1)}, u32[]{:S(2)}, u32[]{:S(2)}) collective-permute-start(bf16[98,1024]{1,0:T(8,128)(2,1)S(1)} %broadcast_select_fusion.refs_0_.rows), channel_id=1, source_target_pairs={{0,4},{1,5},{2,6},{3,7},{4,0},{5,1},{6,2},{7,3},{8,12},{9,13},{10,... | collective-permute-start | bytes 602120 | tf_op jit(solution)/shard_map/ppermute | solution.py:38
  28.9 0.0 collective-permute-done.12.arrived
  28.9 1.6 %collective-permute-start.1 = (bf16[98,1024]{1,0:T(8,128)(2,1)S(1)}, bf16[98,1024]{1,0:T(8,128)(2,1)S(1)}, u32[]{:S(2)}, u32[]{:S(2)}) collective-permute-start(bf16[98,1024]{1,0:T(8,128)(2,1)S(1)} %broadcast_select_fusion.refs_0_.rows), channel_id=1, source_target_pairs={{0,2},{1,3},{2,0},{3,1},{4,6},{5,7},{6,4},{7,5},{8,10},{9,11},{10,... | collective-permute-start | bytes 602120 | tf_op jit(solution)/shard_map/ppermute | solution.py:38
  30.5 2.5 %shard_map.162 = (bf16[1120,256]{1,0:T(8,128)(2,1)S(1)}, bf16[1120,1024]{1,0:T(8,128)(2,1)S(1)}, f32[256,1024]{1,0:T(8,128)S(1)}, f32[256,1024]{1,0:T(8,128)S(1)}) custom-call(bf16[1568,256]{1,0:T(8,128)(2,1)S(1)} %bitcast.16, bf16[1568,256]{1,0:T(8,128)(2,1)S(1)} %copy-done, bf16[1120,256]{1,0:T(8,128)(2,1)S(1)} %collective-permute-done.12.arrived, ...), custom_call_target="tpu_custom_call" | custom-call | flops 1761607680 | bytes 12255232 | tf_op jit(solution)/shard_map/pallas_call | solution.py:86
  33.1 0.0 collective-permute-done.13.arrived
  33.1 0.0 copy-start.11
  33.1 0.0 copy-start.12
  33.1 0.0 copy-start.7
  33.1 0.0 copy-start.8
  33.1 0.0 copy-start.9
  33.1 1.0 %shard_map.163 = (bf16[448,256]{1,0:T(8,128)(2,1)S(1)}, bf16[448,1024]{1,0:T(8,128)(2,1)S(1)}, f32[256,1024]{1,0:T(8,128)S(1)}, bf16[256,1024]{1,0:T(8,128)(2,1)S(1)}, bf16[64,1024]{1,0:T(8,128)(2,1)S(1)}) custom-call(bf16[448,256]{1,0:T(8,128)(2,1)S(1)} %get-tuple-element.44.saved, bf16[1568,256]{1,0:T(8,128)(2,1)S(1)} %copy-done, ...), custom_call_target="tpu_custom_call" | custom-call | flops 704643072 | bytes 8568832 | tf_op jit(solution)/shard_map/pallas_call | solution.py:86
  34.2 0.1 collective-permute-start.14
  34.2 2.7 %collective-permute-done.2.refs_2_ = bf16[98,1024]{1,0:T(8,128)(2,1)S(1)} collective-permute-done((bf16[98,1024]{1,0:T(8,128)(2,1)S(1)}, bf16[98,1024]{1,0:T(8,128)(2,1)S(1)}, u32[]{:S(2)}, u32[]{:S(2)}) %collective-permute-start.2) | collective-permute-done | bytes 200736 | tf_op jit(solution)/shard_map/ppermute | solution.py:38
  36.9 0.5 collective-permute-start.3
  37.5 0.0 collective-permute-done.1.refs_1_
  37.5 0.0 collective-permute-start.16
  37.5 5.6 %collective-permute-done.3.refs_3_ = bf16[98,1024]{1,0:T(8,128)(2,1)S(1)} collective-permute-done((bf16[98,1024]{1,0:T(8,128)(2,1)S(1)}, bf16[98,1024]{1,0:T(8,128)(2,1)S(1)}, u32[]{:S(2)}, u32[]{:S(2)}) %collective-permute-start.3) | collective-permute-done | bytes 200736 | tf_op jit(solution)/shard_map/ppermute | solution.py:38
  43.0 0.2 shard_map.156.refs_4_
  43.3 0.1 collective-permute-start.4
  43.4 0.9 %collective-permute-start.17 = (bf16[64,1024]{1,0:T(8,128)(2,1)S(1)}, bf16[64,1024]{1,0:T(8,128)(2,1)S(1)}, u32[]{:S(2)}, u32[]{:S(2)}) collective-permute-start(bf16[64,1024]{1,0:T(8,128)(2,1)S(1)} %shard_map.166), channel_id=1, source_target_pairs={{0,2},{1,3},{2,0},{3,1},{4,6},{5,7},{6,4},{7,5},{8,10},{9,11},{10,... | collective-permute-start | bytes 393224 | tf_op jit(solution)/shard_map/ppermute | solution.py:38
  44.3 0.0 copy-start.2
  44.3 0.2 collective-permute-done.4.refs_5_
  44.5 0.2 collective-permute-start.7
  44.7 2.4 %shard_map.157 = (f32[448,1024]{1,0:T(8,128)S(1)}, f32[2,1024]{1,0:T(2,128)S(1)}, f32[2,1024]{1,0:T(2,128)S(1)}) custom-call(bf16[98,1024]{1,0:T(8,128)(2,1)S(1)} %broadcast_select_fusion.refs_0_.rows, bf16[98,1024]{1,0:T(8,128)(2,1)S(1)} %collective-permute-done.1.refs_1_, bf16[98,1024]{1,0:T(8,128)(2,1)S(1)} %collective-permute-done.2.refs_2_, ...), custom_call_target="tpu_custom_call" | custom-call | flops 939524096 | bytes 4775936 | tf_op jit(solution)/shard_map/pallas_call | solution.py:86
  47.1 0.4 collective-permute-start.6
  47.5 0.1 shard_map.165
  47.6 1.8 %collective-permute-done.17 = bf16[64,1024]{1,0:T(8,128)(2,1)S(1)} collective-permute-done((bf16[64,1024]{1,0:T(8,128)(2,1)S(1)}, bf16[64,1024]{1,0:T(8,128)(2,1)S(1)}, u32[]{:S(2)}, u32[]{:S(2)}) %collective-permute-start.17) | collective-permute-done | bytes 131104 | tf_op jit(solution)/shard_map/ppermute | solution.py:38
  49.4 2.5 %collective-permute-start.18 = (bf16[64,1024]{1,0:T(8,128)(2,1)S(1)}, bf16[64,1024]{1,0:T(8,128)(2,1)S(1)}, u32[]{:S(2)}, u32[]{:S(2)}) collective-permute-start(bf16[64,1024]{1,0:T(8,128)(2,1)S(1)} %add_convert_fusion.1), channel_id=1, source_target_pairs={{0,4},{1,5},{2,6},{3,7},{4,0},{5,1},{6,2},{7,3},{8,12},{9,13},{10,... | collective-permute-start | bytes 393224 | tf_op jit(solution)/shard_map/ppermute | solution.py:38
  51.9 1.7 %collective-permute-start.15 = (bf16[64,1024]{1,0:T(8,128)(2,1)S(1)}, bf16[64,1024]{1,0:T(8,128)(2,1)S(1)}, u32[]{:S(2)}, u32[]{:S(2)}) collective-permute-start(bf16[64,1024]{1,0:T(8,128)(2,1)S(1)} %get-tuple-element.55), channel_id=1, source_target_pairs={{0,2},{1,3},{2,0},{3,1},{4,6},{5,7},{6,4},{7,5},{8,10},{9,11},{10,... | collective-permute-start | bytes 393224 | tf_op jit(solution)/shard_map/ppermute | solution.py:38
  53.7 0.0 collective-permute-done.6.got
  53.7 0.0 copy-start.6
  53.7 1.2 %shard_map.158 = (f32[98,1024]{1,0:T(8,128)S(1)}, bf16[98,1024]{1,0:T(8,128)(2,1)S(1)}, bf16[98,1024]{1,0:T(8,128)(2,1)S(1)}, f32[98,1024]{1,0:T(8,128)S(1)}) custom-call(f32[448,1024]{1,0:T(8,128)S(1)} %get-tuple-element.32.inner, f32[2,1024]{1,0:T(2,128)S(1)} %get-tuple-element.33.sums, f32[2,1024]{1,0:T(2,128)S(1)} %collective-permute-done.6.got, ...), custom_call_target="tpu_custom_call" | custom-call | flops 939524096 | bytes 5361664 | tf_op jit(solution)/shard_map/pallas_call | solution.py:86
  54.9 0.3 collective-permute-start.10
  55.2 3.1 %collective-permute-done.18.refs_1_ = bf16[64,1024]{1,0:T(8,128)(2,1)S(1)} collective-permute-done((bf16[64,1024]{1,0:T(8,128)(2,1)S(1)}, bf16[64,1024]{1,0:T(8,128)(2,1)S(1)}, u32[]{:S(2)}, u32[]{:S(2)}) %collective-permute-start.18) | collective-permute-done | bytes 131104 | tf_op jit(solution)/shard_map/ppermute | solution.py:38
  58.3 1.1 %collective-permute-done.15.refs_0_ = bf16[64,1024]{1,0:T(8,128)(2,1)S(1)} collective-permute-done((bf16[64,1024]{1,0:T(8,128)(2,1)S(1)}, bf16[64,1024]{1,0:T(8,128)(2,1)S(1)}, u32[]{:S(2)}, u32[]{:S(2)}) %collective-permute-start.15) | collective-permute-done | bytes 131104 | tf_op jit(solution)/shard_map/ppermute | solution.py:38
  59.4 0.1 shard_map.167.refs_0_
  59.5 1.4 %collective-permute-start.20 = (bf16[64,1024]{1,0:T(8,128)(2,1)S(1)}, bf16[64,1024]{1,0:T(8,128)(2,1)S(1)}, u32[]{:S(2)}, u32[]{:S(2)}) collective-permute-start(bf16[64,1024]{1,0:T(8,128)(2,1)S(1)} %shard_map.167.refs_0_), channel_id=1, source_target_pairs={{0,4},{1,5},{2,6},{3,7},{4,0},{5,1},{6,2},{7,3},{8,12},{9,13},{10,... | collective-permute-start | bytes 393224 | tf_op jit(solution)/shard_map/ppermute | solution.py:38
  60.9 2.1 %collective-permute-start.9 = (bf16[98,1024]{1,0:T(8,128)(2,1)S(1)}, bf16[98,1024]{1,0:T(8,128)(2,1)S(1)}, u32[]{:S(2)}, u32[]{:S(2)}) collective-permute-start(bf16[98,1024]{1,0:T(8,128)(2,1)S(1)} %get-tuple-element.36), channel_id=1, source_target_pairs={{0,2},{1,3},{2,0},{3,1},{4,6},{5,7},{6,4},{7,5},{8,10},{9,11},{10,... | collective-permute-start | bytes 602120 | tf_op jit(solution)/shard_map/ppermute | solution.py:38
  63.0 0.0 collective-permute-start.19
  63.0 4.3 %collective-permute-done.20.refs_2_ = bf16[64,1024]{1,0:T(8,128)(2,1)S(1)} collective-permute-done((bf16[64,1024]{1,0:T(8,128)(2,1)S(1)}, bf16[64,1024]{1,0:T(8,128)(2,1)S(1)}, u32[]{:S(2)}, u32[]{:S(2)}) %collective-permute-start.20) | collective-permute-done | bytes 131104 | tf_op jit(solution)/shard_map/ppermute | solution.py:38
  67.3 1.2 %collective-permute-start.21 = (bf16[64,1024]{1,0:T(8,128)(2,1)S(1)}, bf16[64,1024]{1,0:T(8,128)(2,1)S(1)}, u32[]{:S(2)}, u32[]{:S(2)}) collective-permute-start(bf16[64,1024]{1,0:T(8,128)(2,1)S(1)} %collective-permute-done.20.refs_2_), channel_id=1, source_target_pairs={{0,2},{1,3},{2,0},{3,1},{4,6},{5,7},{6,4},{7,5},{8,10},{9,11},{10,... | collective-permute-start | bytes 393224 | tf_op jit(solution)/shard_map/ppermute | solution.py:38
  68.5 0.0 collective-permute-done.10
  68.5 0.1 add_convert_fusion
  68.5 2.4 %collective-permute-start.11 = (bf16[98,1024]{1,0:T(8,128)(2,1)S(1)}, bf16[98,1024]{1,0:T(8,128)(2,1)S(1)}, u32[]{:S(2)}, u32[]{:S(2)}) collective-permute-start(bf16[98,1024]{1,0:T(8,128)(2,1)S(1)} %add_convert_fusion), channel_id=1, source_target_pairs={{0,6},{1,7},{2,4},{3,5},{4,2},{5,3},{6,0},{7,1},{8,14},{9,15},{10,... | collective-permute-start | bytes 602120 | tf_op jit(solution)/shard_map/ppermute | solution.py:38
  71.0 0.4 collective-permute-done.9.refs_0_
  71.4 0.1 collective-permute-start.24
  71.5 2.7 %collective-permute-done.19.refs_1_ = bf16[64,1024]{1,0:T(8,128)(2,1)S(1)} collective-permute-done((bf16[64,1024]{1,0:T(8,128)(2,1)S(1)}, bf16[64,1024]{1,0:T(8,128)(2,1)S(1)}, u32[]{:S(2)}, u32[]{:S(2)}) %collective-permute-start.19) | collective-permute-done | bytes 131104 | tf_op jit(solution)/shard_map/ppermute | solution.py:38
  74.2 2.6 %collective-permute-done.21.refs_3_ = bf16[64,1024]{1,0:T(8,128)(2,1)S(1)} collective-permute-done((bf16[64,1024]{1,0:T(8,128)(2,1)S(1)}, bf16[64,1024]{1,0:T(8,128)(2,1)S(1)}, u32[]{:S(2)}, u32[]{:S(2)}) %collective-permute-start.21) | collective-permute-done | bytes 131104 | tf_op jit(solution)/shard_map/ppermute | solution.py:38
  76.8 2.3 %shard_map.164 = bf16[1568,256]{1,0:T(8,128)(2,1)} custom-call(bf16[256,1024]{1,0:T(8,128)(2,1)S(1)} %bitcast.19, bf16[1120,256]{1,0:T(8,128)(2,1)S(1)} %get-tuple-element.42.refs_0_, bf16[1120,1024]{1,0:T(8,128)(2,1)S(1)} %get-tuple-element.43.refs_1_, bf16[448,256]{1,0:T(8,128)(2,1)S(1)} %get-tuple-element.50.refs_2_, ...), custom_call_target="tpu_custom_call" | custom-call | flops 822083584 | bytes 5341184 | tf_op jit(solution)/shard_map/pallas_call | solution.py:86
  79.1 2.2 %collective-permute-done.11.refs_1_ = bf16[98,1024]{1,0:T(8,128)(2,1)S(1)} collective-permute-done((bf16[98,1024]{1,0:T(8,128)(2,1)S(1)}, bf16[98,1024]{1,0:T(8,128)(2,1)S(1)}, u32[]{:S(2)}, u32[]{:S(2)}) %collective-permute-start.11) | collective-permute-done | bytes 200736 | tf_op jit(solution)/shard_map/ppermute | solution.py:38
  81.4 0.7 shard_map.159
  82.1 1.5 %assemble.1 = (f32[256,1024]{1,0:T(8,128)}, f32[1024,256]{1,0:T(8,128)}) custom-call(bf16[64,1024]{1,0:T(8,128)(2,1)S(1)} %shard_map.167.refs_0_, bf16[64,1024]{1,0:T(8,128)(2,1)S(1)} %collective-permute-done.19.refs_1_, bf16[64,1024]{1,0:T(8,128)(2,1)S(1)} %collective-permute-done.20.refs_2_, bf16[64,1024]{1,0:T(8,128)(2,1)S(1)} %collective-permute-done.21.refs_3_, ...), custom_call_target="tpu_custom_call" | custom-call | flops 2097152 | bytes 2097152 | tf_op jit(solution)/shard_map/assemble/pallas_call | solution.py:252
  (31 shorter events, 0.1 us)
Async XLA Ops:
  0.6 29.9 %copy-start.1 = (bf16[1,1024,256]{2,1,0:T(8,128)(2,1)S(1)}, bf16[1,1024,256]{2,1,0:T(8,128)(2,1)}, u32[]{:S(2)}) copy-start(bf16[1,1024,256]{2,1,0:T(8,128)(2,1)} %param.25) | copy-start | bytes 1572868
  0.6 29.9 %copy-start = (bf16[1568,256]{1,0:T(8,128)(2,1)S(1)}, bf16[1568,256]{1,0:T(8,128)(2,1)}, u32[]{:S(2)}) copy-start(bf16[1568,256]{1,0:T(8,128)(2,1)} %leaving.3) | copy-start | bytes 2408452
  0.7 1.2 %copy-start.4 = (bf16[1,1568,256]{2,1,0:T(8,128)(2,1)S(1)}, bf16[1,1568,256]{2,1,0:T(8,128)(2,1)}, u32[]{:S(2)}) copy-start(bf16[1,1568,256]{2,1,0:T(8,128)(2,1)} %param.22) | copy-start | bytes 2408452
  2.8 26.2 %collective-permute-start.12 = (bf16[1120,256]{1,0:T(8,128)(2,1)}, bf16[1120,256]{1,0:T(8,128)(2,1)S(1)}, u32[]{:S(2)}, u32[]{:S(2)}) collective-permute-start(bf16[1120,256]{1,0:T(8,128)(2,1)} %get-tuple-element.39), channel_id=1, source_target_pairs={{8,0},{16,8},{24,16},{9,1},{17,9},{25,17},{10,2},{18,10},{26,18},{... | collective-permute-start | bytes 1720328 | tf_op jit(solution)/shard_map/ppermute | solution.py:19
  6.1 18.7 %collective-permute-start = (bf16[98,1024]{1,0:T(8,128)(2,1)}, bf16[98,1024]{1,0:T(8,128)(2,1)}, u32[]{:S(2)}, u32[]{:S(2)}) collective-permute-start(bf16[98,1024]{1,0:T(8,128)(2,1)} %bitcast.26), channel_id=1, source_target_pairs={{0,8},{8,16},{16,24},{1,9},{9,17},{17,25},{2,10},{10,18},{18,26},{... | collective-permute-start | bytes 602120 | tf_op jit(solution)/shard_map/ppermute | solution.py:19
  8.6 36.0 %collective-permute-start.5 = (bf16[1024,512]{1,0:T(8,128)(2,1)}, bf16[1024,512]{1,0:T(8,128)(2,1)}, u32[]{:S(2)}, u32[]{:S(2)}) collective-permute-start(bf16[1024,512]{1,0:T(8,128)(2,1)} %bitcast.20), channel_id=1, source_target_pairs={{0,1},{1,0},{2,3},{3,2},{4,5},{5,4},{6,7},{7,6},{8,9},{9,8},{10,11... | collective-permute-start | bytes 3145736 | tf_op jit(solution)/shard_map/ppermute | solution.py:23
  8.7 24.4 %collective-permute-start.13 = (bf16[448,256]{1,0:T(8,128)(2,1)S(1)}, bf16[448,256]{1,0:T(8,128)(2,1)S(1)}, u32[]{:S(2)}, u32[]{:S(2)}) collective-permute-start(bf16[448,256]{1,0:T(8,128)(2,1)S(1)} %get-tuple-element.45), channel_id=1, source_target_pairs={{8,0},{16,8},{24,16},{9,1},{17,9},{25,17},{10,2},{18,10},{26,18},{... | collective-permute-start | bytes 688136 | tf_op jit(solution)/shard_map/ppermute | solution.py:19
  12.9 40.7 %collective-permute-start.8 = (bf16[512,1024]{1,0:T(8,128)(2,1)}, bf16[512,1024]{1,0:T(8,128)(2,1)S(1)}, u32[]{:S(2)}, u32[]{:S(2)}) collective-permute-start(bf16[512,1024]{1,0:T(8,128)(2,1)} %bitcast.13), channel_id=1, source_target_pairs={{0,1},{1,0},{2,3},{3,2},{4,5},{5,4},{6,7},{7,6},{8,9},{9,8},{10,11... | collective-permute-start | bytes 3145736 | tf_op jit(solution)/shard_map/ppermute | solution.py:23
  13.2 1.1 %copy-start.3 = (bf16[1,1568,256]{2,1,0:T(8,128)(2,1)S(1)}, bf16[1,1568,256]{2,1,0:T(8,128)(2,1)}, u32[]{:S(2)}) copy-start(bf16[1,1568,256]{2,1,0:T(8,128)(2,1)} %param.21) | copy-start | bytes 2408452
  14.3 1.0 %copy-start.5 = (bf16[1,256,1024]{2,1,0:T(8,128)(2,1)S(1)}, bf16[1,256,1024]{2,1,0:T(8,128)(2,1)}, u32[]{:S(2)}) copy-start(bf16[1,256,1024]{2,1,0:T(8,128)(2,1)} %param.24) | copy-start | bytes 1572868
  15.4 9.4 %copy-start.10 = (bf16[98,1024]{1,0:T(8,128)(2,1)S(1)}, bf16[98,1024]{1,0:T(8,128)(2,1)}, u32[]{:S(2)}) copy-start(bf16[98,1024]{1,0:T(8,128)(2,1)} %param.14) | copy-start | bytes 602116
  25.7 11.2 %collective-permute-start.2 = (bf16[98,1024]{1,0:T(8,128)(2,1)S(1)}, bf16[98,1024]{1,0:T(8,128)(2,1)S(1)}, u32[]{:S(2)}, u32[]{:S(2)}) collective-permute-start(bf16[98,1024]{1,0:T(8,128)(2,1)S(1)} %broadcast_select_fusion.refs_0_.rows), channel_id=1, source_target_pairs={{0,4},{1,5},{2,6},{3,7},{4,0},{5,1},{6,2},{7,3},{8,12},{9,13},{10,... | collective-permute-start | bytes 602120 | tf_op jit(solution)/shard_map/ppermute | solution.py:38
  28.9 8.6 %collective-permute-start.1 = (bf16[98,1024]{1,0:T(8,128)(2,1)S(1)}, bf16[98,1024]{1,0:T(8,128)(2,1)S(1)}, u32[]{:S(2)}, u32[]{:S(2)}) collective-permute-start(bf16[98,1024]{1,0:T(8,128)(2,1)S(1)} %broadcast_select_fusion.refs_0_.rows), channel_id=1, source_target_pairs={{0,2},{1,3},{2,0},{3,1},{4,6},{5,7},{6,4},{7,5},{8,10},{9,11},{10,... | collective-permute-start | bytes 602120 | tf_op jit(solution)/shard_map/ppermute | solution.py:38
  33.1 11.2 %copy-start.11 = (f32[1,512]{1,0:T(1,128)S(1)}, f32[1,512]{1,0:T(1,128)}, u32[]{:S(2)}) copy-start(f32[1,512]{1,0:T(1,128)} %param.19) | copy-start | bytes 6148
  33.1 11.2 %copy-start.12 = (f32[1,512]{1,0:T(1,128)S(1)}, f32[1,512]{1,0:T(1,128)}, u32[]{:S(2)}) copy-start(f32[1,512]{1,0:T(1,128)} %param.18) | copy-start | bytes 6148
  33.1 11.6 %copy-start.7 = (bf16[1,1024,512]{2,1,0:T(8,128)(2,1)S(1)}, bf16[1,1024,512]{2,1,0:T(8,128)(2,1)}, u32[]{:S(2)}) copy-start(bf16[1,1024,512]{2,1,0:T(8,128)(2,1)} %param.17) | copy-start | bytes 3145732
  33.1 11.6 %copy-start.8 = (f32[1,1024]{1,0:T(1,128)S(1)}, f32[1,1024]{1,0:T(1,128)}, u32[]{:S(2)}) copy-start(f32[1,1024]{1,0:T(1,128)} %refs_6_.1) | copy-start | bytes 12292
  33.1 11.6 %copy-start.9 = (f32[1,1024]{1,0:T(1,128)S(1)}, f32[1,1024]{1,0:T(1,128)}, u32[]{:S(2)}) copy-start(f32[1,1024]{1,0:T(1,128)} %refs_7_.1) | copy-start | bytes 12292
  34.2 13.3 %collective-permute-start.14 = (bf16[256,1024]{1,0:T(8,128)(2,1)S(1)}, bf16[256,1024]{1,0:T(8,128)(2,1)S(1)}, u32[]{:S(2)}, u32[]{:S(2)}) collective-permute-start(bf16[256,1024]{1,0:T(8,128)(2,1)S(1)} %get-tuple-element.53), channel_id=1, source_target_pairs={{0,1},{1,0},{2,3},{3,2},{4,5},{5,4},{6,7},{7,6},{8,9},{9,8},{10,11... | collective-permute-start | bytes 1572872 | tf_op jit(solution)/shard_map/ppermute | solution.py:23
  36.9 6.1 %collective-permute-start.3 = (bf16[98,1024]{1,0:T(8,128)(2,1)S(1)}, bf16[98,1024]{1,0:T(8,128)(2,1)S(1)}, u32[]{:S(2)}, u32[]{:S(2)}) collective-permute-start(bf16[98,1024]{1,0:T(8,128)(2,1)S(1)} %collective-permute-done.2.refs_2_), channel_id=1, source_target_pairs={{0,2},{1,3},{2,0},{3,1},{4,6},{5,7},{6,4},{7,5},{8,10},{9,11},{10,... | collective-permute-start | bytes 602120 | tf_op jit(solution)/shard_map/ppermute | solution.py:38
  37.5 5.9 %collective-permute-start.16 = (bf16[64,1024]{1,0:T(8,128)(2,1)S(1)}, bf16[64,1024]{1,0:T(8,128)(2,1)S(1)}, u32[]{:S(2)}, u32[]{:S(2)}) collective-permute-start(bf16[64,1024]{1,0:T(8,128)(2,1)S(1)} %get-tuple-element.57), channel_id=1, source_target_pairs={{0,1},{1,0},{2,3},{3,2},{4,5},{5,4},{6,7},{7,6},{8,9},{9,8},{10,11... | collective-permute-start | bytes 393224 | tf_op jit(solution)/shard_map/ppermute | solution.py:23
  43.3 1.2 %collective-permute-start.4 = (f32[2,1024]{1,0:T(2,128)S(1)}, f32[2,1024]{1,0:T(2,128)S(1)}, u32[]{:S(2)}, u32[]{:S(2)}) collective-permute-start(f32[2,1024]{1,0:T(2,128)S(1)} %shard_map.156.refs_4_), channel_id=1, source_target_pairs={{0,1},{1,0},{2,3},{3,2},{4,5},{5,4},{6,7},{7,6},{8,9},{9,8},{10,11... | collective-permute-start | bytes 24584 | tf_op jit(solution)/shard_map/ppermute | solution.py:23
  43.4 6.0 %collective-permute-start.17 = (bf16[64,1024]{1,0:T(8,128)(2,1)S(1)}, bf16[64,1024]{1,0:T(8,128)(2,1)S(1)}, u32[]{:S(2)}, u32[]{:S(2)}) collective-permute-start(bf16[64,1024]{1,0:T(8,128)(2,1)S(1)} %shard_map.166), channel_id=1, source_target_pairs={{0,2},{1,3},{2,0},{3,1},{4,6},{5,7},{6,4},{7,5},{8,10},{9,11},{10,... | collective-permute-start | bytes 393224 | tf_op jit(solution)/shard_map/ppermute | solution.py:38
  44.3 9.4 %copy-start.2 = (bf16[1,512,1024]{2,1,0:T(8,128)(2,1)S(1)}, bf16[1,512,1024]{2,1,0:T(8,128)(2,1)}, u32[]{:S(2)}) copy-start(bf16[1,512,1024]{2,1,0:T(8,128)(2,1)} %param.20) | copy-start | bytes 3145732
  44.5 9.1 %collective-permute-start.7 = (f32[2,512]{1,0:T(2,128)S(1)}, f32[2,512]{1,0:T(2,128)S(1)}, u32[]{:S(2)}, u32[]{:S(2)}) collective-permute-start(f32[2,512]{1,0:T(2,128)S(1)} %pad_maximum_fusion.one), channel_id=1, source_target_pairs={{0,1},{1,0},{2,3},{3,2},{4,5},{5,4},{6,7},{7,6},{8,9},{9,8},{10,11... | collective-permute-start | bytes 12296 | tf_op jit(solution)/shard_map/ppermute | solution.py:23
  47.1 6.6 %collective-permute-start.6 = (f32[2,1024]{1,0:T(2,128)S(1)}, f32[2,1024]{1,0:T(2,128)S(1)}, u32[]{:S(2)}, u32[]{:S(2)}) collective-permute-start(f32[2,1024]{1,0:T(2,128)S(1)} %get-tuple-element.34), channel_id=1, source_target_pairs={{0,1},{1,0},{2,3},{3,2},{4,5},{5,4},{6,7},{7,6},{8,9},{9,8},{10,11... | collective-permute-start | bytes 24584 | tf_op jit(solution)/shard_map/ppermute | solution.py:23
  49.4 8.9 %collective-permute-start.18 = (bf16[64,1024]{1,0:T(8,128)(2,1)S(1)}, bf16[64,1024]{1,0:T(8,128)(2,1)S(1)}, u32[]{:S(2)}, u32[]{:S(2)}) collective-permute-start(bf16[64,1024]{1,0:T(8,128)(2,1)S(1)} %add_convert_fusion.1), channel_id=1, source_target_pairs={{0,4},{1,5},{2,6},{3,7},{4,0},{5,1},{6,2},{7,3},{8,12},{9,13},{10,... | collective-permute-start | bytes 393224 | tf_op jit(solution)/shard_map/ppermute | solution.py:38
  51.9 7.5 %collective-permute-start.15 = (bf16[64,1024]{1,0:T(8,128)(2,1)S(1)}, bf16[64,1024]{1,0:T(8,128)(2,1)S(1)}, u32[]{:S(2)}, u32[]{:S(2)}) collective-permute-start(bf16[64,1024]{1,0:T(8,128)(2,1)S(1)} %get-tuple-element.55), channel_id=1, source_target_pairs={{0,2},{1,3},{2,0},{3,1},{4,6},{5,7},{6,4},{7,5},{8,10},{9,11},{10,... | collective-permute-start | bytes 393224 | tf_op jit(solution)/shard_map/ppermute | solution.py:38
  53.7 23.1 %copy-start.6 = (bf16[1,256,1024]{2,1,0:T(8,128)(2,1)S(1)}, bf16[1,256,1024]{2,1,0:T(8,128)(2,1)}, u32[]{:S(2)}) copy-start(bf16[1,256,1024]{2,1,0:T(8,128)(2,1)} %param.24) | copy-start | bytes 1572868
  54.9 13.6 %collective-permute-start.10 = (bf16[98,1024]{1,0:T(8,128)(2,1)S(1)}, bf16[98,1024]{1,0:T(8,128)(2,1)S(1)}, u32[]{:S(2)}, u32[]{:S(2)}) collective-permute-start(bf16[98,1024]{1,0:T(8,128)(2,1)S(1)} %get-tuple-element.38), channel_id=1, source_target_pairs={{0,2},{1,3},{2,0},{3,1},{4,6},{5,7},{6,4},{7,5},{8,10},{9,11},{10,... | collective-permute-start | bytes 602120 | tf_op jit(solution)/shard_map/ppermute | solution.py:38
  59.5 7.8 %collective-permute-start.20 = (bf16[64,1024]{1,0:T(8,128)(2,1)S(1)}, bf16[64,1024]{1,0:T(8,128)(2,1)S(1)}, u32[]{:S(2)}, u32[]{:S(2)}) collective-permute-start(bf16[64,1024]{1,0:T(8,128)(2,1)S(1)} %shard_map.167.refs_0_), channel_id=1, source_target_pairs={{0,4},{1,5},{2,6},{3,7},{4,0},{5,1},{6,2},{7,3},{8,12},{9,13},{10,... | collective-permute-start | bytes 393224 | tf_op jit(solution)/shard_map/ppermute | solution.py:38
  60.9 10.4 %collective-permute-start.9 = (bf16[98,1024]{1,0:T(8,128)(2,1)S(1)}, bf16[98,1024]{1,0:T(8,128)(2,1)S(1)}, u32[]{:S(2)}, u32[]{:S(2)}) collective-permute-start(bf16[98,1024]{1,0:T(8,128)(2,1)S(1)} %get-tuple-element.36), channel_id=1, source_target_pairs={{0,2},{1,3},{2,0},{3,1},{4,6},{5,7},{6,4},{7,5},{8,10},{9,11},{10,... | collective-permute-start | bytes 602120 | tf_op jit(solution)/shard_map/ppermute | solution.py:38
  63.0 11.2 %collective-permute-start.19 = (bf16[64,1024]{1,0:T(8,128)(2,1)S(1)}, bf16[64,1024]{1,0:T(8,128)(2,1)S(1)}, u32[]{:S(2)}, u32[]{:S(2)}) collective-permute-start(bf16[64,1024]{1,0:T(8,128)(2,1)S(1)} %shard_map.167.refs_0_), channel_id=1, source_target_pairs={{0,2},{1,3},{2,0},{3,1},{4,6},{5,7},{6,4},{7,5},{8,10},{9,11},{10,... | collective-permute-start | bytes 393224 | tf_op jit(solution)/shard_map/ppermute | solution.py:38
  67.3 9.5 %collective-permute-start.21 = (bf16[64,1024]{1,0:T(8,128)(2,1)S(1)}, bf16[64,1024]{1,0:T(8,128)(2,1)S(1)}, u32[]{:S(2)}, u32[]{:S(2)}) collective-permute-start(bf16[64,1024]{1,0:T(8,128)(2,1)S(1)} %collective-permute-done.20.refs_2_), channel_id=1, source_target_pairs={{0,2},{1,3},{2,0},{3,1},{4,6},{5,7},{6,4},{7,5},{8,10},{9,11},{10,... | collective-permute-start | bytes 393224 | tf_op jit(solution)/shard_map/ppermute | solution.py:38
  68.5 12.8 %collective-permute-start.11 = (bf16[98,1024]{1,0:T(8,128)(2,1)S(1)}, bf16[98,1024]{1,0:T(8,128)(2,1)S(1)}, u32[]{:S(2)}, u32[]{:S(2)}) collective-permute-start(bf16[98,1024]{1,0:T(8,128)(2,1)S(1)} %add_convert_fusion), channel_id=1, source_target_pairs={{0,6},{1,7},{2,4},{3,5},{4,2},{5,3},{6,0},{7,1},{8,14},{9,15},{10,... | collective-permute-start | bytes 602120 | tf_op jit(solution)/shard_map/ppermute | solution.py:38
  71.0 11.2 %collective-permute-start.22 = (bf16[64,1024]{1,0:T(8,128)(2,1)S(1)}, bf16[64,1024]{1,0:T(8,128)(2,1)S(1)}, u32[]{:S(2)}, u32[]{:S(2)}) collective-permute-start(bf16[64,1024]{1,0:T(8,128)(2,1)S(1)} %shard_map.167.refs_0_), channel_id=1, source_target_pairs={{0,1},{1,0},{2,3},{3,2},{4,5},{5,4},{6,7},{7,6},{8,9},{9,8},{10,11... | collective-permute-start | bytes 393224 | tf_op jit(solution)/shard_map/ppermute | solution.py:23
  71.4 10.7 %collective-permute-start.24 = (bf16[64,1024]{1,0:T(8,128)(2,1)S(1)}, bf16[64,1024]{1,0:T(8,128)(2,1)S(1)}, u32[]{:S(2)}, u32[]{:S(2)}) collective-permute-start(bf16[64,1024]{1,0:T(8,128)(2,1)S(1)} %collective-permute-done.20.refs_2_), channel_id=1, source_target_pairs={{0,1},{1,0},{2,3},{3,2},{4,5},{5,4},{6,7},{7,6},{8,9},{9,8},{10,11... | collective-permute-start | bytes 393224 | tf_op jit(solution)/shard_map/ppermute | solution.py:23
  74.2 7.9 %collective-permute-start.23 = (bf16[64,1024]{1,0:T(8,128)(2,1)S(1)}, bf16[64,1024]{1,0:T(8,128)(2,1)S(1)}, u32[]{:S(2)}, u32[]{:S(2)}) collective-permute-start(bf16[64,1024]{1,0:T(8,128)(2,1)S(1)} %collective-permute-done.19.refs_1_), channel_id=1, source_target_pairs={{0,1},{1,0},{2,3},{3,2},{4,5},{5,4},{6,7},{7,6},{8,9},{9,8},{10,11... | collective-permute-start | bytes 393224 | tf_op jit(solution)/shard_map/ppermute | solution.py:23
  76.8 5.3 %collective-permute-start.25 = (bf16[64,1024]{1,0:T(8,128)(2,1)S(1)}, bf16[64,1024]{1,0:T(8,128)(2,1)S(1)}, u32[]{:S(2)}, u32[]{:S(2)}) collective-permute-start(bf16[64,1024]{1,0:T(8,128)(2,1)S(1)} %collective-permute-done.21.refs_3_), channel_id=1, source_target_pairs={{0,1},{1,0},{2,3},{3,2},{4,5},{5,4},{6,7},{7,6},{8,9},{9,8},{10,11... | collective-permute-start | bytes 393224 | tf_op jit(solution)/shard_map/ppermute | solution.py:23
